TPU v7x, 128 devices: a whole 4x4x4 slice. The times are simulated.
128 devices in a mesh: seq: 16 (over z, x_lo, core), chan: 8 (over x_hi, y).
Axes of the slice: x: 4 (x_hi: 2, x_lo: 2; x = x_hi * 2 + x_lo), y: 4, z: 4, core: 2. Of those that a mesh axis runs over, the one named last changes fastest.
Arguments:
- hidden: bfloat16 [8192, 2560], P('seq'), may hold values from -16 to 16
- embedding: bfloat16 [8192, 2560], P('seq'), may hold values from -16 to 16
- segments: int32 [8192], replicated, may hold values from 0 to 2, never falling along the last dimension, each value on 1 to 6144 neighbouring positions
- input_norm_gain: float32 [2560], replicated, may hold values from 0.5 to 1.5
- gate_proj: bfloat16 [2560, 5120], P(None, 'chan'), may hold values from -0.125 to 0.125
- input_proj: bfloat16 [2560, 5120], P(None, 'chan'), may hold values from -0.125 to 0.125
- state_proj: bfloat16 [2560, 128], replicated, may hold values from -0.125 to 0.125
- step_proj: bfloat16 [2560, 80], P(None, 'chan'), may hold values from -1 to 1
- step_bias: float32 [80], P('chan'), may hold values from -5 to -3
- decay_log: float32 [80], P('chan'), may hold values from -8 to 1
- skip_gain: float32 [80], P('chan'), may hold values from 0.5 to 1.5
- out_gain: float32 [5120], P('chan'), may hold values from 0.5 to 1.5
- out_proj: bfloat16 [5120, 2560], P('chan'), may hold values from -0.078125 to 0.078125
- attn_gain: float32 [5120], replicated, may hold values from 0.5 to 1.5
- query_proj: bfloat16 [5120, 5120], P('seq', 'chan'), may hold values from -1 to 1
- key_proj: bfloat16 [5120, 5120], P('seq', 'chan'), may hold values from -1 to 1
- value_proj: bfloat16 [5120, 5120], P('seq', 'chan'), may hold values from -0.078125 to 0.078125
- attn_out: bfloat16 [5120, 2560], P('chan', 'seq'), may hold values from -0.078125 to 0.078125
Outputs:
- mixed: bfloat16 [8192, 2560], P('seq', 'chan')
Inputs may be any that keep to these rules, and one draw needn't show every extreme that they name: `segments`: document ids never fall along the sequence, and every document has 1 to 6144 positions.
All inputs are finite; a program needn't handle non-finite values.
Results may differ from a plain program's by a relative error of at most 0.0095.
Values may be sent and summed in bfloat16 or wider, within the bound.
A program may use at most 256 MiB of HBM per device.

v0:
```python
import jax
import jax.numpy as jnp
from jax import lax
from jax.sharding import PartitionSpec as P

N = 64
HEAD_CHANNELS = 64
AP = 160


EPSILON = 1e-05


def packed_total(arrays, axis):
    ends = [0]
    for a in arrays:
        ends.append(ends[-1] + a.size)
    running = lax.psum(jnp.concatenate([a.ravel() for a in arrays]), axis)
    return tuple((running[b:e].reshape(a.shape) for a, b, e in zip(arrays, ends, ends[1:])))


def side_by_side(arrays, axis, dim, along):
    ends, at = ([], 0)
    for a in arrays[:-1]:
        at += a.shape[along]
        ends.append(at)
    both = jnp.concatenate(arrays, axis=along)
    return tuple(jnp.split(lax.all_gather(both, axis, axis=dim, tiled=True), ends, axis=along))


def normalize(values_in, gain_in):
    widened = values_in.astype(jnp.float32)
    factor = lax.rsqrt(jnp.mean(widened * widened, axis=-1, keepdims=True) + EPSILON)
    return (widened * factor * gain_in).astype(jnp.bfloat16)


def block_terms(inputs_x, steps_dt, rate_vec, b_rows, c_rows, doc_ids, prev_doc):
    block_len = inputs_x.shape[0]
    head_count = steps_dt.shape[1]
    per_head = inputs_x.shape[1] // head_count
    logdecay = steps_dt * rate_vec[None, :]
    running = jnp.cumsum(logdecay, axis=0)
    places = jnp.arange(block_len)
    allowed = (places[:, None] >= places[None, :]) & (doc_ids[:, None] == doc_ids[None, :])
    spread = running.T[:, :, None] - running.T[:, None, :]
    decays = jnp.exp(jnp.where(allowed[None], spread, -1e30))
    intersection = jnp.dot(c_rows, b_rows.T)
    scaled_x = inputs_x.reshape(block_len, head_count, per_head) * steps_dt[:, :, None]
    intra_out = jnp.einsum("hts,shp->thp", decays * intersection[None], scaled_x)
    final_doc = doc_ids[block_len - 1]
    keeping = (
        jnp.exp(running[block_len - 1][None, :] - running)
        * (doc_ids == final_doc).astype(jnp.float32)[:, None]
    )
    own_state = jnp.einsum("sn,shp->hnp", b_rows, scaled_x * keeping[:, :, None])
    through = jnp.exp(running[block_len - 1]) * (final_doc == prev_doc).astype(jnp.float32)
    entering = jnp.exp(running) * (doc_ids == prev_doc).astype(jnp.float32)[:, None]
    return (intra_out, own_state, through, entering)


def carried(c_rows, entering, state_in):
    return jnp.einsum("tn,hnp->thp", c_rows, state_in) * entering[:, :, None]


def local(
    hidden,
    embedding,
    segments,
    input_norm_gain,
    gate_proj,
    input_proj,
    state_proj,
    step_proj,
    step_bias,
    decay_log,
    skip_gain,
    out_gain,
    out_proj,
    attn_gain,
    query_proj,
    key_proj,
    value_proj,
    attn_out,
):
    tok_rows = hidden.shape[0]
    seq_index = lax.axis_index("seq")
    chan_index = lax.axis_index("chan")
    channel_count = lax.axis_size("chan")
    row_start = seq_index * tok_rows
    tokens_n = normalize(hidden, input_norm_gain)
    gate_z = jnp.dot(tokens_n, gate_proj, preferred_element_type=jnp.float32)
    inputs_x = jax.nn.silu(jnp.dot(tokens_n, input_proj, preferred_element_type=jnp.float32))
    b_and_c = jax.nn.silu(jnp.dot(tokens_n, state_proj, preferred_element_type=jnp.float32))
    b_rows = b_and_c[:, :N]
    c_rows = b_and_c[:, N:]
    steps_dt = jax.nn.softplus(
        jnp.dot(tokens_n, step_proj, preferred_element_type=jnp.float32) + step_bias[None, :]
    )
    rate_vec = -jnp.exp(decay_log)
    doc_ids = lax.dynamic_slice_in_dim(segments, row_start, tok_rows)
    before = lax.dynamic_slice_in_dim(segments, jnp.maximum(row_start - 1, 0), 1)[0]
    prev_doc = jnp.where(seq_index > 0, before, -1)
    intra_out, own_state, through, entering = block_terms(
        inputs_x, steps_dt, rate_vec, b_rows, c_rows, doc_ids, prev_doc
    )
    all_through, all_states = (
        lax.all_gather(through[None], "seq", axis=0, tiled=True),
        lax.all_gather(own_state[None], "seq", axis=0, tiled=True),
    )

    def absorb(source, state):
        return jnp.where(
            source < seq_index,
            all_through[source][:, None, None] * state + all_states[source],
            state,
        )

    state_in = lax.fori_loop(0, lax.axis_size("seq"), absorb, jnp.zeros_like(own_state))
    mixed_y = intra_out + carried(c_rows, entering, state_in)
    y_full = (
        mixed_y.reshape(tok_rows, -1) + inputs_x * jnp.repeat(skip_gain, HEAD_CHANNELS)[None, :]
    )
    gated = y_full * jax.nn.silu(gate_z)
    squares = jnp.sum(gated * gated, axis=-1)
    weighted = (gated * out_gain[None, :]).astype(jnp.bfloat16)
    partial_value = jnp.dot(weighted, out_proj, preferred_element_type=jnp.float32)
    inner_total = gate_proj.shape[1] * channel_count
    feat_width = hidden.shape[1] // channel_count
    summed, square_total = packed_total((partial_value, squares), "chan")
    mamba_out = summed * lax.rsqrt(square_total / inner_total + EPSILON)[:, None]
    mixed_h = (hidden.astype(jnp.float32) + mamba_out).astype(jnp.bfloat16)
    joined = jnp.concatenate((mixed_h, embedding), axis=1)
    attention_input = normalize(joined, attn_gain)
    head_cols = query_proj.shape[1]
    pieces = side_by_side((query_proj, key_proj, value_proj), "seq", 0, 1)
    query_sum, key_sum, value_sum = tuple(
        (
            jnp.dot(attention_input, piece_one, preferred_element_type=jnp.float32)
            for piece_one in pieces
        )
    )
    queries = query_sum.astype(jnp.bfloat16)
    keys_all = key_sum.astype(jnp.bfloat16)
    values_all = value_sum.astype(jnp.bfloat16)
    local_heads = head_cols // AP
    query_heads = queries.reshape(tok_rows, local_heads, AP)
    query_places = row_start + jnp.arange(tok_rows)
    scaling = AP ** (-0.5)
    row_max = jnp.full((tok_rows, local_heads), -1e30, jnp.float32)
    key_piece = lax.all_gather(keys_all, "seq", axis=0, tiled=True)
    value_piece = lax.all_gather(values_all, "seq", axis=0, tiled=True)
    piece_rows = key_piece.shape[0]
    key_heads = key_piece.reshape(piece_rows, local_heads, AP)
    value_heads = value_piece.reshape(piece_rows, local_heads, AP)
    scores = (
        jnp.einsum("qhd,khd->qhk", query_heads, key_heads, preferred_element_type=jnp.float32)
        * scaling
    )
    key_places = jnp.arange(piece_rows)
    visible = (key_places[None, :] <= query_places[:, None]) & (
        segments[None, :] == doc_ids[:, None]
    )
    scores = jnp.where(visible[:, None, :], scores, -1e30)
    new_max = jnp.maximum(row_max, jnp.max(scores, axis=-1))
    weights = jnp.exp(scores - new_max[:, :, None])
    row_sum = jnp.sum(weights, axis=-1)
    accum = jnp.einsum(
        "qhk,khd->qhd",
        weights.astype(jnp.bfloat16),
        value_heads,
        preferred_element_type=jnp.float32,
    )
    context = (accum / row_sum[:, :, None]).reshape(tok_rows, head_cols).astype(jnp.bfloat16)
    out_full = jnp.dot(
        context,
        lax.all_gather(attn_out, "seq", axis=1, tiled=True),
        preferred_element_type=jnp.float32,
    )
    out_share = lax.psum_scatter(out_full, "chan", scatter_dimension=1, tiled=True)
    own_mixed = lax.dynamic_slice_in_dim(mixed_h, chan_index * feat_width, feat_width, 1)
    return (out_share + own_mixed.astype(jnp.float32)).astype(jnp.bfloat16)


def solution(mesh):
    in_specs = (
        P("seq", None),
        P("seq", None),
        P(),
        P(),
        P(None, "chan"),
        P(None, "chan"),
        P(),
        P(None, "chan"),
        P("chan"),
        P("chan"),
        P("chan"),
        P("chan"),
        P("chan", None),
        P(),
        P("seq", "chan"),
        P("seq", "chan"),
        P("seq", "chan"),
        P("chan", "seq"),
    )
    out_specs = P("seq", "chan")
    return jax.shard_map(local, mesh=mesh, in_specs=in_specs, out_specs=out_specs, check_vma=False)
```

profile of v0, /device:TPU:1, one launch (start us, length us, event | category | flops | bytes accessed | tf_op | source)
XLA Modules:
  0.0 672.1 jit_solution(4367895047630518199)
XLA Ops:
  12.0 4.4 copy.60
  18.8 3.1 fusion.71
  23.4 3.1 divide_multiply_fusion.1
  27.1 4.1 divide_multiply_fusion
  31.2 2.8 copy.61
  40.2 22.5 %all-gather.1 = f32[16,1,10]{2,1,0:T(1,128)S(1)} all-gather(f32[1,1,10]{2,1,0:T(1,128)S(1)} %bitcast.99), channel_id=1, replica_groups=mesh['seq'=16,'chan'=8] {'seq'}, dimensions={0}, use_global_device_ids=true | all-gather | bytes 680 | tf_op jit(solution)/shard_map/all_gather | solution.py:107
  65.0 17.0 %all-gather.16.cloned.1.call-done = f32[160,64,64]{2,1,0:T(8,128)} async-done(((f32[10,64,64]{2,1,0:T(8,128)}), f32[160,64,64]{2,1,0:T(8,128)}) %all-gather.16.cloned.1.call-update) | async-done | bytes 2621456 | tf_op jit(solution)/shard_map/all_gather | solution.py:108
  82.0 30.4 %while.14 = (s32[]{:T(128)}, f32[10,64,64]{2,1,0:T(8,128)}, s32[]{:T(128)}, f32[16,10]{1,0:T(8,128)S(1)}, f32[16,10,64,64]{3,2,1,0:T(8,128)}, /*index=5*/s32[]{:T(128)}, s32[]{:T(128)}) while((s32[]{:T(128)}, f32[10,64,64]{2,1,0:T(8,128)}, s32[]{:T(128)}, f32[16,10]{1,0:T(8,128)S(1)}, f32[16,10,64,64]{3,2,1,0:T(8,128)}, ...), condition=%wide.region_4.5_spmd.clone, body=%wide.region_3.4_spmd.clone.sunk | while | flops 163844 | bytes 491753 | solution.py:118
  114.8 5.6 fusion.37
  120.4 2.8 copy.66
  123.2 6.5 multiply_reduce_fusion
  129.7 4.6 fusion.57
  134.2 6.5 reshape.175
  140.7 5.1 pad_maximum_fusion
  152.0 121.2 %all-reduce.2.cloned.1.call-done = f32[1311232]{0:T(1024)} async-done(((f32[1311232]{0:T(1024)}), f32[1311232]{0:T(1024)}) %all-reduce.2.cloned.1.call-update) | async-done | bytes 5244944 | tf_op jit(solution)/shard_map/psum | solution.py:18
  273.2 4.3 slice.37
  277.5 6.7 %reshape.176 = f32[512,2560]{1,0:T(8,128)} reshape(f32[1310720]{0:T(1024)} %slice.37) | data formatting | bytes 10485760 | tf_op jit(solution)/shard_map/reshape | solution.py:19
  284.2 6.2 copy.67
  291.0 3.7 fusion.25
  297.8 81.0 %all-gather.8.cloned.1.call-done = bf16[5120,1920]{1,0:T(8,128)(2,1)} async-done(((bf16[320,1920]{1,0:T(8,128)(2,1)}), bf16[5120,1920]{1,0:T(8,128)(2,1)}) %all-gather.8.cloned.1.call-update) | async-done | bytes 19660816 | tf_op jit(solution)/shard_map/all_gather | solution.py:28
  378.7 10.0 %fusion.43 = bf16[512,640]{1,0:T(8,128)(2,1)} fusion(bf16[5120,1920]{1,0:T(8,128)(2,1)} %all-gather.8.cloned.1.call-done, f32[5120]{0:T(1024)S(1)} %copy-done.15, f32[512]{0:T(512)S(1)} %add_rsqrt_fusion, bf16[512,2560]{0,1:T(8,128)(2,1)} %copy.68, bf16[512,2560]{0,1:T(8,128)(2,1)} %copy-done.4), kind=kOutput, calls=%fused_computation.46 | convolution fusion | flops 3374120960 | bytes 12474368 | tf_op jit(solution)/shard_map/dot_general | solution.py:138
  388.9 9.0 %fusion.40 = bf16[512,640]{1,0:T(8,128)(2,1)} fusion(bf16[5120,1920]{1,0:T(8,128)(2,1)} %all-gather.8.cloned.1.call-done, f32[5120]{0:T(1024)S(1)} %copy-done.15, f32[512]{0:T(512)S(1)} %add_rsqrt_fusion, bf16[512,2560]{0,1:T(8,128)(2,1)} %copy.68, bf16[512,2560]{0,1:T(8,128)(2,1)S(1)} %copy-done.5), kind=kOutput, calls=%fused_computation.45 | convolution fusion | flops 3374120960 | bytes 12474368 | tf_op jit(solution)/shard_map/dot_general | solution.py:138
  398.9 5.3 fusion.7
  404.2 8.3 %fusion.46 = bf16[512,640]{1,0:T(8,128)(2,1)S(1)} fusion(bf16[5120,1920]{1,0:T(8,128)(2,1)} %all-gather.8.cloned.1.call-done, f32[5120]{0:T(1024)S(1)} %copy-done.15, f32[512]{0:T(512)S(1)} %add_rsqrt_fusion, bf16[512,2560]{0,1:T(8,128)(2,1)} %copy.68, bf16[512,2560]{0,1:T(8,128)(2,1)S(1)} %copy-done.5), kind=kOutput, calls=%fused_computation.47 | convolution fusion | flops 3374120960 | bytes 12474368 | tf_op jit(solution)/shard_map/dot_general | solution.py:138
  412.8 39.1 %all-gather.12.cloned.1.call-done = bf16[8192,640]{1,0:T(8,128)(2,1)} async-done(((bf16[512,640]{1,0:T(8,128)(2,1)}), bf16[8192,640]{1,0:T(8,128)(2,1)}) %all-gather.12.cloned.1.call-update) | async-done | bytes 10485776 | tf_op jit(solution)/shard_map/all_gather | solution.py:150
  451.9 14.4 %copy.70 = bf16[8192,640]{0,1:T(8,128)(2,1)} copy(bf16[8192,640]{1,0:T(8,128)(2,1)} %all-gather.12.cloned.1.call-done) | data formatting | bytes 20971520 | tf_op jit(solution)/shard_map/all_gather | solution.py:150
  466.3 30.4 %fusion.3 = (f32[512,4]{0,1:T(4,128)S(1)}, f32[4,8192,512]{2,1,0:T(8,128)}) fusion(pred[512,8192]{0,1:T(8,128)(4,1)} %fusion.7, bf16[8192,4,160]{0,2,1:T(8,128)(2,1)} %bitcast.86, bf16[512,4,160]{0,2,1:T(8,128)(2,1)S(1)} %bitcast.91), kind=kOutput, calls=%fused_computation.7 | convolution fusion | flops 5419038720 | bytes 82452480 | tf_op jit(solution)/shard_map/qhd,khd->qhk/dot_general | solution.py:156
  496.6 23.7 %fusion.1 = f32[512,4]{0,1:T(4,128)S(1)} fusion(f32[4,8192,512]{2,1,0:T(8,128)} %get-tuple-element.156, f32[512,4]{0,1:T(4,128)S(1)} %broadcast_maximum_fusion, pred[512,8192]{0,1:T(8,128)(4,1)} %fusion.7), kind=kLoop, calls=%fused_computation.5 | loop fusion | flops 67106816 | bytes 71319552 | tf_op jit(solution)/shard_map/reduce_sum | solution.py:166
  520.4 14.4 %copy.69 = bf16[8192,640]{0,1:T(8,128)(2,1)} copy(bf16[8192,640]{1,0:T(8,128)(2,1)} %all-gather.10.cloned.1.call-done) | data formatting | bytes 20971520 | tf_op jit(solution)/shard_map/all_gather | solution.py:151
  534.8 31.0 %divide_convert_fusion = bf16[512,4,160]{0,2,1:T(8,128)(2,1)} fusion(f32[512,4]{0,1:T(4,128)S(1)} %fusion.1, bf16[8192,4,160]{0,2,1:T(8,128)(2,1)} %bitcast.85, f32[4,8192,512]{2,1,0:T(8,128)} %get-tuple-element.156, f32[512,4]{0,1:T(4,128)S(1)} %broadcast_maximum_fusion, pred[512,8192]{0,1:T(8,128)(4,1)} %fusion.7), kind=kOutput, calls=%fused_computation.48 | convolution fusion | flops 5436473344 | bytes 82460672 | tf_op jit(solution)/shard_map/qhk,khd->qhd/dot_general | solution.py:167
  565.8 6.7 %fusion.95 = f32[512,2560]{0,1:T(8,128)} fusion(bf16[640,2560]{0,1:T(8,128)(2,1)} %all-gather.14.cloned.1.call-done, bf16[512,640]{0,1:T(8,128)(2,1)} %bitcast.100), kind=kOutput, calls=%fused_computation.107 | convolution fusion | flops 1677721600 | bytes 9175040 | tf_op jit(solution)/shard_map/dot_general | solution.py:174
  572.5 90.5 %reduce-scatter.2.cloned.1.call-done = f32[512,320]{0,1:T(8,128)} async-done(((f32[512,2560]{0,1:T(8,128)}), f32[512,320]{0,1:T(8,128)}) %reduce-scatter.2.cloned.1.call-update) | async-done | bytes 655376 | tf_op jit(solution)/shard_map/reduce_scatter | solution.py:179
  (125 shorter events, 62.9 us)
Async XLA Ops:
  6.5 123.1 %copy-start = (bf16[640,2560]{1,0:T(8,128)(2,1)S(1)}, bf16[640,2560]{1,0:T(8,128)(2,1)}, u32[]{:S(2)}) copy-start(bf16[640,2560]{1,0:T(8,128)(2,1)} %param.32) | copy-start | bytes 9830404
  6.5 12.2 %copy-start.16 = (f32[2560]{0:T(1024)S(1)}, f32[2560]{0:T(1024)}, u32[]{:S(2)}) copy-start(f32[2560]{0:T(1024)} %param.23) | copy-start | bytes 30724
  6.5 12.2 %copy-start.19 = (f32[10]{0:T(128)S(1)}, f32[10]{0:T(128)}, u32[]{:S(2)}) copy-start(f32[10]{0:T(128)} %param.28) | copy-start | bytes 124
  6.5 12.2 %copy-start.14 = (bf16[2560,10]{0,1:T(8,128)(2,1)S(1)}, bf16[2560,10]{0,1:T(8,128)(2,1)}, u32[]{:S(2)}) copy-start(bf16[2560,10]{0,1:T(8,128)(2,1)} %param.27) | copy-start | bytes 153604
  6.5 75.5 %all-gather.16.cloned.1.call-start = ((), (), s32[]{:S(2)}) async-start(), calls=%async_computation.7 | async-start | bytes 5570560 | tf_op jit(solution)/shard_map/all_gather | solution.py:108
  18.8 7.8 %copy-start.11 = (f32[512]{0:T(512)}, f32[512]{0:T(512)S(1)}, u32[]{:S(2)}) copy-start(f32[512]{0:T(512)S(1)} %add_rsqrt_fusion.1) | copy-start | bytes 6148
  23.4 3.2 copy-start.2
  23.4 3.7 copy-start.13
  27.1 36.5 %copy-start.8 = (bf16[512,128]{0,1:T(8,128)(2,1)}, bf16[512,128]{0,1:T(8,128)(2,1)S(1)}, u32[]{:S(2)}) copy-start(bf16[512,128]{0,1:T(8,128)(2,1)S(1)} %divide_multiply_fusion.1) | copy-start | bytes 393220
  39.3 233.8 %all-reduce.2.cloned.1.call-start = ((), (), s32[]{:S(2)}) async-start(), calls=%async_computation.1 | async-start | bytes 10493952 | tf_op jit(solution)/shard_map/psum | solution.py:18
  114.7 8.5 %copy-start.12 = (f32[512]{0:T(512)S(1)}, f32[512]{0:T(512)}, u32[]{:S(2)}) copy-start(f32[512]{0:T(512)} %copy-done.11) | copy-start | bytes 6148
  114.7 8.4 %copy-start.17 = (f32[2560]{0:T(1024)S(1)}, f32[2560]{0:T(1024)}, u32[]{:S(2)}) copy-start(f32[2560]{0:T(1024)} %param.23) | copy-start | bytes 30724
  123.2 6.5 copy-start.18
  145.8 1.0 copy-start.9
  145.8 3.5 copy-start.7
  145.8 233.0 %all-gather.8.cloned.1.call-start = ((), (), s32[]{:S(2)}) async-start(), calls=%async_computation.2 | async-start | bytes 20889600 | tf_op jit(solution)/shard_map/all_gather | solution.py:28
  149.0 302.9 %all-gather.12.cloned.1.call-start = ((), (), s32[]{:S(2)}) async-start(), calls=%async_computation.4 | async-start | bytes 11141120 | tf_op jit(solution)/shard_map/all_gather | solution.py:150
  284.2 6.8 %copy-start.3 = (bf16[512,2560]{0,1:T(8,128)(2,1)S(1)}, bf16[512,2560]{0,1:T(8,128)(2,1)}, u32[]{:S(2)}) copy-start(bf16[512,2560]{0,1:T(8,128)(2,1)} %copy.60) | copy-start | bytes 7864324
  291.0 5.4 copy-start.6
  294.8 1.6 copy-start.4
  296.4 82.4 %copy-start.15 = (f32[5120]{0:T(1024)S(1)}, f32[5120]{0:T(1024)}, u32[]{:S(2)}) copy-start(f32[5120]{0:T(1024)} %param.33) | copy-start | bytes 61444
  297.8 91.1 %copy-start.5 = (bf16[512,2560]{0,1:T(8,128)(2,1)S(1)}, bf16[512,2560]{0,1:T(8,128)(2,1)}, u32[]{:S(2)}) copy-start(bf16[512,2560]{0,1:T(8,128)(2,1)} %copy-done.4) | copy-start | bytes 7864324
  388.8 10.1 %copy-start.10 = (s32[8192]{0:T(1024)S(1)}, s32[8192]{0:T(1024)}, u32[]{:S(2)}) copy-start(s32[8192]{0:T(1024)} %param.22) | copy-start | bytes 98308
  388.8 131.6 %all-gather.10.cloned.1.call-start = ((), (), s32[]{:S(2)}) async-start(), calls=%async_computation.3 | async-start | bytes 11141120 | tf_op jit(solution)/shard_map/all_gather | solution.py:151
  397.9 167.9 %all-gather.14.cloned.1.call-start = ((), (), s32[]{:S(2)}) async-start(), calls=%async_computation.5 | async-start | bytes 3481600 | tf_op jit(solution)/shard_map/all_gather | solution.py:176
  398.5 264.6 %reduce-scatter.2.cloned.1.call-start = ((), (), s32[]{:S(2)}) async-start(), calls=%async_computation.6 | async-start | bytes 5898240 | tf_op jit(solution)/shard_map/reduce_scatter | solution.py:179
  565.8 99.2 %copy-start.1 = (bf16[640,2560]{1,0:T(8,128)(2,1)S(1)}, bf16[640,2560]{1,0:T(8,128)(2,1)}, u32[]{:S(2)}) copy-start(bf16[640,2560]{1,0:T(8,128)(2,1)} %param.32) | copy-start | bytes 9830404
Sparse Core Ops, SparseCore 0:
  39.4 42.5 all-gather.15
  145.9 127.2 all-reduce.1
  274.9 103.8 all-gather.7
  388.9 62.9 all-gather.11
  453.5 62.9 all-gather.9
  518.0 36.7 all-gather.13
  572.7 90.3 reduce-scatter.1
where the time goes:
time: 679 us; the launch traced here: 672 us
  waiting for transfers between devices  349 us (51%)
  matrix products  127 us (19%)
  other arithmetic  82 us (12%)
  local copies, waits for them, and re-layouts  74.6 us (11%)
  blocking collectives  22.5 us (3%)
  between operations  15.3 us (2%)
    psum x1, waiting for transfers between devices, packed_total(): running = lax.psum(jnp.concatenate([a.ravel() for a in arrays]), axis)  121 us
    reduce_scatter x1, waiting for transfers between devices, local(): lax.psum_scatter(out_full, 'chan', scatter_dimension=1, tiled=True)  90.5 us
    all_gather x1, waiting for transfers between devices, side_by_side(): lax.all_gather(both, axis, axis=dim, tiled=True)  81 us
    all_gather x1, waiting for transfers between devices, local(): key_piece = lax.all_gather(keys_all, 'seq', axis=0, tiled=True)  39.1 us
    dot_general x1, matrix products, local(): jnp.einsum('qhk,khd->qhd', weights.astype(jnp.bfloat16), value_heads, pre...  31 us
    dot_general x1, matrix products, local(): jnp.einsum('qhd,khd->qhk', query_heads, key_heads, preferred_element_type...  30.4 us
    select_n x16, other arithmetic, absorb(): jnp.where(source < seq_index, all_through[source][:, None, None] * state...  30.3 us
    dot_general x3, matrix products, local(): jnp.dot(attention_input, piece_one, preferred_element_type=jnp.float32)  27.3 us
  transfers between devices with their start and end apart: 7, of which 5 were waited for; matrix products, arithmetic and copies ran while one was open for 25% of the time, Pallas kernels for 0%

commit v1 on v0

v1 whole, which is shorter than its diff:
```python
import functools
import jax
import jax.numpy as jnp
from jax import lax
from jax.experimental import pallas as pl
from jax.experimental.pallas import tpu as pltpu
from jax.sharding import PartitionSpec as P

N = 64
HEAD_CHANNELS = 64
AP = 160
EPSILON = 1e-05
MESH = pl.DeviceIdType.MESH
VMEM = pltpu.VMEM
LIMIT = 62 * 1024 * 1024
F32 = jnp.float32
BF16 = jnp.bfloat16


def normalize(values_in, gain_in):
    widened = values_in.astype(jnp.float32)
    factor = lax.rsqrt(jnp.mean(widened * widened, axis=-1, keepdims=True) + EPSILON)
    return (widened * factor * gain_in).astype(jnp.bfloat16)


def block_terms(inputs_x, steps_dt, rate_vec, b_rows, c_rows, doc_ids, prev_doc):
    block_len = inputs_x.shape[0]
    head_count = steps_dt.shape[1]
    per_head = inputs_x.shape[1] // head_count
    logdecay = steps_dt * rate_vec[None, :]
    running = jnp.cumsum(logdecay, axis=0)
    places = jnp.arange(block_len)
    allowed = (places[:, None] >= places[None, :]) & (doc_ids[:, None] == doc_ids[None, :])
    spread = running.T[:, :, None] - running.T[:, None, :]
    decays = jnp.exp(jnp.where(allowed[None], spread, -1e30))
    intersection = jnp.dot(c_rows, b_rows.T)
    scaled_x = inputs_x.reshape(block_len, head_count, per_head) * steps_dt[:, :, None]
    intra_out = jnp.einsum("hts,shp->thp", decays * intersection[None], scaled_x)
    final_doc = doc_ids[block_len - 1]
    keeping = (
        jnp.exp(running[block_len - 1][None, :] - running)
        * (doc_ids == final_doc).astype(jnp.float32)[:, None]
    )
    own_state = jnp.einsum("sn,shp->hnp", b_rows, scaled_x * keeping[:, :, None])
    through = jnp.exp(running[block_len - 1]) * (final_doc == prev_doc).astype(jnp.float32)
    entering = jnp.exp(running) * (doc_ids == prev_doc).astype(jnp.float32)[:, None]
    return (intra_out, own_state, through, entering)


def carried(c_rows, entering, state_in):
    return jnp.einsum("tn,hnp->thp", c_rows, state_in) * entering[:, :, None]


def greet(peers):
    barrier = pltpu.get_barrier_semaphore()
    for peer in peers:
        pl.semaphore_signal(barrier, inc=1, device_id=peer, device_id_type=MESH)
    pl.semaphore_wait(barrier, len(peers))


def copy_to(src, dst, send, recv, where):
    return pltpu.make_async_remote_copy(
        src_ref=src, dst_ref=dst, send_sem=send, recv_sem=recv,
        device_id=where, device_id_type=MESH,
    )


OFFSETS = ((1, 2), (1, 1), (1, 3), (0, 2), (1, 0), (0, 1), (0, 3))


def chan_peers(s, c):
    half, place = c // 4, lax.rem(c, 4)
    return [lax.rem(half + a, 2) * 4 + lax.rem(place + b, 4) for a, b in OFFSETS]


def chan_sources(s, c):
    half, place = c // 4, lax.rem(c, 4)
    return [lax.rem(half + a, 2) * 4 + lax.rem(place + 4 - b, 4) for a, b in OFFSETS]


def sum_kernel(weighted, squares, proj, hidden, mixed, part, sqbuf, recv, send_sem, recv_sem,
               sq_send, sq_recv, out_send, out_recv):
    s, c = lax.axis_index("seq"), lax.axis_index("chan")
    peers, sources = chan_peers(s, c), chan_sources(s, c)
    greet([(s, p) for p in peers])

    def columns(n, _):
        at = pl.ds(pl.multiple_of(n * 256, 256), 256)
        tile = jnp.dot(weighted[...], proj[:, at], preferred_element_type=F32)
        part[:, :, at] = tile.astype(BF16).reshape(8, 64, 256)
        return 0

    lax.fori_loop(0, 10, columns, 0)
    copies = []
    for i, p in enumerate(peers):
        small = copy_to(squares.at[p], sqbuf.at[i], sq_send.at[i], sq_recv.at[i], (s, p))
        small.start()
        big = copy_to(part.at[p], recv.at[i], send_sem.at[i], recv_sem.at[i], (s, p))
        big.start()
        copies += [small, big]
    for one in copies:
        one.wait_recv()
    rows = pl.ds(pl.multiple_of(c * 64, 64), 64)
    total = squares[c]
    for i in range(7):
        total = total + sqbuf[i]
    column = jnp.broadcast_to(total, (128, 128)).T[:64, :1]
    factor = lax.rsqrt(column / 5120.0 + EPSILON)

    def gather_sum(n, _):
        at = pl.ds(pl.multiple_of(n * 256, 256), 256)
        value = part[c, :, at].astype(F32)
        for i in range(7):
            value = value + recv[i, :, at].astype(F32)
        mixed[c, :, at] = (hidden[rows, at].astype(F32) + value * factor).astype(BF16)
        return 0

    lax.fori_loop(0, 10, gather_sum, 0)
    outs = []
    for i, p in enumerate(peers):
        one = copy_to(mixed.at[c], mixed.at[c], out_send.at[i], out_recv.at[c], (s, p))
        one.start()
        outs.append(one)
    for p in sources:
        copy_to(mixed.at[p], mixed.at[p], out_send.at[0], out_recv.at[p], (s, p)).wait_recv()
    for one in copies + outs:
        one.wait_send()


def sum_and_share(weighted, squares, proj, hidden):
    return pl.pallas_call(
        sum_kernel,
        out_shape=jax.ShapeDtypeStruct((8, 64, 2560), BF16),
        in_specs=[pl.BlockSpec(memory_space=VMEM)] * 4,
        out_specs=pl.BlockSpec(memory_space=VMEM),
        scratch_shapes=[
            VMEM((8, 64, 2560), BF16),
            VMEM((7, 1, 128), F32),
            VMEM((7, 64, 2560), BF16),
            pltpu.SemaphoreType.DMA((7,)),
            pltpu.SemaphoreType.DMA((7,)),
            pltpu.SemaphoreType.DMA((7,)),
            pltpu.SemaphoreType.DMA((7,)),
            pltpu.SemaphoreType.DMA((7,)),
            pltpu.SemaphoreType.DMA((8,)),
        ],
        compiler_params=pltpu.CompilerParams(
            collective_id=0, has_side_effects=True, vmem_limit_bytes=40 * 1024 * 1024
        ),
        cost_estimate=pl.CostEstimate(flops=60_000_000_000, bytes_accessed=9_000_000, transcendentals=0),
        name="sum_and_share",
    )(weighted, squares, proj, hidden)


def seq_parts(s):
    return s // 4, lax.rem(s // 2, 2), lax.rem(s, 2)


def seq_at(z, xl, core):
    return z * 4 + xl * 2 + core


def qkv_kernel(mixed, embedding, gain, wk, wv, wq, k_out, v_out, q_out, weights, rows_in, flat,
               w_sem, z_send, x_send, d_send, f_send, k_recv, v_recv, q_send, q_recv, local_sem):
    s, c = lax.axis_index("seq"), lax.axis_index("chan")
    z, xl, core = seq_parts(s)
    greet([(lax.rem(s + d, 16), c) for d in range(1, 16)])
    loads = []
    for i, w in enumerate((wk, wv, wq)):
        one = pltpu.make_async_copy(w, weights.at[:, pl.ds(i * 640, 640)], w_sem.at[i])
        one.start()
        loads.append(one)

    def norm(p, _):
        at = pl.ds(pl.multiple_of(p * 64, 64), 64)
        top = mixed[p].astype(F32)
        low = embedding[at, :].astype(F32)
        mean = (jnp.sum(top * top, axis=-1, keepdims=True)
                + jnp.sum(low * low, axis=-1, keepdims=True)) / 5120.0
        factor = lax.rsqrt(mean + EPSILON)
        rows_in[at, pl.ds(0, 2560)] = (top * factor * gain[:, pl.ds(0, 2560)]).astype(BF16)
        rows_in[at, pl.ds(2560, 2560)] = (low * factor * gain[:, pl.ds(2560, 2560)]).astype(BF16)
        return 0

    lax.fori_loop(0, 8, norm, 0)

    def tile(n, _):
        at = pl.ds(pl.multiple_of(n * 256, 256), 256)
        value = jnp.dot(rows_in[...], weights[:, at], preferred_element_type=F32)
        flat[at, :] = value.T.astype(BF16)
        return 0

    waits = []

    def first_stage(base, out, recv, lane):
        mine = pltpu.make_async_copy(
            flat.at[pl.ds(pl.multiple_of(base + z * 160, 32), 160), :], out.at[s], local_sem.at[lane])
        mine.start()
        for d in (2, 1, 3):
            to = lax.rem(z + d, 4)
            one = copy_to(
                flat.at[pl.ds(pl.multiple_of(base + to * 160, 32), 160), :], out.at[s],
                z_send.at[lane, d - 1], recv.at[s], (seq_at(to, xl, core), c))
            one.start()
            waits.append(one)
        return mine

    def pass_on(out, recv, lane, d, own):
        block = seq_at(lax.rem(z + 4 - d, 4), xl, core)
        if own is None:
            copy_to(out.at[block], out.at[block], z_send.at[lane, 0], recv.at[block], (block, c)).wait_recv()
        else:
            own.wait()
        across = copy_to(out.at[block], out.at[block], x_send.at[lane, d], recv.at[block],
                         (seq_at(z, 1 - xl, core), c))
        across.start()
        beside = copy_to(out.at[block], out.at[block], d_send.at[lane, d], recv.at[block],
                         (seq_at(z, xl, 1 - core), c))
        beside.start()
        waits.append(across)
        waits.append(beside)

    def relay(out, recv, lane, d):
        block = seq_at(lax.rem(z + 4 - d, 4), 1 - xl, core)
        copy_to(out.at[block], out.at[block], z_send.at[lane, 0], recv.at[block],
                (seq_at(z, 1 - xl, core), c)).wait_recv()
        beside = copy_to(out.at[block], out.at[block], f_send.at[lane, d], recv.at[block],
                         (seq_at(z, xl, 1 - core), c))
        beside.start()
        waits.append(beside)

    def settle(out, recv, d, side):
        block = seq_at(lax.rem(z + 4 - d, 4), side, 1 - core)
        copy_to(out.at[block], out.at[block], z_send.at[0, 0], recv.at[block],
                (seq_at(z, xl, 1 - core), c)).wait_recv()

    loads[0].wait()
    loads[1].wait()
    lax.fori_loop(0, 3, tile, 0)
    own_k = first_stage(0, k_out, k_recv, 0)
    pass_on(k_out, k_recv, 0, 0, own_k)
    lax.fori_loop(3, 5, tile, 0)
    own_v = first_stage(640, v_out, v_recv, 1)
    pass_on(v_out, v_recv, 1, 0, own_v)
    loads[2].wait()
    lax.fori_loop(5, 7, tile, 0)
    last = pl.ds(1792, 128)
    flat[last, :] = jnp.dot(rows_in[...], weights[:, last], preferred_element_type=F32).T.astype(BF16)
    quarter = xl * 2 + core
    for d in range(16):
        to = lax.rem(s + d, 16)
        piece = flat.at[pl.ds(pl.multiple_of(1280 + (to // 4) * 160, 32), 160),
                        pl.ds(pl.multiple_of(lax.rem(to, 4) * 128, 128), 128)]
        if d == 0:
            own_q = pltpu.make_async_copy(piece, q_out.at[s], local_sem.at[2])
            own_q.start()
        else:
            one = copy_to(piece, q_out.at[s], q_send.at[d - 1], q_recv.at[s], (to, c))
            one.start()
            waits.append(one)
    for d in (1, 3, 2):
        pass_on(k_out, k_recv, 0, d, None)
    relay(k_out, k_recv, 0, 0)
    for d in (1, 3, 2):
        pass_on(v_out, v_recv, 1, d, None)
    relay(v_out, v_recv, 1, 0)
    for d in (1, 3, 2):
        relay(k_out, k_recv, 0, d)
    for d in (1, 3, 2):
        relay(v_out, v_recv, 1, d)
    for d in (0, 1, 3, 2):
        for side in (0, 1):
            settle(k_out, k_recv, d, side)
            settle(v_out, v_recv, d, side)
    own_q.wait()
    for d in range(1, 16):
        block = lax.rem(s + d, 16)
        copy_to(q_out.at[block], q_out.at[block], q_send.at[0], q_recv.at[block], (block, c)).wait_recv()
    for one in waits:
        one.wait_send()


def project(mixed, embedding, gain, wk, wv, wq):
    dma = pltpu.SemaphoreType.DMA
    vm, anyw = pl.BlockSpec(memory_space=VMEM), pl.BlockSpec(memory_space=pl.ANY)
    return pl.pallas_call(
        qkv_kernel,
        out_shape=(
            jax.ShapeDtypeStruct((16, 160, 512), BF16),
            jax.ShapeDtypeStruct((16, 160, 512), BF16),
            jax.ShapeDtypeStruct((16, 160, 128), BF16),
        ),
        in_specs=[vm, vm, vm, anyw, anyw, anyw],
        out_specs=(vm, vm, vm),
        scratch_shapes=[
            VMEM((5120, 1920), BF16),
            VMEM((512, 5120), BF16),
            VMEM((1920, 512), BF16),
            dma((3,)),
            dma((2, 3)),
            dma((2, 4)),
            dma((2, 4)),
            dma((2, 4)),
            dma((16,)),
            dma((16,)),
            dma((15,)),
            dma((16,)),
            dma((3,)),
        ],
        compiler_params=pltpu.CompilerParams(
            collective_id=1, has_side_effects=True, vmem_limit_bytes=LIMIT
        ),
        cost_estimate=pl.CostEstimate(flops=60_000_000_000, bytes_accessed=30_000_000, transcendentals=0),
        name="project",
    )(mixed, embedding, gain, wk, wv, wq)


def attend_kernel(ends, q_in, k_in, v_in, out):
    quarter = lax.rem(lax.axis_index("seq"), 4)
    i = pl.program_id(0)
    first, second = ends[0], ends[1]
    queries = jnp.concatenate(
        [q_in[2 * i].astype(F32).T, q_in[2 * i + 1].astype(F32).T], axis=0
    ).astype(BF16)
    row = lax.broadcasted_iota(jnp.int32, (256, 1), 0)
    place = i * 1024 + quarter * 128 + row + jnp.where(row >= 128, 384, 0)

    def start_of(p):
        return jnp.where(p >= second, second, jnp.where(p >= first, first, 0))

    begin = start_of(place)
    low_place = i * 1024 + quarter * 128
    top_begin = start_of(low_place + 512 + 127)
    low_begin = start_of(low_place)
    lowest = low_begin // 512
    scale = (AP ** -0.5) * 1.4426950408889634

    def step(b, carry, masked):
        top, total, acc = carry
        scores = jnp.dot(queries, k_in[b], preferred_element_type=F32)
        if masked:
            key = b * 512 + lax.broadcasted_iota(jnp.int32, (256, 512), 1)
            visible = (key >= begin) & (key <= place)
            scores = jnp.where(visible, scores, -1e30)
        new_top = jnp.maximum(top, jnp.max(scores, axis=-1, keepdims=True))
        weights = jnp.exp2((scores - new_top) * scale)
        if masked:
            weights = jnp.where(visible, weights, 0.0)
        keep = jnp.exp2((top - new_top) * scale)
        total = total * keep + jnp.sum(weights, axis=-1, keepdims=True)
        acc = acc * keep + lax.dot_general(
            weights.astype(BF16), v_in[b], (((1,), (1,)), ((), ())), preferred_element_type=F32
        )
        return new_top, total, acc

    carry = (jnp.full((256, 1), -1e30, F32), jnp.zeros((256, 1), F32), jnp.zeros((256, AP), F32))
    plain_from = jnp.minimum((top_begin + 511) // 512, 2 * i)
    carry = lax.fori_loop(lowest, plain_from, lambda b, t: step(b, t, True), carry)
    carry = lax.fori_loop(jnp.maximum(lowest, plain_from), 2 * i, lambda b, t: step(b, t, False), carry)
    carry = lax.fori_loop(jnp.maximum(lowest, 2 * i), 2 * i + 2, lambda b, t: step(b, t, True), carry)
    top, total, acc = carry
    context = (acc / total).T.astype(BF16)
    out[0] = context[:, :128]
    out[1] = context[:, 128:]


def attend(ends, q_in, k_in, v_in):
    vm = pl.BlockSpec(memory_space=VMEM)
    return pl.pallas_call(
        attend_kernel,
        out_shape=jax.ShapeDtypeStruct((16, 160, 128), BF16),
        grid=(8,),
        in_specs=[pl.BlockSpec(memory_space=pltpu.SMEM), vm, vm, vm],
        out_specs=pl.BlockSpec((2, 160, 128), lambda i: (i, 0, 0)),
        compiler_params=pltpu.CompilerParams(vmem_limit_bytes=40 * 1024 * 1024),
        cost_estimate=pl.CostEstimate(flops=10_000_000_000, bytes_accessed=6_000_000, transcendentals=0),
        name="attend",
    )(ends, q_in, k_in, v_in)


def finish_kernel(ctx, proj_t, out, gathered, part, recv, in_send, in_recv, send_sem, recv_sem, local_sem):
    s, c = lax.axis_index("seq"), lax.axis_index("chan")
    peers, sources = chan_peers(s, c), chan_sources(s, c)
    greet([(s, p) for p in peers] + [(lax.rem(s + d, 16), c) for d in range(1, 16)])
    z = s // 4
    lanes = pl.ds(pl.multiple_of(lax.rem(s, 4) * 128, 128), 128)
    waits = []
    for d in range(16):
        to = lax.rem(s + d, 16)
        where = gathered.at[pl.ds(pl.multiple_of(z * 160, 32), 160), lanes]
        if d == 0:
            own = pltpu.make_async_copy(ctx.at[s], where, local_sem.at[0])
            own.start()
        else:
            one = copy_to(ctx.at[to], where, in_send.at[d - 1], in_recv.at[s], (to, c))
            one.start()
            waits.append(one)
    own.wait()
    for d in range(1, 16):
        block = lax.rem(s + d, 16)
        where = gathered.at[pl.ds(pl.multiple_of((block // 4) * 160, 32), 160),
                            pl.ds(pl.multiple_of(lax.rem(block, 4) * 128, 128), 128)]
        copy_to(ctx.at[0], where, in_send.at[0], in_recv.at[block], (block, c)).wait_recv()
    copies = []
    for i, p in enumerate(peers):
        at = pl.ds(pl.multiple_of(p * 320, 32), 320)
        part[p] = jnp.dot(proj_t[at, :], gathered[...], preferred_element_type=F32).astype(BF16)
        one = copy_to(part.at[p], recv.at[i], send_sem.at[i], recv_sem.at[i], (s, p))
        one.start()
        copies.append(one)
    at = pl.ds(pl.multiple_of(c * 320, 32), 320)
    value = jnp.dot(proj_t[at, :], gathered[...], preferred_element_type=F32)
    for i in (6, 5, 4, 3, 2, 1, 0):
        copies[i].wait_recv()
        value = value + recv[i].astype(F32)
    out[...] = value.T
    for one in waits + copies:
        one.wait_send()


def finish(ctx, proj_t):
    dma = pltpu.SemaphoreType.DMA
    vm = pl.BlockSpec(memory_space=VMEM)
    return pl.pallas_call(
        finish_kernel,
        out_shape=jax.ShapeDtypeStruct((512, 320), F32),
        in_specs=[vm, vm],
        out_specs=vm,
        scratch_shapes=[
            VMEM((640, 512), BF16),
            VMEM((8, 320, 512), BF16),
            VMEM((7, 320, 512), BF16),
            dma((15,)),
            dma((16,)),
            dma((7,)),
            dma((7,)),
            dma((1,)),
        ],
        compiler_params=pltpu.CompilerParams(
            collective_id=2, has_side_effects=True, vmem_limit_bytes=40 * 1024 * 1024
        ),
        cost_estimate=pl.CostEstimate(flops=50_000_000_000, bytes_accessed=6_000_000, transcendentals=0),
        name="finish",
    )(ctx, proj_t)


def local(
    hidden,
    embedding,
    segments,
    input_norm_gain,
    gate_proj,
    input_proj,
    state_proj,
    step_proj,
    step_bias,
    decay_log,
    skip_gain,
    out_gain,
    out_proj,
    attn_gain,
    query_proj,
    key_proj,
    value_proj,
    attn_out,
):
    tok_rows = hidden.shape[0]
    seq_index = lax.axis_index("seq")
    chan_index = lax.axis_index("chan")
    row_start = seq_index * tok_rows
    wk, wv, wq = (lax.all_gather(w, "seq", axis=0, tiled=True) for w in (key_proj, value_proj, query_proj))
    proj_t = lax.all_gather(attn_out.T, "seq", axis=0, tiled=True)
    ends = jnp.stack([jnp.sum((segments < 1).astype(jnp.int32)), jnp.sum((segments < 2).astype(jnp.int32))])
    tokens_n = normalize(hidden, input_norm_gain)
    gate_z = jnp.dot(tokens_n, gate_proj, preferred_element_type=jnp.float32)
    inputs_x = jax.nn.silu(jnp.dot(tokens_n, input_proj, preferred_element_type=jnp.float32))
    b_and_c = jax.nn.silu(jnp.dot(tokens_n, state_proj, preferred_element_type=jnp.float32))
    b_rows = b_and_c[:, :N]
    c_rows = b_and_c[:, N:]
    steps_dt = jax.nn.softplus(
        jnp.dot(tokens_n, step_proj, preferred_element_type=jnp.float32) + step_bias[None, :]
    )
    rate_vec = -jnp.exp(decay_log)
    doc_ids = lax.dynamic_slice_in_dim(segments, row_start, tok_rows)
    before = lax.dynamic_slice_in_dim(segments, jnp.maximum(row_start - 1, 0), 1)[0]
    prev_doc = jnp.where(seq_index > 0, before, -1)
    intra_out, own_state, through, entering = block_terms(
        inputs_x, steps_dt, rate_vec, b_rows, c_rows, doc_ids, prev_doc
    )
    packed = jnp.concatenate(
        [own_state, jnp.broadcast_to(through[:, None, None], (10, 1, HEAD_CHANNELS))], axis=1
    )
    everything = lax.all_gather(packed, "seq", axis=0)
    all_states, all_through = everything[:, :, :N], everything[:, :, N, 0]
    spots = jnp.arange(16)
    between = (spots[None, :] > spots[:, None]) & (spots[None, :] < seq_index)
    factors = jnp.prod(jnp.where(between[:, :, None], all_through[None], 1.0), axis=1)
    factors = jnp.where((spots < seq_index)[:, None], factors, 0.0)
    state_in = jnp.sum(all_states * factors[:, :, None, None], axis=0)
    mixed_y = intra_out + carried(c_rows, entering, state_in)
    y_full = (
        mixed_y.reshape(tok_rows, -1) + inputs_x * jnp.repeat(skip_gain, HEAD_CHANNELS)[None, :]
    )
    gated = y_full * jax.nn.silu(gate_z)
    squares = jnp.sum(gated * gated, axis=-1)
    weighted = (gated * out_gain[None, :]).astype(jnp.bfloat16)
    squares = jnp.pad(squares.reshape(8, 1, 64), ((0, 0), (0, 0), (0, 64)))
    mixed = sum_and_share(weighted, squares, out_proj, hidden)
    k_all, v_all, q_all = project(mixed, embedding, attn_gain[None, :], wk, wv, wq)
    ctx = attend(ends, q_all, k_all, v_all)
    out_share = finish(ctx, proj_t)
    own_mixed = lax.dynamic_slice_in_dim(mixed.reshape(512, 2560), chan_index * 320, 320, 1)
    return (out_share + own_mixed.astype(jnp.float32)).astype(jnp.bfloat16)


def solution(mesh):
    in_specs = (
        P("seq", None),
        P("seq", None),
        P(),
        P(),
        P(None, "chan"),
        P(None, "chan"),
        P(),
        P(None, "chan"),
        P("chan"),
        P("chan"),
        P("chan"),
        P("chan"),
        P("chan", None),
        P(),
        P("seq", "chan"),
        P("seq", "chan"),
        P("seq", "chan"),
        P("chan", "seq"),
    )
    out_specs = P("seq", "chan")
    return jax.shard_map(local, mesh=mesh, in_specs=in_specs, out_specs=out_specs, check_vma=False)
```

time: 679 us -> 418 us (0.62)
  waiting for transfers between devices: 349 us -> 87.6 us
  Pallas kernels: 0 us -> 259 us
  matrix products: 127 us -> 21.5 us
  other arithmetic: 82 us -> 13.1 us
  local copies, waits for them, and re-layouts: 74.6 us -> 20.9 us
  blocking collectives: 22.5 us -> 0 us
    pallas_call x0 -> x4, Pallas kernels: none -> 259 us  [the longest x1 111 us: sum_and_share(): pl.pallas_call(sum_kernel, out_shape=jax.ShapeDtypeStruct((8, 64, 2560),...]
    psum x1 -> x0, waiting for transfers between devices: 121 us -> none  [packed_total(): running = lax.psum(jnp.concatenate([a.ravel() for a in arrays]), axis)]
    dot_general x7 -> x0, matrix products: 99.9 us -> none  [the longest x1 31 us: local(): jnp.einsum('qhk,khd->qhd', weights.astype(jnp.bfloat16), value_heads, pre...]
    reduce_scatter x1 -> x0, waiting for transfers between devices: 90.5 us -> none  [local(): lax.psum_scatter(out_full, 'chan', scatter_dimension=1, tiled=True)]
    all_gather x5, waiting for transfers between devices: 137 us -> 85.2 us  [the longest x3 49 us: local(): lax.all_gather(w, 'seq', axis=0, tiled=True)]
    select_n x16 -> x1, other arithmetic: 30.3 us -> 0.01 us  [local(): factors = jnp.where((spots < seq_index)[:, None], factors, 0.0)]
    all_gather x2 -> x0, local copies, waits for them, and re-layouts: 28.8 us -> none  [the longest x1 14.4 us: local(): value_piece = lax.all_gather(values_all, 'seq', axis=0, tiled=True)]
    all_gather x1 -> x0, blocking collectives: 22.5 us -> none  [local(): lax.all_gather(through[None], 'seq', axis=0, tiled=True)]
  transfers between devices with their start and end apart: 7 -> 5, of which waited for: 5 -> 3; matrix products, arithmetic and copies ran while one was open for 25% -> 5% of each run, Pallas kernels for 0% -> 51%
where the time goes in v1:
time: 418 us; the launch traced here: 417 us
  Pallas kernels  259 us (62%)
  waiting for transfers between devices  87.6 us (21%)
  matrix products  21.5 us (5%)
  local copies, waits for them, and re-layouts  20.9 us (5%)
  between operations  14.8 us (4%)
  other arithmetic  13.1 us (3%)
    pallas_call x1, Pallas kernels, sum_and_share(): pl.pallas_call(sum_kernel, out_shape=jax.ShapeDtypeStruct((8, 64, 2560),...  111 us
    pallas_call x1, Pallas kernels, project(): pl.pallas_call(qkv_kernel, out_shape=(jax.ShapeDtypeStruct((16, 160, 512)...  70.1 us
    all_gather x3, waiting for transfers between devices, local(): lax.all_gather(w, 'seq', axis=0, tiled=True)  49 us
    pallas_call x1, Pallas kernels, finish(): pl.pallas_call(finish_kernel, out_shape=jax.ShapeDtypeStruct((512, 320),...  47.6 us
    all_gather x1, waiting for transfers between devices, local(): everything = lax.all_gather(packed, 'seq', axis=0)  36.2 us
    pallas_call x1, Pallas kernels, attend(): pl.pallas_call(attend_kernel, out_shape=jax.ShapeDtypeStruct((16, 160, 12...  30.7 us
    unnamed x42, local copies, waits for them, and re-layouts  10.1 us
  transfers between devices with their start and end apart: 5, of which 3 were waited for; matrix products, arithmetic and copies ran while one was open for 5% of the time, Pallas kernels for 51%

profile of v1, /device:TPU:1, one launch (start us, length us, event | category | flops | bytes accessed | tf_op | source)
XLA Modules:
  0.0 417.3 jit_solution(851930250625094643)
XLA Ops:
  6.6 1.4 dynamic_slice.10
  8.7 0.8 compare_convert_fusion
  11.3 2.3 fusion.5
  13.7 1.8 fusion.38
  15.5 1.2 reduce-window.6
  17.2 5.8 %divide_multiply_fusion = (f32[512,640]{1,0:T(8,128)}, f32[512,640]{1,0:T(8,128)}) fusion(bf16[2560,640]{1,0:T(8,128)(2,1)} %param.23, bf16[512,2560]{1,0:T(8,128)(2,1)S(1)} %copy-done.2, f32[2560]{0:T(1024)S(1)} %copy-done.15, f32[512]{0:T(512)S(1)} %add_rsqrt_fusion), kind=kOutput, calls=%fused_computation.24 | convolution fusion | flops 1684275200 | bytes 8531968 | tf_op jit(solution)/shard_map/dot_general | solution.py:476
  23.0 2.8 copy.50
  25.8 1.1 divide_multiply_fusion.1
  27.1 1.6 fusion.24
  28.8 0.9 pad_maximum_fusion
  32.6 1.3 fusion.33
  34.8 1.4 pad_add_fusion.ends
  36.1 36.2 %all-gather.15.cloned.1.call-done = f32[160,65,64]{1,2,0:T(8,128)} async-done(((f32[10,65,64]{1,2,0:T(8,128)}), f32[160,65,64]{1,2,0:T(8,128)}) %all-gather.15.cloned.1.call-update) | async-done | bytes 2662416 | tf_op jit(solution)/shard_map/all_gather | solution.py:493
  72.3 1.3 slice.38
  74.2 3.2 fusion.8
  77.7 4.2 fusion.17
  81.9 2.8 copy.55
  84.8 5.5 %multiply_reduce_fusion = (f32[512]{0:T(512)S(1)}, bf16[512,640]{1,0:T(8,128)(2,1)S(1)}) fusion(f32[640]{0:T(1024)S(1)} %copy-done.17, bf16[2560,640]{1,0:T(8,128)(2,1)} %param.22, bf16[512,2560]{1,0:T(8,128)(2,1)S(1)} %copy-done.2, f32[2560]{0:T(1024)S(1)} %copy-done.16, f32[512]{0:T(512)S(1)} %copy-done.13, f32[512,640]{1,0:T(8,128)} %copy.55, ...), kind=kOutput, calls=%fused_computation.19 | convolution fusion | flops 1687879168 | bytes 9194496 | tf_op jit(solution)/shard_map/dot_general | solution.py:475
  90.3 2.0 copy-done.4
  92.3 110.9 %sum_and_share.1.mixed = bf16[8,64,2560]{2,1,0:T(8,128)(2,1)S(1)} custom-call(bf16[512,640]{1,0:T(8,128)(2,1)S(1)} %get-tuple-element.16.weighted, f32[8,1,128]{2,1,0:T(1,128)S(1)} %pad.4.squares, bf16[640,2560]{1,0:T(8,128)(2,1)S(1)} %copy-done.4, bf16[512,2560]{1,0:T(8,128)(2,1)S(1)} %copy-done.2), custom_call_target="tpu_custom_call" | custom-call | flops 60000002048 | bytes 9000000 | tf_op jit(solution)/shard_map/sum_and_share/pallas_call | solution.py:131
  203.2 1.5 copy-done.3
  204.8 3.8 all-gather.7.cloned.1.call-done.wk
  208.5 45.2 %all-gather.9.cloned.1.call-done.wv = bf16[5120,640]{1,0:T(8,128)(2,1)} async-done(((bf16[320,640]{1,0:T(8,128)(2,1)}), bf16[5120,640]{1,0:T(8,128)(2,1)}) %all-gather.9.cloned.1.call-update) | async-done | bytes 6553616 | tf_op jit(solution)/shard_map/all_gather | solution.py:471
  253.8 70.1 %project.1 = (bf16[16,160,512]{2,1,0:T(8,128)(2,1)}, bf16[16,160,512]{2,1,0:T(8,128)(2,1)}, bf16[16,160,128]{2,1,0:T(8,128)(2,1)}) custom-call(bf16[8,64,2560]{2,1,0:T(8,128)(2,1)} %copy-done.3, bf16[512,2560]{1,0:T(8,128)(2,1)} %embedding.1, f32[1,5120]{1,0:T(1,128)} %bitcast.66, bf16[5120,640]{1,0:T(8,128)(2,1)} %all-gather.7.cloned.1.call-done.wk, ...), custom_call_target="tpu_custom_call" | custom-call | flops 60000002048 | bytes 30000000 | tf_op jit(solution)/shard_map/project/pallas_call | solution.py:286
  323.9 1.7 copy-done.6
  325.6 1.7 copy-done.7
  327.3 1.1 copy-done.8
  328.4 30.7 %attend.1.ctx = bf16[16,160,128]{2,1,0:T(8,128)(2,1)S(1)} custom-call(s32[2]{0:T(128)S(1)} %pad_add_fusion.ends, bf16[16,160,128]{2,1,0:T(8,128)(2,1)S(1)} %copy-done.8, bf16[16,160,512]{2,1,0:T(8,128)(2,1)S(1)} %copy-done.6, bf16[16,160,512]{2,1,0:T(8,128)(2,1)S(1)} %copy-done.7), custom_call_target="tpu_custom_call" | custom-call | flops 10000000000 | bytes 6000000 | tf_op jit(solution)/shard_map/attend/pallas_call | solution.py:369
  359.2 1.9 copy-done.5
  361.1 47.6 %finish.1 = f32[512,320]{1,0:T(8,128)S(1)} custom-call(bf16[16,160,128]{2,1,0:T(8,128)(2,1)S(1)} %attend.1.ctx, bf16[2560,640]{1,0:T(8,128)(2,1)S(1)} %copy-done.5), custom_call_target="tpu_custom_call" | custom-call | flops 49999998976 | bytes 6000000 | tf_op jit(solution)/shard_map/finish/pallas_call | solution.py:424
  408.7 1.3 add_convert_fusion
  409.9 0.9 copy.56
  (76 shorter events, 6.7 us)
Async XLA Ops:
  6.5 19.3 %copy-start = (bf16[2560,128]{1,0:T(8,128)(2,1)S(1)}, bf16[2560,128]{1,0:T(8,128)(2,1)}, u32[]{:S(2)}) copy-start(bf16[2560,128]{1,0:T(8,128)(2,1)} %param.24) | copy-start | bytes 1966084
  6.5 7.2 %copy-start.2 = (bf16[512,2560]{1,0:T(8,128)(2,1)S(1)}, bf16[512,2560]{1,0:T(8,128)(2,1)}, u32[]{:S(2)}) copy-start(bf16[512,2560]{1,0:T(8,128)(2,1)} %hidden.1) | copy-start | bytes 7864324
  6.5 7.1 %copy-start.18 = (f32[10]{0:T(128)S(1)}, f32[10]{0:T(128)}, u32[]{:S(2)}) copy-start(f32[10]{0:T(128)} %param.27) | copy-start | bytes 124
  6.5 7.2 %copy-start.15 = (f32[2560]{0:T(1024)S(1)}, f32[2560]{0:T(1024)}, u32[]{:S(2)}) copy-start(f32[2560]{0:T(1024)} %param.21) | copy-start | bytes 30724
  6.5 7.2 %copy-start.19 = (f32[10]{0:T(128)S(1)}, f32[10]{0:T(128)}, u32[]{:S(2)}) copy-start(f32[10]{0:T(128)} %param.26) | copy-start | bytes 124
  6.5 65.8 %all-gather.15.cloned.1.call-start = ((), (), s32[]{:S(2)}) async-start(), calls=%async_computation.4 | async-start | bytes 5570560 | tf_op jit(solution)/shard_map/all_gather | solution.py:493
  13.7 12.1 %copy-start.12 = (f32[512]{0:T(512)}, f32[512]{0:T(512)S(1)}, u32[]{:S(2)}) copy-start(f32[512]{0:T(512)S(1)} %add_rsqrt_fusion) | copy-start | bytes 6148
  28.7 5.2 %copy-start.11 = (s32[8192]{0:T(1024)S(1)}, s32[8192]{0:T(1024)}, u32[]{:S(2)}) copy-start(s32[8192]{0:T(1024)} %param.20) | copy-start | bytes 98308
  28.7 5.9 %copy-start.14 = (f32[10]{0:T(128)S(1)}, f32[10]{0:T(128)}, u32[]{:S(2)}) copy-start(f32[10]{0:T(128)} %param.28) | copy-start | bytes 124
  29.7 175.0 %all-gather.11.cloned.1.call-start = ((), (), s32[]{:S(2)}) async-start(), calls=%async_computation.2 | async-start | bytes 6963200 | tf_op jit(solution)/shard_map/all_gather | solution.py:471
  30.5 178.0 %all-gather.7.cloned.1.call-start = ((), (), s32[]{:S(2)}) async-start(), calls=%async_computation | async-start | bytes 6963200 | tf_op jit(solution)/shard_map/all_gather | solution.py:471
  31.2 222.5 %all-gather.9.cloned.1.call-start = ((), (), s32[]{:S(2)}) async-start(), calls=%async_computation.1 | async-start | bytes 6963200 | tf_op jit(solution)/shard_map/all_gather | solution.py:471
  31.8 327.4 %all-gather.13.cloned.1.call-start = ((), (), s32[]{:S(2)}) async-start(), calls=%async_computation.3 | async-start | bytes 3481600 | tf_op jit(solution)/shard_map/all_gather | solution.py:472
  74.2 3.5 copy-start.9
  74.2 3.5 copy-start.10
  81.9 2.8 copy-start.13
  81.9 2.8 copy-start.16
  81.9 2.8 copy-start.17
  90.3 2.0 copy-start.4
  203.2 1.6 copy-start.3
  323.8 1.7 copy-start.6
  325.6 1.7 copy-start.7
  327.3 1.1 copy-start.8
  359.1 1.9 copy-start.5
  361.1 49.7 %copy-start.1 = (bf16[2560,128]{1,0:T(8,128)(2,1)S(1)}, bf16[2560,128]{1,0:T(8,128)(2,1)}, u32[]{:S(2)}) copy-start(bf16[2560,128]{1,0:T(8,128)(2,1)} %param.24) | copy-start | bytes 1966084
Sparse Core Ops, SparseCore 0:
  29.8 42.4 all-gather.14
  74.0 57.2 all-gather.10
  133.1 75.3 all-gather.6
  210.1 43.6 all-gather.8
  255.3 53.3 all-gather.12

commit v2 on v1

v2 whole, which is shorter than its diff:
```python
import jax
import jax.numpy as jnp
from jax import lax
from jax.experimental import pallas as pl
from jax.experimental.pallas import tpu as pltpu
from jax.sharding import PartitionSpec as P

N = 64
HEAD_CHANNELS = 64
AP = 160
EPSILON = 1e-05
MESH = pl.DeviceIdType.MESH
VMEM = pltpu.VMEM
LIMIT = 62 * 1024 * 1024
F32 = jnp.float32
BF16 = jnp.bfloat16


def greet(peers):
    barrier = pltpu.get_barrier_semaphore()
    for peer in peers:
        pl.semaphore_signal(barrier, inc=1, device_id=peer, device_id_type=MESH)
    pl.semaphore_wait(barrier, len(peers))


def copy_to(src, dst, send, recv, where):
    return pltpu.make_async_remote_copy(
        src_ref=src, dst_ref=dst, send_sem=send, recv_sem=recv,
        device_id=where, device_id_type=MESH,
    )


OFFSETS = ((1, 2), (1, 1), (1, 3), (0, 2), (1, 0), (0, 1), (0, 3))


def chan_peers(s, c):
    half, place = c // 4, lax.rem(c, 4)
    return [lax.rem(half + a, 2) * 4 + lax.rem(place + b, 4) for a, b in OFFSETS]


def chan_sources(s, c):
    half, place = c // 4, lax.rem(c, 4)
    return [lax.rem(half + a, 2) * 4 + lax.rem(place + 4 - b, 4) for a, b in OFFSETS]


def seq_parts(s):
    return s // 4, lax.rem(s // 2, 2), lax.rem(s, 2)


def seq_at(z, xl, core):
    return z * 4 + xl * 2 + core


def start_of(place, first, second):
    return jnp.where(place >= second, second, jnp.where(place >= first, first, 0))


def silu(v):
    return v / (1.0 + jnp.exp(-v))


def front_kernel(ends, hidden, norm_gain, input_w, gate_w, state_w, small, out_w, embedding, attn_gain,
                 wk, wv, wq, p_in,
                 mixed, k_out, v_out, q_out, p_out,
                 hid, iw, gw, sw, ow, w, rows_in, part, recv, flat_t, run_e, xs, ys, states, tx, rx, planes,
                 run_rows, run_cols, step_e, bc_rows, bc_cols, pb, sq_all, sq_cols, weighted,
                 load_sem, w_send, w_recv, p_send, p_recv, st_send, st_recv,
                 sq_send, sq_recv, rs_send, rs_recv, ag_send, ag_recv,
                 z_send, x_send, d_send, f_send, k_recv, v_recv, q_send, q_recv, local_sem):
    s, c = lax.axis_index("seq"), lax.axis_index("chan")
    z, xl, core = seq_parts(s)
    peers, sources = chan_peers(s, c), chan_sources(s, c)
    up, down, far = lax.rem(z + 1, 4), lax.rem(z + 3, 4), lax.rem(z + 2, 4)
    waits = []

    def load(i, src, dst):
        one = pltpu.make_async_copy(src, dst, load_sem.at[i])
        one.start()
        return one

    own_rows = pl.ds(pl.multiple_of(s * 320, 64), 320)
    w_loads = [load(i, src, w.at[own_rows, pl.ds(i * 640, 640)]) for i, src in enumerate((wk, wv, wq))]
    l_hid = load(3, hidden, hid)
    l_sw = load(4, state_w, sw)
    l_iw = load(5, input_w, iw)
    l_pb = load(6, p_in, pb)
    l_gw = load(7, gate_w, gw)
    l_ow = load(8, out_w, ow)
    greet([(s, p) for p in peers] + [(lax.rem(s + d, 16), c) for d in range(1, 16)])

    used = [0, 0]

    def w_rows(block, half):
        return w.at[pl.ds(pl.multiple_of(block * 320 + half * 160, 32), 160), :]

    def w_to(block, half, to):
        rows = w_rows(block, half)
        one = copy_to(rows, rows, w_send.at[used[0]], w_recv.at[block, half], (to, c))
        used[0] += 1
        one.start()
        waits.append(one)

    def w_wait(block, half):
        rows = w_rows(block, half)
        copy_to(rows, rows, w_send.at[0], w_recv.at[block, half], (seq_at(z, xl, 1 - core), c)).wait_recv()

    def p_rows(block):
        return p_out.at[pl.ds(pl.multiple_of(block * 160, 32), 160), :]

    def p_to(block, to, src=None):
        rows = p_rows(block)
        one = copy_to(rows if src is None else src, rows, p_send.at[used[1]], p_recv.at[block], (to, c))
        used[1] += 1
        one.start()
        waits.append(one)

    def p_wait(block):
        rows = p_rows(block)
        copy_to(rows, rows, p_send.at[0], p_recv.at[block], (seq_at(z, xl, 1 - core), c)).wait_recv()

    sibling = seq_at(z, xl, 1 - core)

    def w_first(half):
        w_to(s, half, seq_at(z, 1 - xl, core))
        w_to(s, half, seq_at(up, xl, core))
        w_to(s, half, seq_at(down, xl, core))
        w_to(s, half, sibling)

    def w_second():
        block = seq_at(z, 1 - xl, core)
        for half in (0, 1):
            w_wait(block, half)
            w_to(block, half, seq_at(up, xl, core))
            w_to(block, half, seq_at(down, xl, core))
            w_to(block, half, sibling)
        for half in (0, 1):
            w_wait(seq_at(down, xl, core), half)
            w_wait(seq_at(up, xl, core), half)
        w_to(seq_at(down, xl, core), 0, seq_at(up, xl, core))
        w_to(seq_at(up, xl, core), 1, seq_at(down, xl, core))
        for half in (0, 1):
            w_to(seq_at(down, xl, core), half, sibling)
            w_to(seq_at(up, xl, core), half, sibling)

    def w_third():
        for half in (0, 1):
            w_wait(seq_at(down, 1 - xl, core), half)
            w_wait(seq_at(up, 1 - xl, core), half)
        w_to(seq_at(down, 1 - xl, core), 0, seq_at(up, xl, core))
        w_to(seq_at(up, 1 - xl, core), 1, seq_at(down, xl, core))
        for half in (0, 1):
            w_to(seq_at(down, 1 - xl, core), half, sibling)
            w_to(seq_at(up, 1 - xl, core), half, sibling)
        for half in (0, 1):
            w_wait(seq_at(far, xl, core), half)
            w_to(seq_at(far, xl, core), half, sibling)

    def w_last():
        for half in (0, 1):
            w_wait(seq_at(far, 1 - xl, core), half)
            w_to(seq_at(far, 1 - xl, core), half, sibling)
        for zz in range(4):
            for xx in range(2):
                for half in (0, 1):
                    w_wait(seq_at(zz, xx, 1 - core), half)

    def p_first():
        for to in (seq_at(z, 1 - xl, core), seq_at(up, xl, core), seq_at(down, xl, core), sibling):
            p_to(s, to, pb)

    def p_second():
        block = seq_at(z, 1 - xl, core)
        p_wait(block)
        for to in (seq_at(up, xl, core), seq_at(down, xl, core), sibling):
            p_to(block, to)
        p_wait(seq_at(down, xl, core))
        p_wait(seq_at(up, xl, core))
        p_to(seq_at(down, xl, core), seq_at(up, xl, core))
        p_to(seq_at(down, xl, core), sibling)
        p_to(seq_at(up, xl, core), sibling)

    def p_third():
        p_wait(seq_at(down, 1 - xl, core))
        p_wait(seq_at(up, 1 - xl, core))
        p_to(seq_at(down, 1 - xl, core), seq_at(up, xl, core))
        p_to(seq_at(down, 1 - xl, core), sibling)
        p_to(seq_at(up, 1 - xl, core), sibling)
        p_wait(seq_at(far, xl, core))
        p_to(seq_at(far, xl, core), sibling)

    def p_last():
        p_wait(seq_at(far, 1 - xl, core))
        p_to(seq_at(far, 1 - xl, core), sibling)
        for zz in range(4):
            for xx in range(2):
                p_wait(seq_at(zz, xx, 1 - core))

    for one in w_loads:
        one.wait()
    w_first(0)

    first, second = ends[0], ends[1]
    base = s * 512
    l_hid.wait()

    def norm_first(p, _):
        at = pl.ds(pl.multiple_of(p * 64, 64), 64)
        value = hid[p].astype(F32)
        factor = lax.rsqrt(jnp.sum(value * value, axis=-1, keepdims=True) / 2560.0 + EPSILON)
        rows_in[at, pl.ds(0, 2560)] = (value * factor * norm_gain[...]).astype(BF16)
        return 0

    lax.fori_loop(0, 8, norm_first, 0)
    tokens = rows_in.at[:, pl.ds(0, 2560)]
    l_sw.wait()
    both = jnp.dot(tokens[...], sw[...], preferred_element_type=F32)
    bc = silu(both[:, :128])
    bc_rows[...] = bc.astype(BF16)
    bc_cols[...] = bc.T.astype(BF16)
    logits = both[:, 128:] + small[0:1, :128]
    steps = jnp.maximum(logits, 0.0) + jnp.log1p(jnp.exp(-jnp.abs(logits)))
    rate = -jnp.exp(small[1:2, :128])
    lower = (lax.broadcasted_iota(jnp.int32, (512, 512), 0)
             >= lax.broadcasted_iota(jnp.int32, (512, 512), 1)).astype(F32)
    running = jnp.dot(lower, steps * rate, preferred_element_type=F32, precision=lax.Precision.HIGHEST)
    spread = (lax.broadcasted_iota(jnp.int32, (128, 640), 1) // 64
              == lax.broadcasted_iota(jnp.int32, (128, 640), 0)).astype(F32)
    run_rows[...] = running
    run_cols[...] = running.T
    wide_steps = jnp.dot(steps, spread, preferred_element_type=F32, precision=lax.Precision.HIGHEST)
    run_e[...] = jnp.dot(running, spread, preferred_element_type=F32, precision=lax.Precision.HIGHEST)
    step_e[...] = wide_steps
    l_iw.wait()

    def input_tile(n, width):
        at = pl.ds(n, width)
        xs[:, at] = silu(jnp.dot(tokens[...], iw[:, at], preferred_element_type=F32))
        step_e[:, at] = xs[:, at] * step_e[:, at]

    input_tile(0, 256)
    input_tile(256, 256)
    input_tile(512, 128)

    states[0] = jnp.zeros((64, 640), F32)
    total = None
    for k in range(4):
        rows = slice(k * 128, k * 128 + 128)
        end = run_e[k * 128 + 127:k * 128 + 128, :]
        begin_end = start_of(base + k * 128 + 127, first, second)
        place = base + k * 128 + lax.broadcasted_iota(jnp.int32, (128, 1), 0)
        keep = jnp.where(place >= begin_end, jnp.exp(end - run_e[rows, :]), 0.0)
        own = jnp.dot(bc_cols[:64, rows], (step_e[rows, :] * keep).astype(BF16), preferred_element_type=F32)
        gap = end if k == 0 else end - run_e[k * 128 - 1:k * 128, :]
        through = jnp.where(base + k * 128 - 1 >= begin_end, jnp.exp(gap), 0.0)
        if k == 0:
            total = through
            states[1] = own
        else:
            total = total * through
            if k < 3:
                states[k + 1] = through * states[k] + own
            else:
                tx[0, 0:64, :] = through * states[k] + own
    tx[0, 64:72, :] = jnp.broadcast_to(total, (8, 640))

    def state_to(src, dst, i, to):
        one = copy_to(src, dst, st_send.at[i], st_recv.at[i], (to, c))
        one.start()
        waits.append(one)
        return one

    one = state_to(tx.at[0], rx.at[0], 0, sibling)
    one.wait_recv()
    mine_s, mine_t = tx[0, 0:64, :], tx[0, 64:65, :]
    its_s, its_t = rx[0, 0:64, :], rx[0, 64:65, :]
    s0, t0 = jnp.where(core == 0, mine_s, its_s), jnp.where(core == 0, mine_t, its_t)
    s1, t1 = jnp.where(core == 0, its_s, mine_s), jnp.where(core == 0, its_t, mine_t)
    tx[1, 0:64, :] = t1 * s0 + s1
    tx[1, 64:72, :] = jnp.broadcast_to(t0 * t1, (8, 640))
    one = state_to(tx.at[1], rx.at[1], 1, seq_at(z, 1 - xl, core))

    def chunk(k, _):
        at = pl.ds(pl.multiple_of(k * 128, 128), 128)
        place = base + k * 128 + lax.broadcasted_iota(jnp.int32, (128, 1), 0)
        key = base + k * 128 + lax.broadcasted_iota(jnp.int32, (1, 128), 1)
        begin = start_of(place, first, second)
        allowed = (key >= begin) & (key <= place)
        cross = jnp.dot(bc_rows[at, 64:128], bc_cols[0:64, at], preferred_element_type=F32)
        cross = jnp.where(allowed, cross, 0.0)
        lane = lax.broadcasted_iota(jnp.int32, (128, 128), 1)
        for pair in range(5):
            lanes = pl.ds(pair * 128, 128)
            scaled = step_e[at, lanes].astype(BF16)
            halves = []
            for h in (2 * pair, 2 * pair + 1):
                gap = run_rows[at, h:h + 1] - run_cols[h:h + 1, at]
                decay = jnp.exp(jnp.where(allowed, gap, -1e30))
                halves.append(jnp.dot((decay * cross).astype(BF16), scaled, preferred_element_type=F32))
            ys[at, lanes] = jnp.where(lane < 64, halves[0], halves[1])
        return 0

    lax.fori_loop(0, 2, chunk, 0)
    one.wait_recv()
    mine_s, mine_t = tx[1, 0:64, :], tx[1, 64:65, :]
    its_s, its_t = rx[1, 0:64, :], rx[1, 64:65, :]
    q0, u0 = jnp.where(xl == 0, mine_s, its_s), jnp.where(xl == 0, mine_t, its_t)
    q1, u1 = jnp.where(xl == 0, its_s, mine_s), jnp.where(xl == 0, its_t, mine_t)
    planes[z, 0:64, :] = u1 * q0 + q1
    planes[z, 64:72, :] = jnp.broadcast_to(u0 * u1, (8, 640))
    for d in (2, 1, 3):
        to = lax.rem(z + d, 4)
        one = copy_to(planes.at[z], planes.at[z], st_send.at[1 + d], st_recv.at[2 + z], (seq_at(to, xl, core), c))
        one.start()
        waits.append(one)
    w_first(1)
    l_pb.wait()
    own_p = pltpu.make_async_copy(pb, p_rows(s), local_sem.at[3])
    own_p.start()
    lax.fori_loop(2, 4, chunk, 0)

    for k in range(1, 4):
        rows = slice(k * 128, k * 128 + 128)
        place = base + k * 128 + lax.broadcasted_iota(jnp.int32, (128, 1), 0)
        begin = start_of(place, first, second)
        enter = jnp.where(base + k * 128 - 1 >= begin,
                          jnp.exp(run_e[rows, :] - run_e[k * 128 - 1:k * 128, :]), 0.0)
        ys[rows, :] += enter * jnp.dot(bc_rows[rows, 64:128], states[k].astype(BF16), preferred_element_type=F32)

    l_gw.wait()
    for n, width in ((0, 256), (256, 256), (512, 128)):
        at = pl.ds(n, width)
        step_e[:, at] = silu(jnp.dot(tokens[...], gw[:, at], preferred_element_type=F32))

    enter_s = jnp.zeros((64, 640), F32)
    for d in (1, 2, 3):
        zz = lax.rem(z + d, 4)
        copy_to(planes.at[zz], planes.at[zz], st_send.at[0], st_recv.at[2 + zz], (seq_at(zz, xl, core), c)).wait_recv()
    for zz in range(3):
        enter_s = jnp.where(zz < z, planes[zz, 64:65, :] * enter_s + planes[zz, 0:64, :], enter_s)
    first_s = jnp.where(xl == 0, tx[1, 0:64, :], rx[1, 0:64, :])
    first_t = jnp.where(xl == 0, tx[1, 64:65, :], rx[1, 64:65, :])
    enter_s = jnp.where(xl == 1, first_t * enter_s + first_s, enter_s)
    first_s = jnp.where(core == 0, tx[0, 0:64, :], rx[0, 0:64, :])
    first_t = jnp.where(core == 0, tx[0, 64:65, :], rx[0, 64:65, :])
    enter_s = jnp.where(core == 1, first_t * enter_s + first_s, enter_s)
    states[0] = enter_s

    def gating(k, _):
        at = pl.ds(pl.multiple_of(k * 128, 128), 128)
        place = base + k * 128 + lax.broadcasted_iota(jnp.int32, (128, 1), 0)
        begin = start_of(place, first, second)
        enter = jnp.where(base - 1 >= begin, jnp.exp(run_e[at, :]), 0.0)
        y = ys[at, :] + enter * jnp.dot(bc_rows[at, 64:128], states[0].astype(BF16), preferred_element_type=F32)
        y = y + xs[at, :] * small[2:3, :]
        gated = y * step_e[at, :]
        sq_cols[at, :] = jnp.broadcast_to(jnp.sum(gated * gated, axis=-1, keepdims=True), (128, 128))
        weighted[at, :] = (gated * small[3:4, :]).astype(BF16)
        return 0

    lax.fori_loop(0, 4, gating, 0)
    sq_all[c] = sq_cols[...].T[0:1, :]
    l_ow.wait()

    def columns(n, _):
        at = pl.ds(pl.multiple_of(n * 256, 256), 256)
        tile = jnp.dot(weighted[...], ow[:, at], preferred_element_type=F32)
        part[:, :, at] = tile.astype(BF16).reshape(8, 64, 256)
        return 0

    lax.fori_loop(0, 10, columns, 0)
    copies = []
    for i, p in enumerate(peers):
        few = copy_to(sq_all.at[c], sq_all.at[c], sq_send.at[i], sq_recv.at[c], (s, p))
        few.start()
        waits.append(few)
        big = copy_to(part.at[p], recv.at[i], rs_send.at[i], rs_recv.at[i], (s, p))
        big.start()
        copies.append(big)
    w_second()
    p_first()
    for i, p in enumerate(sources):
        copy_to(sq_all.at[p], sq_all.at[p], sq_send.at[0], sq_recv.at[p], (s, p)).wait_recv()
    for one in copies:
        one.wait_recv()
    own64 = pl.ds(pl.multiple_of(c * 64, 64), 64)
    squares = sq_all[0]
    for i in range(1, 8):
        squares = squares + sq_all[i]
    sq_cols[...] = jnp.broadcast_to(squares, (128, 512)).T
    factor = lax.rsqrt(sq_cols[own64, 0:1] / 5120.0 + EPSILON)

    def gather_sum(n, _):
        at = pl.ds(pl.multiple_of(n * 256, 256), 256)
        value = part[c, :, at].astype(F32)
        for i in range(7):
            value = value + recv[i, :, at].astype(F32)
        mixed[c, :, at] = (hid[c, :, at].astype(F32) + value * factor).astype(BF16)
        return 0

    lax.fori_loop(0, 10, gather_sum, 0)
    for i, p in enumerate(peers):
        one = copy_to(mixed.at[c], mixed.at[c], ag_send.at[i], ag_recv.at[c], (s, p))
        one.start()
        waits.append(one)
    for one in copies:
        one.wait_send()
    l_emb = load(9, embedding, part)
    w_third()
    p_second()
    l_emb.wait()
    for p in sources:
        copy_to(mixed.at[p], mixed.at[p], ag_send.at[0], ag_recv.at[p], (s, p)).wait_recv()

    def norm_second(p, _):
        at = pl.ds(pl.multiple_of(p * 64, 64), 64)
        top = mixed[p].astype(F32)
        low = part[p].astype(F32)
        mean = (jnp.sum(top * top, axis=-1, keepdims=True)
                + jnp.sum(low * low, axis=-1, keepdims=True)) / 5120.0
        scale = lax.rsqrt(mean + EPSILON)
        rows_in[at, pl.ds(0, 2560)] = (top * scale * attn_gain[:, pl.ds(0, 2560)]).astype(BF16)
        rows_in[at, pl.ds(2560, 2560)] = (low * scale * attn_gain[:, pl.ds(2560, 2560)]).astype(BF16)
        return 0

    lax.fori_loop(0, 8, norm_second, 0)
    w_last()

    def project_tile(n, _):
        at = pl.ds(pl.multiple_of(n * 256, 256), 256)
        value = jnp.dot(rows_in[...], w[:, at], preferred_element_type=F32)
        flat_t[at, :] = value.T.astype(BF16)
        return 0

    def first_stage(base, out, recv, lane):
        mine = pltpu.make_async_copy(
            flat_t.at[pl.ds(pl.multiple_of(base + z * 160, 32), 160), :], out.at[s], local_sem.at[lane])
        mine.start()
        for d in (2, 1, 3):
            to = lax.rem(z + d, 4)
            one = copy_to(
                flat_t.at[pl.ds(pl.multiple_of(base + to * 160, 32), 160), :], out.at[s],
                z_send.at[lane, d - 1], recv.at[s], (seq_at(to, xl, core), c))
            one.start()
            waits.append(one)
        return mine

    def pass_on(out, recv, lane, d, own):
        block = seq_at(lax.rem(z + 4 - d, 4), xl, core)
        if own is None:
            copy_to(out.at[block], out.at[block], z_send.at[lane, 0], recv.at[block], (block, c)).wait_recv()
        else:
            own.wait()
        across = copy_to(out.at[block], out.at[block], x_send.at[lane, d], recv.at[block],
                         (seq_at(z, 1 - xl, core), c))
        across.start()
        beside = copy_to(out.at[block], out.at[block], d_send.at[lane, d], recv.at[block],
                         (seq_at(z, xl, 1 - core), c))
        beside.start()
        waits.append(across)
        waits.append(beside)

    def relay(out, recv, lane, d):
        block = seq_at(lax.rem(z + 4 - d, 4), 1 - xl, core)
        copy_to(out.at[block], out.at[block], z_send.at[lane, 0], recv.at[block],
                (seq_at(z, 1 - xl, core), c)).wait_recv()
        beside = copy_to(out.at[block], out.at[block], f_send.at[lane, d], recv.at[block],
                         (seq_at(z, xl, 1 - core), c))
        beside.start()
        waits.append(beside)

    def settle(out, recv, d, side):
        block = seq_at(lax.rem(z + 4 - d, 4), side, 1 - core)
        copy_to(out.at[block], out.at[block], z_send.at[0, 0], recv.at[block],
                (seq_at(z, xl, 1 - core), c)).wait_recv()

    lax.fori_loop(0, 3, project_tile, 0)
    own_k = first_stage(0, k_out, k_recv, 0)
    pass_on(k_out, k_recv, 0, 0, own_k)
    lax.fori_loop(3, 5, project_tile, 0)
    own_v = first_stage(640, v_out, v_recv, 1)
    pass_on(v_out, v_recv, 1, 0, own_v)
    lax.fori_loop(5, 7, project_tile, 0)
    last = pl.ds(1792, 128)
    flat_t[last, :] = jnp.dot(rows_in[...], w[:, last], preferred_element_type=F32).T.astype(BF16)
    quarter = xl * 2 + core
    for d in range(16):
        to = lax.rem(s + d, 16)
        piece = flat_t.at[pl.ds(pl.multiple_of(1280 + (to // 4) * 160, 32), 160),
                        pl.ds(pl.multiple_of(lax.rem(to, 4) * 128, 128), 128)]
        if d == 0:
            own_q = pltpu.make_async_copy(piece, q_out.at[s], local_sem.at[2])
            own_q.start()
        else:
            one = copy_to(piece, q_out.at[s], q_send.at[d - 1], q_recv.at[s], (to, c))
            one.start()
            waits.append(one)
    for d in (1, 3, 2):
        pass_on(k_out, k_recv, 0, d, None)
    relay(k_out, k_recv, 0, 0)
    for d in (1, 3, 2):
        pass_on(v_out, v_recv, 1, d, None)
    relay(v_out, v_recv, 1, 0)
    for d in (1, 3, 2):
        relay(k_out, k_recv, 0, d)
    for d in (1, 3, 2):
        relay(v_out, v_recv, 1, d)
    for d in (0, 1, 3, 2):
        for side in (0, 1):
            settle(k_out, k_recv, d, side)
            settle(v_out, v_recv, d, side)
    own_q.wait()
    own_p.wait()
    p_third()
    p_last()
    for d in range(1, 16):
        block = lax.rem(s + d, 16)
        copy_to(q_out.at[block], q_out.at[block], q_send.at[0], q_recv.at[block], (block, c)).wait_recv()
    for one in waits:
        one.wait_send()


def front(ends, hidden, norm_gain, input_w, gate_w, state_w, small, out_w, embedding, attn_gain, wk, wv, wq, p_in):
    dma = pltpu.SemaphoreType.DMA
    vm, anyw = pl.BlockSpec(memory_space=VMEM), pl.BlockSpec(memory_space=pl.ANY)
    return pl.pallas_call(
        front_kernel,
        out_shape=(
            jax.ShapeDtypeStruct((8, 64, 2560), BF16),
            jax.ShapeDtypeStruct((16, 160, 512), BF16),
            jax.ShapeDtypeStruct((16, 160, 512), BF16),
            jax.ShapeDtypeStruct((16, 160, 128), BF16),
            jax.ShapeDtypeStruct((2560, 640), BF16),
        ),
        in_specs=[pl.BlockSpec(memory_space=pltpu.SMEM), anyw, vm, anyw, anyw, anyw, vm, anyw, anyw, vm,
                  anyw, anyw, anyw, anyw],
        out_specs=(vm, anyw, anyw, vm, anyw),
        scratch_shapes=[
            VMEM((8, 64, 2560), BF16),
            VMEM((2560, 640), BF16),
            VMEM((2560, 640), BF16),
            VMEM((2560, 256), BF16),
            VMEM((640, 2560), BF16),
            VMEM((5120, 1920), BF16),
            VMEM((512, 5120), BF16),
            VMEM((8, 64, 2560), BF16),
            VMEM((7, 64, 2560), BF16),
            VMEM((1920, 512), BF16),
            VMEM((512, 640), F32),
            VMEM((512, 640), F32),
            VMEM((512, 640), F32),
            VMEM((4, 64, 640), F32),
            VMEM((2, 72, 640), F32),
            VMEM((2, 72, 640), F32),
            VMEM((4, 72, 640), F32),
            VMEM((512, 128), F32),
            VMEM((128, 512), F32),
            VMEM((512, 640), F32),
            VMEM((512, 128), BF16),
            VMEM((128, 512), BF16),
            VMEM((160, 640), BF16),
            VMEM((8, 1, 512), F32),
            VMEM((512, 128), F32),
            VMEM((512, 640), BF16),
            dma((10,)),
            dma((30,)),
            dma((16, 2)),
            dma((15,)),
            dma((16,)),
            dma((5,)),
            dma((6,)),
            dma((7,)),
            dma((8,)),
            dma((7,)),
            dma((7,)),
            dma((7,)),
            dma((8,)),
            dma((2, 3)),
            dma((2, 4)),
            dma((2, 4)),
            dma((2, 4)),
            dma((16,)),
            dma((16,)),
            dma((15,)),
            dma((16,)),
            dma((4,)),
        ],
        compiler_params=pltpu.CompilerParams(
            collective_id=0, has_side_effects=True, vmem_limit_bytes=67043328
        ),
        name="front",
    )(ends, hidden, norm_gain, input_w, gate_w, state_w, small, out_w, embedding, attn_gain, wk, wv, wq, p_in)


def attend_kernel(ends, q_in, k_in, v_in, out):
    quarter = lax.rem(lax.axis_index("seq"), 4)
    i = pl.program_id(0)
    first, second = ends[0], ends[1]
    queries = jnp.concatenate(
        [q_in[2 * i].astype(F32).T, q_in[2 * i + 1].astype(F32).T], axis=0
    ).astype(BF16)
    row = lax.broadcasted_iota(jnp.int32, (256, 1), 0)
    place = i * 1024 + quarter * 128 + row + jnp.where(row >= 128, 384, 0)

    def start_of(p):
        return jnp.where(p >= second, second, jnp.where(p >= first, first, 0))

    begin = start_of(place)
    low_place = i * 1024 + quarter * 128
    top_begin = start_of(low_place + 512 + 127)
    low_begin = start_of(low_place)
    lowest = low_begin // 512
    scale = (AP ** -0.5) * 1.4426950408889634

    def step(b, carry, masked):
        top, total, acc = carry
        scores = jnp.dot(queries, k_in[b], preferred_element_type=F32)
        if masked:
            key = b * 512 + lax.broadcasted_iota(jnp.int32, (256, 512), 1)
            visible = (key >= begin) & (key <= place)
            scores = jnp.where(visible, scores, -1e30)
        new_top = jnp.maximum(top, jnp.max(scores, axis=-1, keepdims=True))
        weights = jnp.exp2((scores - new_top) * scale)
        if masked:
            weights = jnp.where(visible, weights, 0.0)
        keep = jnp.exp2((top - new_top) * scale)
        total = total * keep + jnp.sum(weights, axis=-1, keepdims=True)
        acc = acc * keep + lax.dot_general(
            weights.astype(BF16), v_in[b], (((1,), (1,)), ((), ())), preferred_element_type=F32
        )
        return new_top, total, acc

    carry = (jnp.full((256, 1), -1e30, F32), jnp.zeros((256, 1), F32), jnp.zeros((256, AP), F32))
    plain_from = jnp.minimum((top_begin + 511) // 512, 2 * i)
    carry = lax.fori_loop(lowest, plain_from, lambda b, t: step(b, t, True), carry)
    carry = lax.fori_loop(jnp.maximum(lowest, plain_from), 2 * i, lambda b, t: step(b, t, False), carry)
    carry = lax.fori_loop(jnp.maximum(lowest, 2 * i), 2 * i + 2, lambda b, t: step(b, t, True), carry)
    top, total, acc = carry
    context = (acc / total).T.astype(BF16)
    out[0] = context[:, :128]
    out[1] = context[:, 128:]


def attend(ends, q_in, k_in, v_in):
    vm = pl.BlockSpec(memory_space=VMEM)
    return pl.pallas_call(
        attend_kernel,
        out_shape=jax.ShapeDtypeStruct((16, 160, 128), BF16),
        grid=(8,),
        in_specs=[pl.BlockSpec(memory_space=pltpu.SMEM), vm, vm, vm],
        out_specs=pl.BlockSpec((2, 160, 128), lambda i: (i, 0, 0)),
        compiler_params=pltpu.CompilerParams(vmem_limit_bytes=40 * 1024 * 1024),
        cost_estimate=pl.CostEstimate(flops=10_000_000_000, bytes_accessed=6_000_000, transcendentals=0),
        name="attend",
    )(ends, q_in, k_in, v_in)


def finish_kernel(ctx, proj_t, out, gathered, part, recv, in_send, in_recv, send_sem, recv_sem, local_sem):
    s, c = lax.axis_index("seq"), lax.axis_index("chan")
    peers, sources = chan_peers(s, c), chan_sources(s, c)
    greet([(s, p) for p in peers] + [(lax.rem(s + d, 16), c) for d in range(1, 16)])
    z = s // 4
    lanes = pl.ds(pl.multiple_of(lax.rem(s, 4) * 128, 128), 128)
    waits = []
    for d in range(16):
        to = lax.rem(s + d, 16)
        where = gathered.at[pl.ds(pl.multiple_of(z * 160, 32), 160), lanes]
        if d == 0:
            own = pltpu.make_async_copy(ctx.at[s], where, local_sem.at[0])
            own.start()
        else:
            one = copy_to(ctx.at[to], where, in_send.at[d - 1], in_recv.at[s], (to, c))
            one.start()
            waits.append(one)
    own.wait()
    for d in range(1, 16):
        block = lax.rem(s + d, 16)
        where = gathered.at[pl.ds(pl.multiple_of((block // 4) * 160, 32), 160),
                            pl.ds(pl.multiple_of(lax.rem(block, 4) * 128, 128), 128)]
        copy_to(ctx.at[0], where, in_send.at[0], in_recv.at[block], (block, c)).wait_recv()
    copies = []
    for i, p in enumerate(peers):
        at = pl.ds(pl.multiple_of(p * 320, 32), 320)
        part[p] = jnp.dot(proj_t[at, :], gathered[...], preferred_element_type=F32).astype(BF16)
        one = copy_to(part.at[p], recv.at[i], send_sem.at[i], recv_sem.at[i], (s, p))
        one.start()
        copies.append(one)
    at = pl.ds(pl.multiple_of(c * 320, 32), 320)
    value = jnp.dot(proj_t[at, :], gathered[...], preferred_element_type=F32)
    for i in (6, 5, 4, 3, 2, 1, 0):
        copies[i].wait_recv()
        value = value + recv[i].astype(F32)
    out[...] = value.T
    for one in waits + copies:
        one.wait_send()


def finish(ctx, proj_t):
    dma = pltpu.SemaphoreType.DMA
    vm = pl.BlockSpec(memory_space=VMEM)
    return pl.pallas_call(
        finish_kernel,
        out_shape=jax.ShapeDtypeStruct((512, 320), F32),
        in_specs=[vm, vm],
        out_specs=vm,
        scratch_shapes=[
            VMEM((640, 512), BF16),
            VMEM((8, 320, 512), BF16),
            VMEM((7, 320, 512), BF16),
            dma((15,)),
            dma((16,)),
            dma((7,)),
            dma((7,)),
            dma((1,)),
        ],
        compiler_params=pltpu.CompilerParams(
            collective_id=2, has_side_effects=True, vmem_limit_bytes=40 * 1024 * 1024
        ),
        cost_estimate=pl.CostEstimate(flops=50_000_000_000, bytes_accessed=6_000_000, transcendentals=0),
        name="finish",
    )(ctx, proj_t)


def local(
    hidden,
    embedding,
    segments,
    input_norm_gain,
    gate_proj,
    input_proj,
    state_proj,
    step_proj,
    step_bias,
    decay_log,
    skip_gain,
    out_gain,
    out_proj,
    attn_gain,
    query_proj,
    key_proj,
    value_proj,
    attn_out,
):
    chan_index = lax.axis_index("chan")
    ends = jnp.stack([jnp.sum((segments < 1).astype(jnp.int32)), jnp.sum((segments < 2).astype(jnp.int32))])
    state_w = jnp.concatenate([state_proj, jnp.pad(step_proj, ((0, 0), (0, 118)))], axis=1)
    small = jnp.stack([
        jnp.pad(step_bias, (0, 630)), jnp.pad(decay_log, (0, 630)),
        jnp.repeat(skip_gain, HEAD_CHANNELS), out_gain,
    ])
    mixed, k_all, v_all, q_all, proj_t = front(
        ends, hidden.reshape(8, 64, 2560), input_norm_gain[None, :], input_proj, gate_proj, state_w, small,
        out_proj, embedding.reshape(8, 64, 2560), attn_gain[None, :], key_proj, value_proj, query_proj,
        attn_out.T,
    )
    ctx = attend(ends, q_all, k_all, v_all)
    out_share = finish(ctx, proj_t)
    own_mixed = lax.dynamic_slice_in_dim(mixed.reshape(512, 2560), chan_index * 320, 320, 1)
    return (out_share + own_mixed.astype(jnp.float32)).astype(jnp.bfloat16)


def solution(mesh):
    in_specs = (
        P("seq", None),
        P("seq", None),
        P(),
        P(),
        P(None, "chan"),
        P(None, "chan"),
        P(),
        P(None, "chan"),
        P("chan"),
        P("chan"),
        P("chan"),
        P("chan"),
        P("chan", None),
        P(),
        P("seq", "chan"),
        P("seq", "chan"),
        P("seq", "chan"),
        P("chan", "seq"),
    )
    out_specs = P("seq", "chan")
    return jax.shard_map(local, mesh=mesh, in_specs=in_specs, out_specs=out_specs, check_vma=False)
```

time: 418 us -> 260 us (0.62)
  waiting for transfers between devices: 87.6 us -> 0 us
  matrix products: 21.5 us -> 0 us
  Pallas kernels: 259 us -> 243 us
  between operations: 14.8 us -> 0.12 us
  local copies, waits for them, and re-layouts: 20.9 us -> 8.1 us
  other arithmetic: 13.1 us -> 7.7 us
    all_gather x5 -> x0, waiting for transfers between devices: 85.2 us -> none  [the longest x3 49 us: local(): lax.all_gather(w, 'seq', axis=0, tiled=True)]
    dot_general x7 -> x0, matrix products: 21.2 us -> none  [the longest x1 5.78 us: local(): jnp.dot(tokens_n, input_proj, preferred_element_type=jnp.float32)]
    pallas_call x2 -> x1, Pallas kernels: 181 us -> 168 us  [front(): pl.pallas_call(front_kernel, out_shape=(jax.ShapeDtypeStruct((8, 64, 2560...]
    reduce_sum x2 -> x0, other arithmetic: 5.54 us -> none  [the longest x1 3.22 us: local(): state_in = jnp.sum(all_states * factors[:, :, None, None], axis=0)]
    unnamed x42 -> x21, local copies, waits for them, and re-layouts: 10.1 us -> 6.42 us
  transfers between devices with their start and end apart: 5 -> 0, of which waited for: 3 -> 0; matrix products, arithmetic and copies ran while one was open for 5% -> 0% of each run, Pallas kernels for 51% -> 0%
where the time goes in v2:
time: 260 us; the launch traced here: 259 us
  Pallas kernels  243 us (93%)
  local copies, waits for them, and re-layouts  8.1 us (3%)
  other arithmetic  7.7 us (3%)
    pallas_call x1, Pallas kernels, front(): pl.pallas_call(front_kernel, out_shape=(jax.ShapeDtypeStruct((8, 64, 2560...  168 us
    pallas_call x1, Pallas kernels, finish(): pl.pallas_call(finish_kernel, out_shape=jax.ShapeDtypeStruct((512, 320),...  47.4 us
    pallas_call x1, Pallas kernels, attend(): pl.pallas_call(attend_kernel, out_shape=jax.ShapeDtypeStruct((16, 160, 12...  27.6 us
    unnamed x21, local copies, waits for them, and re-layouts  6.42 us

profile of v2, /device:TPU:1, one launch (start us, length us, event | category | flops | bytes accessed | tf_op | source)
XLA Modules:
  0.0 259.0 jit_solution(8622165237385608607)
XLA Ops:
  0.0 0.0 copy-start.7
  0.0 0.0 copy-start.8
  0.0 0.0 copy-start.6
  0.0 0.0 copy-start.5
  0.0 1.5 convert_reduce_fusion.1
  1.6 1.9 pad_add_fusion.ends
  3.5 1.2 copy.19
  4.7 2.4 fusion.1.state_w
  7.1 0.0 copy-done.7
  7.1 0.1 broadcast_in_dim.10
  7.2 0.1 stack_reshape.3
  7.3 0.0 copy-done.8
  7.3 0.0 copy-done.9
  7.3 0.0 copy-done.6
  7.3 0.6 pad_maximum_fusion.small
  7.9 0.0 copy-done.5
  7.9 0.6 broadcast_in_dim.9.norm_gain
  8.6 168.2 %front.1 = (bf16[8,64,2560]{2,1,0:T(8,128)(2,1)}, bf16[16,160,512]{2,1,0:T(8,128)(2,1)}, bf16[16,160,512]{2,1,0:T(8,128)(2,1)}, bf16[16,160,128]{2,1,0:T(8,128)(2,1)}, bf16[2560,640]{1,0:T(8,128)(2,1)}) custom-call(s32[2]{0:T(128)} %pad_add_fusion.ends, bf16[8,64,2560]{2,1,0:T(8,128)(2,1)} %bitcast.7, f32[1,2560]{1,0:T(1,128)} %broadcast_in_dim.9.norm_gain, ...), custom_call_target="tpu_custom_call" | custom-call | tf_op jit(solution)/shard_map/front/pallas_call | solution.py:525
  176.7 0.0 copy-start
  176.7 0.6 copy-done
  177.3 0.0 copy-start.2
  177.3 1.7 copy-done.2
  179.0 0.0 copy-start.3
  179.1 1.7 copy-done.3
  180.8 0.0 copy-start.4
  180.8 1.1 copy-done.4
  181.9 0.0 copy-start.1
  181.9 27.6 %attend.1.ctx = bf16[16,160,128]{2,1,0:T(8,128)(2,1)S(1)} custom-call(s32[2]{0:T(128)S(1)} %copy-done, bf16[16,160,128]{2,1,0:T(8,128)(2,1)S(1)} %copy-done.4, bf16[16,160,512]{2,1,0:T(8,128)(2,1)S(1)} %copy-done.2, bf16[16,160,512]{2,1,0:T(8,128)(2,1)S(1)} %copy-done.3), custom_call_target="tpu_custom_call" | custom-call | flops 10000000000 | bytes 6000000 | tf_op jit(solution)/shard_map/attend/pallas_call | solution.py:645
  209.5 0.0 copy-done.1
  209.5 47.4 %finish.1 = f32[512,320]{1,0:T(8,128)S(1)} custom-call(bf16[16,160,128]{2,1,0:T(8,128)(2,1)S(1)} %attend.1.ctx, bf16[2560,640]{1,0:T(8,128)(2,1)S(1)} %copy-done.1), custom_call_target="tpu_custom_call" | custom-call | flops 49999998976 | bytes 6000000 | tf_op jit(solution)/shard_map/finish/pallas_call | solution.py:700
  256.9 1.3 add_convert_fusion
  258.1 0.9 copy.20
  (6 shorter events, 0.0 us)
Async XLA Ops:
  0.0 7.1 %copy-start.7 = (f32[10]{0:T(128)S(1)}, f32[10]{0:T(128)}, u32[]{:S(2)}) copy-start(f32[10]{0:T(128)} %param.28) | copy-start | bytes 124
  0.0 7.3 %copy-start.8 = (f32[10]{0:T(128)S(1)}, f32[10]{0:T(128)}, u32[]{:S(2)}) copy-start(f32[10]{0:T(128)} %param.26) | copy-start | bytes 124
  0.0 7.3 %copy-start.9 = (f32[10]{0:T(128)S(1)}, f32[10]{0:T(128)}, u32[]{:S(2)}) copy-start(f32[10]{0:T(128)} %param.27) | copy-start | bytes 124
  0.0 7.3 %copy-start.6 = (f32[640]{0:T(1024)S(1)}, f32[640]{0:T(1024)}, u32[]{:S(2)}) copy-start(f32[640]{0:T(1024)} %param.29) | copy-start | bytes 7684
  0.0 7.9 %copy-start.5 = (f32[2560]{0:T(1024)S(1)}, f32[2560]{0:T(1024)}, u32[]{:S(2)}) copy-start(f32[2560]{0:T(1024)} %param.21) | copy-start | bytes 30724
  176.7 0.6 copy-start
  177.3 1.7 copy-start.2
  179.0 1.7 copy-start.3
  180.8 1.1 copy-start.4
  181.9 27.6 %copy-start.1 = (bf16[2560,640]{1,0:T(8,128)(2,1)S(1)}, bf16[2560,640]{1,0:T(8,128)(2,1)}, u32[]{:S(2)}) copy-start(bf16[2560,640]{1,0:T(8,128)(2,1)} %get-tuple-element.13.proj_t) | copy-start | bytes 9830404

commit v3 on v2

v3 whole, which is shorter than its diff:
```python
import jax
import jax.numpy as jnp
from jax import lax
from jax.experimental import pallas as pl
from jax.experimental.pallas import tpu as pltpu
from jax.sharding import PartitionSpec as P

N = 64
HEAD_CHANNELS = 64
AP = 160
EPSILON = 1e-05
MESH = pl.DeviceIdType.MESH
VMEM = pltpu.VMEM
LIMIT = 62 * 1024 * 1024
F32 = jnp.float32
BF16 = jnp.bfloat16


def greet(peers):
    barrier = pltpu.get_barrier_semaphore()
    for peer in peers:
        pl.semaphore_signal(barrier, inc=1, device_id=peer, device_id_type=MESH)
    pl.semaphore_wait(barrier, len(peers))


def copy_to(src, dst, send, recv, where):
    return pltpu.make_async_remote_copy(
        src_ref=src, dst_ref=dst, send_sem=send, recv_sem=recv,
        device_id=where, device_id_type=MESH,
    )


OFFSETS = ((1, 2), (1, 1), (1, 3), (0, 2), (1, 0), (0, 1), (0, 3))


def chan_peers(s, c):
    half, place = c // 4, lax.rem(c, 4)
    return [lax.rem(half + a, 2) * 4 + lax.rem(place + b, 4) for a, b in OFFSETS]


def chan_sources(s, c):
    half, place = c // 4, lax.rem(c, 4)
    return [lax.rem(half + a, 2) * 4 + lax.rem(place + 4 - b, 4) for a, b in OFFSETS]


def seq_parts(s):
    return s // 4, lax.rem(s // 2, 2), lax.rem(s, 2)


def seq_at(z, xl, core):
    return z * 4 + xl * 2 + core


class ChanSum:
    def __init__(self, s, c, part, ring, fin, comb, across, send_sem, recv_sem):
        self.s, self.part, self.ring, self.fin = s, part, ring, fin
        self.comb, self.across, self.send_sem, self.recv_sem = comb, across, send_sem, recv_sem
        self.rows, self.width = part.shape[1] // 2, part.shape[2]
        self.xh, self.yy = c // 4, lax.rem(c, 4)
        self.up = lax.rem(self.yy + 1, 4)
        self.down = lax.rem(self.yy + 3, 4)
        self.far = lax.rem(self.yy + 2, 4)
        self.sent = []

    def column(self, turn):
        return 1 - self.xh if turn == 0 else self.xh

    def side(self, ref, half):
        return ref.at[pl.ds(half * self.rows, self.rows), :]

    def piece(self, turn, y, half):
        return self.side(self.part.at[self.column(turn) * 4 + y], half)

    def copy(self, i, src, dst, y, turn=1):
        to = self.column(turn) * 4 + y
        return copy_to(src, dst, self.send_sem.at[i], self.recv_sem.at[i], (self.s, to))

    def send(self, i, src, dst, y, turn=1):
        one = self.copy(i, src, dst, y, turn)
        one.start()
        self.sent.append(one)

    def wait(self, i, dst):
        self.copy(i, dst, dst, self.up).wait_recv()

    def first(self, turn):
        i = 6 * turn
        self.send(i, self.piece(turn, self.far, 0), self.ring.at[turn, 0], self.up)
        self.send(i + 2, self.piece(turn, self.far, 1), self.ring.at[turn, 1], self.down)
        self.send(i + 1, self.piece(turn, self.up, 1), self.side(self.fin.at[turn, 0], 1), self.up)
        self.send(i + 3, self.piece(turn, self.down, 0), self.side(self.fin.at[turn, 1], 0), self.down)

    def second(self, turn):
        for way, y in ((0, self.up), (1, self.down)):
            self.wait(6 * turn + 2 * way, self.ring.at[turn, way])
            mine, its, both = self.piece(turn, y, way), self.ring.at[turn, way], self.comb.at[turn, way]

            def add(n, _):
                at = pl.ds(pl.multiple_of(n * 256, 256), 256)
                both[:, at] = (mine[:, at].astype(F32) + its[:, at].astype(F32)).astype(BF16)
                return 0

            lax.fori_loop(0, self.width // 256, add, 0)
            self.send(6 * turn + 4 + way, both, self.side(self.fin.at[turn, way], way), y)

    def arrived(self, turn):
        i = 6 * turn
        for way in (0, 1):
            self.wait(i + 1 + 2 * way, self.side(self.fin.at[turn, way], 1 - way))
            self.wait(i + 4 + way, self.side(self.fin.at[turn, way], way))

    def total(self, turn, at):
        value = self.part[self.column(turn) * 4 + self.yy, :, at].astype(F32)
        return value + self.fin[turn, 0, :, at].astype(F32) + self.fin[turn, 1, :, at].astype(F32)

    def cross(self):
        self.arrived(0)
        own = self.column(0) * 4 + self.yy

        def add(n, _):
            at = pl.ds(pl.multiple_of(n * 256, 256), 256)
            self.part[own, :, at] = self.total(0, at).astype(BF16)
            return 0

        lax.fori_loop(0, self.width // 256, add, 0)
        self.send(12, self.part.at[own], self.across, self.yy, 0)

    def close(self):
        self.arrived(1)
        self.wait(12, self.across)

    def result(self, at):
        return self.total(1, at) + self.across[:, at].astype(F32)


def ring_scratch(rows, width):
    return [
        VMEM((2, 2, rows // 2, width), BF16),
        VMEM((2, 2, rows, width), BF16),
        VMEM((2, 2, rows // 2, width), BF16),
        VMEM((rows, width), BF16),
        pltpu.SemaphoreType.DMA((13,)),
        pltpu.SemaphoreType.DMA((13,)),
    ]


def start_of(place, first, second):
    return jnp.where(place >= second, second, jnp.where(place >= first, first, 0))


def silu(v):
    return v / (1.0 + jnp.exp(-v))


def front_kernel(segments, hidden, norm_gain, input_w, gate_w, state_w, step_w, bias, decay, skip, out_gain,
                 out_w, embedding, attn_gain, wk, wv, wq, p_in,
                 mixed, k_out, v_out, q_out, p_out,
                 hid, iw, gw, sw, dw, ow, ao, vec, w, rows_in, part, flat_t, run_e, xs, ys, states, tx, rx, planes, tx_t, rx_t, planes_t,
                 run_rows, run_cols, step_e, bc_rows, bc_cols, pb, sq_all, sq_cols, weighted,
                 load_sem, w_send, w_recv, p_send, p_recv, st_send, st_recv,
                 sq_send, sq_recv, ring, fin, comb, across, rs_send, rs_recv, ag_send, ag_recv,
                 z_send, x_send, d_send, f_send, k_recv, v_recv, q_send, q_recv, local_sem, own_sem):
    s, c = lax.axis_index("seq"), lax.axis_index("chan")
    z, xl, core = seq_parts(s)
    peers, sources = chan_peers(s, c), chan_sources(s, c)
    up, down, far = lax.rem(z + 1, 4), lax.rem(z + 3, 4), lax.rem(z + 2, 4)
    waits = []

    def load(i, src, dst):
        one = pltpu.make_async_copy(src, dst, load_sem.at[i])
        one.start()
        return one

    own_rows = pl.ds(pl.multiple_of(s * 320, 64), 320)
    w_loads = [load(i, src, w.at[own_rows, pl.ds(i * 640, 640)]) for i, src in enumerate((wk, wv, wq))]
    l_hid = load(3, hidden, hid)
    l_sw = load(4, state_w, sw.at[:, pl.ds(0, 128)])
    l_dw = load(10, step_w, dw)
    l_iw = load(5, input_w, iw)
    l_pb = load(6, p_in, ao)
    l_gw = load(7, gate_w, gw)
    l_ow = load(8, out_w, ow)
    greet([(s, p) for p in peers] + [(lax.rem(s + d, 16), c) for d in range(1, 16)])

    used = [0, 0]
    sibling = seq_at(z, xl, 1 - core)

    def w_rows(block, half, group):
        rows = pl.ds(pl.multiple_of(block * 320 + half * 160, 32), 160)
        return w.at[rows, pl.ds(1280 * group, 1280 - 640 * group)]

    def w_to(block, half, group, to):
        rows = w_rows(block, half, group)
        one = copy_to(rows, rows, w_send.at[used[0]], w_recv.at[block, half, group], (to, c))
        used[0] += 1
        one.start()
        waits.append(one)

    def w_wait(block, half, group):
        rows = w_rows(block, half, group)
        copy_to(rows, rows, w_send.at[0], w_recv.at[block, half, group], (sibling, c)).wait_recv()

    def p_rows(block):
        return p_out.at[pl.ds(pl.multiple_of(block * 160, 32), 160), :]

    def p_to(block, to, src=None):
        rows = p_rows(block)
        one = copy_to(rows if src is None else src, rows, p_send.at[used[1]], p_recv.at[block], (to, c))
        used[1] += 1
        one.start()
        waits.append(one)

    def p_wait(block):
        rows = p_rows(block)
        copy_to(rows, rows, p_send.at[0], p_recv.at[block], (seq_at(z, xl, 1 - core), c)).wait_recv()

    def w_across(half, group):
        w_to(s, half, group, seq_at(z, 1 - xl, core))

    def w_first(half, group):
        w_to(s, half, group, seq_at(up, xl, core))
        w_to(s, half, group, seq_at(down, xl, core))
        w_to(s, half, group, sibling)

    def w_second(half, group):
        block = seq_at(z, 1 - xl, core)
        w_wait(block, half, group)
        w_to(block, half, group, seq_at(up, xl, core))
        w_to(block, half, group, seq_at(down, xl, core))
        w_to(block, half, group, sibling)

    def w_ring(side, group):
        for half in (0, 1):
            w_wait(seq_at(down, side, core), half, group)
            w_wait(seq_at(up, side, core), half, group)
            if half == 0:
                w_to(seq_at(down, side, core), 0, group, seq_at(up, xl, core))
        w_to(seq_at(up, side, core), 1, group, seq_at(down, xl, core))
        for half in (0, 1):
            w_to(seq_at(down, side, core), half, group, sibling)
            w_to(seq_at(up, side, core), half, group, sibling)

    def w_far(side, group):
        for half in (0, 1):
            w_wait(seq_at(far, side, core), half, group)
            w_to(seq_at(far, side, core), half, group, sibling)

    def w_last(group):
        for zz in range(4):
            for xx in range(2):
                for half in (0, 1):
                    w_wait(seq_at(zz, xx, 1 - core), half, group)

    def p_first():
        for to in (seq_at(z, 1 - xl, core), seq_at(up, xl, core), seq_at(down, xl, core), sibling):
            p_to(s, to, pb)

    def p_second():
        block = seq_at(z, 1 - xl, core)
        p_wait(block)
        for to in (seq_at(up, xl, core), seq_at(down, xl, core), sibling):
            p_to(block, to)
        p_wait(seq_at(down, xl, core))
        p_wait(seq_at(up, xl, core))
        p_to(seq_at(down, xl, core), seq_at(up, xl, core))
        p_to(seq_at(down, xl, core), sibling)
        p_to(seq_at(up, xl, core), sibling)

    def p_third():
        p_wait(seq_at(down, 1 - xl, core))
        p_wait(seq_at(up, 1 - xl, core))
        p_to(seq_at(down, 1 - xl, core), seq_at(up, xl, core))
        p_to(seq_at(down, 1 - xl, core), sibling)
        p_to(seq_at(up, 1 - xl, core), sibling)
        p_wait(seq_at(far, xl, core))
        p_to(seq_at(far, xl, core), sibling)

    def p_last():
        p_wait(seq_at(far, 1 - xl, core))
        p_to(seq_at(far, 1 - xl, core), sibling)
        for zz in range(4):
            for xx in range(2):
                p_wait(seq_at(zz, xx, 1 - core))

    for one in w_loads:
        one.wait()
    w_first(0, 0)
    w_first(0, 1)

    first, second = boundary(segments, 1), boundary(segments, 2)
    base = s * 512
    l_hid.wait()

    def norm_first(p, _):
        at = pl.ds(pl.multiple_of(p * 64, 64), 64)
        value = hid[p].astype(F32)
        factor = lax.rsqrt(jnp.sum(value * value, axis=-1, keepdims=True) / 2560.0 + EPSILON)
        rows_in[at, pl.ds(0, 2560)] = (value * factor * norm_gain[...]).astype(BF16)
        return 0

    lax.fori_loop(0, 8, norm_first, 0)
    tokens = rows_in.at[:, pl.ds(0, 2560)]
    sw[:, 128:256] = jnp.zeros((2560, 128), BF16)
    vec[...] = jnp.zeros((8, 128), F32)
    vec[0:1, 0:10] = bias[...]
    vec[1:2, 0:10] = decay[...]
    vec[2:3, 0:10] = skip[...]
    l_sw.wait()
    l_dw.wait()
    sw[:, 128:138] = dw[...]
    both = jnp.dot(tokens[...], sw[...], preferred_element_type=F32)
    bc = silu(both[:, :128])
    bc_rows[...] = bc.astype(BF16)
    bc_cols[...] = bc.T.astype(BF16)
    logits = both[:, 128:] + vec[0:1, :]
    steps = jnp.maximum(logits, 0.0) + jnp.log1p(jnp.exp(-jnp.abs(logits)))
    rate = -jnp.exp(vec[1:2, :])
    lower = (lax.broadcasted_iota(jnp.int32, (512, 512), 0)
             >= lax.broadcasted_iota(jnp.int32, (512, 512), 1)).astype(F32)
    running = jnp.dot(lower, steps * rate, preferred_element_type=F32, precision=lax.Precision.HIGHEST)
    spread = (lax.broadcasted_iota(jnp.int32, (128, 640), 1) // 64
              == lax.broadcasted_iota(jnp.int32, (128, 640), 0)).astype(F32)
    run_rows[...] = running
    run_cols[...] = running.T
    wide_steps = jnp.dot(steps, spread, preferred_element_type=F32, precision=lax.Precision.HIGHEST)
    run_e[...] = jnp.dot(running, spread, preferred_element_type=F32, precision=lax.Precision.HIGHEST)
    step_e[...] = wide_steps
    skip_e = jnp.dot(vec[...], spread, preferred_element_type=F32, precision=lax.Precision.HIGHEST)[2:3, :]
    l_iw.wait()

    def input_tile(n, width):
        at = pl.ds(n, width)
        xs[:, at] = silu(jnp.dot(tokens[...], iw[:, at], preferred_element_type=F32))
        step_e[:, at] = xs[:, at] * step_e[:, at]

    input_tile(0, 256)
    input_tile(256, 256)
    input_tile(512, 128)

    states[0] = jnp.zeros((64, 640), F32)
    total = None
    for k in range(4):
        rows = slice(k * 128, k * 128 + 128)
        end = run_e[k * 128 + 127:k * 128 + 128, :]
        begin_end = start_of(base + k * 128 + 127, first, second)
        place = base + k * 128 + lax.broadcasted_iota(jnp.int32, (128, 1), 0)
        keep = jnp.where(place >= begin_end, jnp.exp(end - run_e[rows, :]), 0.0)
        own = jnp.dot(bc_cols[:64, rows], (step_e[rows, :] * keep).astype(BF16), preferred_element_type=F32)
        gap = end if k == 0 else end - run_e[k * 128 - 1:k * 128, :]
        through = jnp.where(base + k * 128 - 1 >= begin_end, jnp.exp(gap), 0.0)
        if k == 0:
            total = through
            states[1] = own
        else:
            total = total * through
            if k < 3:
                states[k + 1] = through * states[k] + own
            else:
                tx[0] = (through * states[k] + own).astype(BF16)
    tx_t[0] = jnp.broadcast_to(total, (8, 640))

    def state_to(i, to):
        pair = [
            copy_to(tx_t.at[i], rx_t.at[i], st_send.at[2 * i], st_recv.at[2 * i], (to, c)),
            copy_to(tx.at[i], rx.at[i], st_send.at[2 * i + 1], st_recv.at[2 * i + 1], (to, c)),
        ]
        for one in pair:
            one.start()
            waits.append(one)
        return pair

    def joined(i, low):
        mine_s, mine_t = tx[i].astype(F32), tx_t[i, 0:1, :]
        its_s, its_t = rx[i].astype(F32), rx_t[i, 0:1, :]
        first_s, first_t = jnp.where(low, mine_s, its_s), jnp.where(low, mine_t, its_t)
        last_s, last_t = jnp.where(low, its_s, mine_s), jnp.where(low, its_t, mine_t)
        return (last_t * first_s + last_s).astype(BF16), jnp.broadcast_to(first_t * last_t, (8, 640))

    for one in state_to(0, sibling):
        one.wait_recv()
    tx[1], tx_t[1] = joined(0, core == 0)
    pair = state_to(1, seq_at(z, 1 - xl, core))
    for group in (0, 1):
        w_across(0, group)
        w_across(1, group)

    def chunk(k, _):
        at = pl.ds(pl.multiple_of(k * 128, 128), 128)
        place = base + k * 128 + lax.broadcasted_iota(jnp.int32, (128, 1), 0)
        key = base + k * 128 + lax.broadcasted_iota(jnp.int32, (1, 128), 1)
        begin = start_of(place, first, second)
        allowed = (key >= begin) & (key <= place)
        cross = jnp.dot(bc_rows[at, 64:128], bc_cols[0:64, at], preferred_element_type=F32)
        cross = jnp.where(allowed, cross, 0.0)
        lane = lax.broadcasted_iota(jnp.int32, (128, 128), 1)
        for pair in range(5):
            lanes = pl.ds(pair * 128, 128)
            scaled = step_e[at, lanes].astype(BF16)
            halves = []
            for h in (2 * pair, 2 * pair + 1):
                gap = run_rows[at, h:h + 1] - run_cols[h:h + 1, at]
                decay = jnp.exp(jnp.where(allowed, gap, -1e30))
                halves.append(jnp.dot((decay * cross).astype(BF16), scaled, preferred_element_type=F32))
            ys[at, lanes] = jnp.where(lane < 64, halves[0], halves[1])
        return 0

    lax.fori_loop(0, 2, chunk, 0)
    for one in pair:
        one.wait_recv()
    planes[z], planes_t[z] = joined(1, xl == 0)
    for d in (2, 1, 3):
        to = (seq_at(lax.rem(z + d, 4), xl, core), c)
        for one in (
            copy_to(planes_t.at[z], planes_t.at[z], st_send.at[2 + 2 * d], st_recv.at[4 + 2 * z], to),
            copy_to(planes.at[z], planes.at[z], st_send.at[3 + 2 * d], st_recv.at[5 + 2 * z], to),
        ):
            one.start()
            waits.append(one)
    w_first(1, 0)
    l_pb.wait()
    pb[...] = ao[...].astype(F32).T.astype(BF16)
    own_p = pltpu.make_async_copy(pb, p_rows(s), own_sem.at[0])
    own_p.start()
    lax.fori_loop(2, 4, chunk, 0)

    for k in range(1, 4):
        rows = slice(k * 128, k * 128 + 128)
        place = base + k * 128 + lax.broadcasted_iota(jnp.int32, (128, 1), 0)
        begin = start_of(place, first, second)
        enter = jnp.where(base + k * 128 - 1 >= begin,
                          jnp.exp(run_e[rows, :] - run_e[k * 128 - 1:k * 128, :]), 0.0)
        ys[rows, :] += enter * jnp.dot(bc_rows[rows, 64:128], states[k].astype(BF16), preferred_element_type=F32)

    l_gw.wait()
    for n, width in ((0, 256), (256, 256), (512, 128)):
        at = pl.ds(n, width)
        step_e[:, at] = silu(jnp.dot(tokens[...], gw[:, at], preferred_element_type=F32))

    enter_s = jnp.zeros((64, 640), F32)
    for d in (1, 2, 3):
        zz = lax.rem(z + d, 4)
        of = (seq_at(zz, xl, core), c)
        copy_to(planes_t.at[zz], planes_t.at[zz], st_send.at[0], st_recv.at[4 + 2 * zz], of).wait_recv()
        copy_to(planes.at[zz], planes.at[zz], st_send.at[0], st_recv.at[5 + 2 * zz], of).wait_recv()
    for zz in range(3):
        enter_s = jnp.where(zz < z, planes_t[zz, 0:1, :] * enter_s + planes[zz].astype(F32), enter_s)
    for i, low in ((1, xl == 0), (0, core == 0)):
        first_s = jnp.where(low, tx[i].astype(F32), rx[i].astype(F32))
        first_t = jnp.where(low, tx_t[i, 0:1, :], rx_t[i, 0:1, :])
        enter_s = jnp.where(low, enter_s, first_t * enter_s + first_s)
    states[0] = enter_s

    def gating(k, _):
        at = pl.ds(pl.multiple_of(k * 128, 128), 128)
        place = base + k * 128 + lax.broadcasted_iota(jnp.int32, (128, 1), 0)
        begin = start_of(place, first, second)
        enter = jnp.where(base - 1 >= begin, jnp.exp(run_e[at, :]), 0.0)
        y = ys[at, :] + enter * jnp.dot(bc_rows[at, 64:128], states[0].astype(BF16), preferred_element_type=F32)
        y = y + xs[at, :] * skip_e
        gated = y * step_e[at, :]
        sq_cols[at, :] = jnp.broadcast_to(jnp.sum(gated * gated, axis=-1, keepdims=True), (128, 128))
        weighted[at, :] = (gated * out_gain[...]).astype(BF16)
        return 0

    w_second(0, 0)
    lax.fori_loop(0, 4, gating, 0)
    sq_all[c] = sq_cols[...].T[0:1, :]
    l_ow.wait()

    gather = ChanSum(s, c, part, ring, fin, comb, across, rs_send, rs_recv)

    def make(turn):
        rows = pl.ds(pl.multiple_of(gather.column(turn) * 256, 256), 256)
        first_piece = gather.column(turn) * 4

        def columns(n, _):
            at = pl.ds(pl.multiple_of(n * 256, 256), 256)
            tile = jnp.dot(weighted[rows, :], ow[:, at], preferred_element_type=F32)
            part[pl.ds(first_piece, 4), :, at] = tile.astype(BF16).reshape(4, 64, 256)
            return 0

        lax.fori_loop(0, 10, columns, 0)

    make(0)
    gather.first(0)
    for i, p in enumerate(peers):
        few = copy_to(sq_all.at[c], sq_all.at[c], sq_send.at[i], sq_recv.at[c], (s, p))
        few.start()
        waits.append(few)
    make(1)
    gather.second(0)
    gather.first(1)
    w_second(1, 0)
    w_ring(xl, 0)
    gather.second(1)
    gather.cross()
    for i, p in enumerate(sources):
        copy_to(sq_all.at[p], sq_all.at[p], sq_send.at[0], sq_recv.at[p], (s, p)).wait_recv()
    gather.close()
    own64 = pl.ds(pl.multiple_of(c * 64, 64), 64)
    squares = sq_all[0]
    for i in range(1, 8):
        squares = squares + sq_all[i]
    sq_cols[...] = jnp.broadcast_to(squares, (128, 512)).T
    factor = lax.rsqrt(sq_cols[own64, 0:1] / 5120.0 + EPSILON)

    def gather_sum(n, _):
        at = pl.ds(pl.multiple_of(n * 256, 256), 256)
        mixed[c, :, at] = (hid[c, :, at].astype(F32) + gather.result(at) * factor).astype(BF16)
        return 0

    lax.fori_loop(0, 10, gather_sum, 0)
    xh, yy = c // 4, lax.rem(c, 4)
    y_up, y_down, y_far = lax.rem(yy + 1, 4), lax.rem(yy + 3, 4), lax.rem(yy + 2, 4)
    shared = [0]

    def m_rows(piece, side):
        return mixed.at[piece, pl.ds(side * 32, 32), :]

    def m_to(piece, side, to):
        rows = m_rows(piece, side)
        one = copy_to(rows, rows, ag_send.at[shared[0]], ag_recv.at[piece, side], (s, to))
        shared[0] += 1
        one.start()
        waits.append(one)

    def m_wait(piece, side):
        rows = m_rows(piece, side)
        copy_to(rows, rows, ag_send.at[0], ag_recv.at[piece, side], (s, (1 - xh) * 4 + yy)).wait_recv()

    def m_spread(piece):
        for side in (0, 1):
            m_to(piece, side, xh * 4 + y_up)
            m_to(piece, side, xh * 4 + y_down)

    def m_ring(col):
        for side in (0, 1):
            m_wait(col * 4 + y_down, side)
            m_wait(col * 4 + y_up, side)
            if side == 0:
                m_to(col * 4 + y_down, 0, xh * 4 + y_up)
        m_to(col * 4 + y_up, 1, xh * 4 + y_down)

    def m_end(col):
        for side in (0, 1):
            m_wait(col * 4 + y_far, side)

    for side in (0, 1):
        m_to(c, side, (1 - xh) * 4 + yy)
    m_spread(c)
    for one in gather.sent:
        one.wait_send()
    l_emb = load(9, embedding, part)
    w_ring(1 - xl, 0)
    w_first(1, 1)
    w_second(0, 1)
    m_ring(xh)
    for side in (0, 1):
        m_wait((1 - xh) * 4 + yy, side)
    m_spread((1 - xh) * 4 + yy)
    l_emb.wait()
    w_far(xl, 0)
    m_end(xh)

    def norm_second(p, _):
        at = pl.ds(pl.multiple_of(p * 64, 64), 64)
        top = mixed[p].astype(F32)
        low = part[p].astype(F32)
        mean = (jnp.sum(top * top, axis=-1, keepdims=True)
                + jnp.sum(low * low, axis=-1, keepdims=True)) / 5120.0
        scale = lax.rsqrt(mean + EPSILON)
        rows_in[at, pl.ds(0, 2560)] = (top * scale * attn_gain[:, pl.ds(0, 2560)]).astype(BF16)
        rows_in[at, pl.ds(2560, 2560)] = (low * scale * attn_gain[:, pl.ds(2560, 2560)]).astype(BF16)
        return 0

    def project_tiles(low, high, half):
        tokens_at = pl.ds(pl.multiple_of(half * 256, 256), 256)

        def project_tile(n, _):
            at = pl.ds(pl.multiple_of(n * 256, 256), 256)
            value = jnp.dot(rows_in[tokens_at, :], w[:, at], preferred_element_type=F32)
            flat_t[at, tokens_at] = value.T.astype(BF16)
            return 0

        lax.fori_loop(low, high, project_tile, 0)
        if high == 7:
            last = pl.ds(1792, 128)
            value = jnp.dot(rows_in[tokens_at, :], w[:, last], preferred_element_type=F32)
            flat_t[last, tokens_at] = value.T.astype(BF16)

    outs, recvs = (k_out, v_out), (k_recv, v_recv)

    def landing(lane, block, half):
        return outs[lane].at[block, :, pl.ds(pl.multiple_of(half * 256, 256), 256)]

    def head_rows(lane, head, half):
        return flat_t.at[pl.ds(pl.multiple_of(lane * 640 + head * 160, 32), 160),
                         pl.ds(pl.multiple_of(half * 256, 256), 256)]

    def first_stage(lane, half, turn):
        mine = pltpu.make_async_copy(head_rows(lane, z, half), landing(lane, s, half), local_sem.at[lane, turn])
        mine.start()
        for d in (2, 1, 3):
            to = lax.rem(z + d, 4)
            one = copy_to(head_rows(lane, to, half), landing(lane, s, half), z_send.at[lane, turn, d - 1],
                          recvs[lane].at[s, half], (seq_at(to, xl, core), c))
            one.start()
            waits.append(one)
        for there, sem in ((seq_at(z, 1 - xl, core), x_send), (sibling, d_send)):
            one = copy_to(head_rows(lane, z, half), landing(lane, s, half), sem.at[lane, turn, 0],
                          recvs[lane].at[s, half], (there, c))
            one.start()
            waits.append(one)
        return mine

    def block_wait(lane, block, half):
        rows = landing(lane, block, half)
        copy_to(rows, rows, z_send.at[0, 0, 0], recvs[lane].at[block, half], (sibling, c)).wait_recv()

    def block_to(lane, block, half, sem, there):
        rows = landing(lane, block, half)
        one = copy_to(rows, rows, sem, recvs[lane].at[block, half], (there, c))
        one.start()
        waits.append(one)

    def pass_on(lane, half, turn, d):
        block = seq_at(lax.rem(z + 4 - d, 4), xl, core)
        block_wait(lane, block, half)
        block_to(lane, block, half, x_send.at[lane, turn, d], seq_at(z, 1 - xl, core))
        block_to(lane, block, half, d_send.at[lane, turn, d], sibling)

    def relay(lane, half, turn, d):
        block = seq_at(lax.rem(z + 4 - d, 4), 1 - xl, core)
        block_wait(lane, block, half)
        block_to(lane, block, half, f_send.at[lane, turn, d], sibling)

    def send_queries(half, turn):
        for d in range(4):
            for j in range(2):
                to_z = lax.rem(z + d, 4)
                to = seq_at(to_z, half, j)
                piece = flat_t.at[pl.ds(pl.multiple_of(1280 + to_z * 160, 32), 160),
                                  pl.ds(pl.multiple_of(half * 256 + j * 128, 128), 128)]
                send_query(piece, to, d, j, turn, half)

    def send_query(piece, to, d, j, turn, half):
        remote = copy_to(piece, q_out.at[s], q_send.at[turn, d, j], q_recv.at[s], (to, c))
        if d:
            remote.start()
            waits.append(remote)
        else:
            mine = (half == xl) & (j == core)

            @pl.when(mine)
            def _():
                q_out[s] = piece[...]

            @pl.when(jnp.logical_not(mine))
            def _():
                remote.start()
                remote.wait_send()

    early, late = xh, 1 - xh
    lax.fori_loop(early * 4, early * 4 + 4, norm_second, 0)
    w_far(1 - xl, 0)
    w_last(0)
    project_tiles(0, 3, early)
    own = [first_stage(0, early, 0)]
    project_tiles(3, 5, early)
    own.append(first_stage(1, early, 0))
    w_second(1, 1)
    m_ring(1 - xh)
    for d in (1, 3):
        pass_on(0, early, 0, d)
    m_end(1 - xh)
    lax.fori_loop(late * 4, late * 4 + 4, norm_second, 0)
    project_tiles(0, 3, late)
    own.append(first_stage(0, late, 1))
    pass_on(0, early, 0, 2)
    for d in (1, 3):
        pass_on(1, early, 0, d)
    project_tiles(3, 5, late)
    own.append(first_stage(1, late, 1))
    w_ring(xl, 1)
    pass_on(1, early, 0, 2)
    relay(0, early, 0, 0)
    w_ring(1 - xl, 1)
    for lane in (0, 1):
        for d in (1, 3):
            pass_on(lane, late, 1, d)
    for d in (1, 3):
        relay(0, early, 0, d)
    for lane in (0, 1):
        pass_on(lane, late, 1, 2)
    p_first()
    w_far(xl, 1)
    w_far(1 - xl, 1)
    w_last(1)
    project_tiles(5, 7, early)
    send_queries(early, 0)
    project_tiles(5, 7, late)
    send_queries(late, 1)
    p_second()
    relay(0, early, 0, 2)
    for d in (0, 1, 3, 2):
        relay(1, early, 0, d)
    p_third()
    for lane in (0, 1):
        for d in (0, 1, 3, 2):
            relay(lane, late, 1, d)
    for half in (0, 1):
        for zz in range(4):
            for side in (0, 1):
                for lane in (0, 1):
                    block_wait(lane, seq_at(zz, side, 1 - core), half)
    for one in own:
        one.wait()
    for d in range(1, 16):
        block = lax.rem(s + d, 16)
        copy_to(q_out.at[block], q_out.at[block], q_send.at[0, 0, 0], q_recv.at[block], (block, c)).wait_recv()
    own_p.wait()
    p_last()
    for one in waits:
        one.wait_send()


def front(*operands):
    dma = pltpu.SemaphoreType.DMA
    vm, anyw = pl.BlockSpec(memory_space=VMEM), pl.BlockSpec(memory_space=pl.ANY)
    return pl.pallas_call(
        front_kernel,
        out_shape=(
            jax.ShapeDtypeStruct((8, 64, 2560), BF16),
            jax.ShapeDtypeStruct((16, 160, 512), BF16),
            jax.ShapeDtypeStruct((16, 160, 512), BF16),
            jax.ShapeDtypeStruct((16, 160, 128), BF16),
            jax.ShapeDtypeStruct((2560, 640), BF16),
        ),
        in_specs=[pl.BlockSpec(memory_space=pltpu.SMEM), anyw, vm, anyw, anyw, anyw, anyw, vm, vm, vm, vm,
                  anyw, anyw, vm, anyw, anyw, anyw, anyw],
        out_specs=(vm, anyw, anyw, vm, anyw),
        scratch_shapes=[
            VMEM((8, 64, 2560), BF16),
            VMEM((2560, 640), BF16),
            VMEM((2560, 640), BF16),
            VMEM((2560, 256), BF16),
            VMEM((2560, 10), BF16),
            VMEM((640, 2560), BF16),
            VMEM((640, 160), BF16),
            VMEM((8, 128), F32),
            VMEM((5120, 1920), BF16),
            VMEM((512, 5120), BF16),
            VMEM((8, 64, 2560), BF16),
            VMEM((1920, 512), BF16),
            VMEM((512, 640), F32),
            VMEM((512, 640), F32),
            VMEM((512, 640), F32),
            VMEM((4, 64, 640), F32),
            VMEM((2, 64, 640), BF16),
            VMEM((2, 64, 640), BF16),
            VMEM((4, 64, 640), BF16),
            VMEM((2, 8, 640), F32),
            VMEM((2, 8, 640), F32),
            VMEM((4, 8, 640), F32),
            VMEM((512, 128), F32),
            VMEM((128, 512), F32),
            VMEM((512, 640), F32),
            VMEM((512, 128), BF16),
            VMEM((128, 512), BF16),
            VMEM((160, 640), BF16),
            VMEM((8, 1, 512), F32),
            VMEM((512, 128), F32),
            VMEM((512, 640), BF16),
            dma((11,)),
            dma((60,)),
            dma((16, 2, 2)),
            dma((15,)),
            dma((16,)),
            dma((10,)),
            dma((12,)),
            dma((7,)),
            dma((8,)),
            *ring_scratch(64, 2560),
            dma((18,)),
            dma((8, 2)),
            dma((2, 2, 3)),
            dma((2, 2, 4)),
            dma((2, 2, 4)),
            dma((2, 2, 4)),
            dma((16, 2)),
            dma((16, 2)),
            dma((2, 4, 2)),
            dma((16,)),
            dma((2, 2)),
            dma((1,)),
        ],
        compiler_params=pltpu.CompilerParams(
            collective_id=0, has_side_effects=True, vmem_limit_bytes=67043328
        ),
        name="front",
    )(*operands)


def boundary(segments, value):
    count = jnp.int32(0)
    for bit in range(12, -1, -1):
        step = 1 << bit
        count = jnp.where(segments[count + step - 1] < value, count + step, count)
    return jnp.where(segments[jnp.minimum(count, 8191)] < value, count + 1, count)


def attend_kernel(segments, q_in, k_in, v_in, out, landed, keys, values, k_sem, v_sem):
    quarter = lax.rem(lax.axis_index("seq"), 4)

    def loads(j):
        return [
            pltpu.make_async_copy(src.at[2 * j + side], dst.at[j, :, pl.ds(side * 512, 512)], sem.at[2 * j + side])
            for side in (0, 1) for src, dst, sem in ((k_in, landed, k_sem), (v_in, values, v_sem))
        ]

    for j in range(8):
        for one in loads(j):
            one.start()
    first, second = boundary(segments, 1), boundary(segments, 2)
    scale = (AP ** -0.5) * 1.4426950408889634
    lane = lax.broadcasted_iota(jnp.int32, (1, 256), 1)

    def tile(i, _):
        for one in loads(i):
            one.wait()
        keys[i] = landed[i].astype(F32).T.astype(BF16)
        queries = jnp.concatenate([q_in[2 * i], q_in[2 * i + 1]], axis=1)
        low_place = i * 1024 + quarter * 128
        place = low_place + lane + jnp.where(lane >= 128, 384, 0)
        begin = start_of(place, first, second)
        lowest = start_of(low_place, first, second) // 1024
        plain_from = jnp.minimum((start_of(low_place + 639, first, second) + 1023) // 1024, i)

        def step(j, carry, masked):
            top, total, acc = carry
            scores = jnp.dot(keys[j], queries, preferred_element_type=F32)
            if masked:
                key = j * 1024 + lax.broadcasted_iota(jnp.int32, (1024, 256), 0)
                visible = (key >= begin) & (key <= place)
                scores = jnp.where(visible, scores, -1e30)
            new_top = jnp.maximum(top, jnp.max(scores, axis=0, keepdims=True))
            weights = jnp.exp2((scores - new_top) * scale)
            if masked:
                weights = jnp.where(visible, weights, 0.0)
            keep = jnp.exp2((top - new_top) * scale)
            total = total * keep + jnp.sum(weights, axis=0, keepdims=True)
            acc = acc * keep + jnp.dot(values[j], weights.astype(BF16), preferred_element_type=F32)
            return new_top, total, acc

        carry = (jnp.full((1, 256), -1e30, F32), jnp.zeros((1, 256), F32), jnp.zeros((AP, 256), F32))
        carry = lax.fori_loop(lowest, plain_from, lambda j, t: step(j, t, True), carry)
        carry = lax.fori_loop(jnp.maximum(lowest, plain_from), i, lambda j, t: step(j, t, False), carry)
        top, total, acc = step(i, carry, True)
        context = (acc / total).astype(BF16)
        out[2 * i] = context[:, :128]
        out[2 * i + 1] = context[:, 128:]
        return 0

    lax.fori_loop(0, 8, tile, 0)


def attend(segments, q_in, k_in, v_in):
    vm, anyw = pl.BlockSpec(memory_space=VMEM), pl.BlockSpec(memory_space=pl.ANY)
    return pl.pallas_call(
        attend_kernel,
        out_shape=jax.ShapeDtypeStruct((16, 160, 128), BF16),
        in_specs=[pl.BlockSpec(memory_space=pltpu.SMEM), vm, anyw, anyw],
        out_specs=vm,
        scratch_shapes=[
            VMEM((8, 160, 1024), BF16),
            VMEM((8, 1024, 160), BF16),
            VMEM((8, 160, 1024), BF16),
            pltpu.SemaphoreType.DMA((16,)),
            pltpu.SemaphoreType.DMA((16,)),
        ],
        compiler_params=pltpu.CompilerParams(vmem_limit_bytes=LIMIT),
        name="attend",
    )(segments, q_in, k_in, v_in)


def finish_kernel(ctx, proj_t, out, gathered, part, in_send, in_recv, ring, fin, comb, across, rs_send, rs_recv, local_sem):
    s, c = lax.axis_index("seq"), lax.axis_index("chan")
    peers = chan_peers(s, c)
    greet([(s, p) for p in peers] + [(lax.rem(s + d, 16), c) for d in range(1, 16)])
    z = s // 4
    lanes = pl.ds(pl.multiple_of(lax.rem(s, 4) * 128, 128), 128)
    waits = []
    for d in range(16):
        to = lax.rem(s + d, 16)
        where = gathered.at[pl.ds(pl.multiple_of(z * 160, 32), 160), lanes]
        if d == 0:
            own = pltpu.make_async_copy(ctx.at[s], where, local_sem.at[0])
            own.start()
        else:
            one = copy_to(ctx.at[to], where, in_send.at[d - 1], in_recv.at[s], (to, c))
            one.start()
            waits.append(one)
    own.wait()
    for d in range(1, 16):
        block = lax.rem(s + d, 16)
        where = gathered.at[pl.ds(pl.multiple_of((block // 4) * 160, 32), 160),
                            pl.ds(pl.multiple_of(lax.rem(block, 4) * 128, 128), 128)]
        copy_to(ctx.at[0], where, in_send.at[0], in_recv.at[block], (block, c)).wait_recv()
    gather = ChanSum(s, c, part, ring, fin, comb, across, rs_send, rs_recv)

    def make(turn):
        def rows_of(n, _):
            p = gather.column(turn) * 4 + n
            at = pl.ds(pl.multiple_of(p * 320, 32), 320)
            part[p] = jnp.dot(proj_t[at, :], gathered[...], preferred_element_type=F32).astype(BF16)
            return 0

        lax.fori_loop(0, 4, rows_of, 0)

    make(0)
    gather.first(0)
    make(1)
    gather.second(0)
    gather.first(1)
    gather.second(1)
    gather.cross()
    gather.close()
    for n in range(2):
        at = pl.ds(n * 256, 256)
        out[at, :] = gather.result(at).T
    for one in waits + gather.sent:
        one.wait_send()


def finish(ctx, proj_t):
    dma = pltpu.SemaphoreType.DMA
    vm = pl.BlockSpec(memory_space=VMEM)
    return pl.pallas_call(
        finish_kernel,
        out_shape=jax.ShapeDtypeStruct((512, 320), F32),
        in_specs=[vm, vm],
        out_specs=vm,
        scratch_shapes=[
            VMEM((640, 512), BF16),
            VMEM((8, 320, 512), BF16),
            dma((15,)),
            dma((16,)),
            *ring_scratch(320, 512),
            dma((1,)),
        ],
        compiler_params=pltpu.CompilerParams(
            collective_id=2, has_side_effects=True, vmem_limit_bytes=40 * 1024 * 1024
        ),
        cost_estimate=pl.CostEstimate(flops=50_000_000_000, bytes_accessed=6_000_000, transcendentals=0),
        name="finish",
    )(ctx, proj_t)


def local(
    hidden,
    embedding,
    segments,
    input_norm_gain,
    gate_proj,
    input_proj,
    state_proj,
    step_proj,
    step_bias,
    decay_log,
    skip_gain,
    out_gain,
    out_proj,
    attn_gain,
    query_proj,
    key_proj,
    value_proj,
    attn_out,
):
    chan_index = lax.axis_index("chan")
    mixed, k_all, v_all, q_all, proj_t = front(
        segments, hidden.reshape(8, 64, 2560), input_norm_gain[None, :], input_proj, gate_proj, state_proj,
        step_proj, step_bias[None, :], decay_log[None, :], skip_gain[None, :], out_gain[None, :],
        out_proj, embedding.reshape(8, 64, 2560), attn_gain[None, :], key_proj, value_proj, query_proj,
        attn_out,
    )
    ctx = attend(segments, q_all, k_all, v_all)
    out_share = finish(ctx, proj_t)
    own_mixed = lax.dynamic_slice_in_dim(mixed.reshape(512, 2560), chan_index * 320, 320, 1)
    return (out_share + own_mixed.astype(jnp.float32)).astype(jnp.bfloat16)


def solution(mesh):
    in_specs = (
        P("seq", None),
        P("seq", None),
        P(),
        P(),
        P(None, "chan"),
        P(None, "chan"),
        P(),
        P(None, "chan"),
        P("chan"),
        P("chan"),
        P("chan"),
        P("chan"),
        P("chan", None),
        P(),
        P("seq", "chan"),
        P("seq", "chan"),
        P("seq", "chan"),
        P("chan", "seq"),
    )
    out_specs = P("seq", "chan")
    return jax.shard_map(local, mesh=mesh, in_specs=in_specs, out_specs=out_specs, check_vma=False)
```

time: 260 us -> 234 us (0.900)
  Pallas kernels: 243 us -> 222 us
  other arithmetic: 7.7 us -> 1.25 us
    pallas_call x1, Pallas kernels: 168 us -> 153 us  [front(): pl.pallas_call(front_kernel, out_shape=(jax.ShapeDtypeStruct((8, 64, 2560...]
    pallas_call x1, Pallas kernels: 47.4 us -> 44.2 us  [finish(): pl.pallas_call(finish_kernel, out_shape=jax.ShapeDtypeStruct((512, 320),...]
    pallas_call x1, Pallas kernels: 27.6 us -> 24.6 us  [attend(): pl.pallas_call(attend_kernel, out_shape=jax.ShapeDtypeStruct((16, 160, 12...]
    unnamed x21 -> x6, local copies, waits for them, and re-layouts: 6.42 us -> 6.84 us
where the time goes in v3:
time: 234 us
  Pallas kernels  222 us (95%)
  local copies, waits for them, and re-layouts  10.3 us (4%)
    pallas_call x1, Pallas kernels, front(): pl.pallas_call(front_kernel, out_shape=(jax.ShapeDtypeStruct((8, 64, 2560...  153 us
    pallas_call x1, Pallas kernels, finish(): pl.pallas_call(finish_kernel, out_shape=jax.ShapeDtypeStruct((512, 320),...  44.2 us
    pallas_call x1, Pallas kernels, attend(): pl.pallas_call(attend_kernel, out_shape=jax.ShapeDtypeStruct((16, 160, 12...  24.6 us
    unnamed x6, local copies, waits for them, and re-layouts  6.84 us

profile of v3, /device:TPU:1, one launch (start us, length us, event | category | flops | bytes accessed | tf_op | source)
XLA Modules:
  0.0 233.5 jit_solution(8332931812017084006)
XLA Ops:
  0.0 2.0 copy.19.step_w
  2.0 1.8 copy.20.p_in
  3.8 1.3 broadcast_in_dim.18.norm_gain
  5.2 1.3 broadcast_in_dim.22.out_gain
  6.4 153.0 %front.1 = (bf16[8,64,2560]{2,1,0:T(8,128)(2,1)}, bf16[16,160,512]{2,1,0:T(8,128)(2,1)}, bf16[16,160,512]{2,1,0:T(8,128)(2,1)}, bf16[16,160,128]{2,1,0:T(8,128)(2,1)}, bf16[2560,640]{1,0:T(8,128)(2,1)}) custom-call(s32[8192]{0:T(1024)} %segments.3, bf16[8,64,2560]{2,1,0:T(8,128)(2,1)} %bitcast.7, f32[1,2560]{1,0:T(1,128)} %broadcast_in_dim.18.norm_gain, ...), custom_call_target="tpu_custom_call" | custom-call | tf_op jit(solution)/shard_map/front/pallas_call | solution.py:730
  159.4 24.6 %attend.1.ctx = bf16[16,160,128]{2,1,0:T(8,128)(2,1)} custom-call(s32[8192]{0:T(1024)} %segments.3, bf16[16,160,128]{2,1,0:T(8,128)(2,1)} %get-tuple-element.10.q_in, bf16[16,160,512]{2,1,0:T(8,128)(2,1)} %get-tuple-element.11.k_in, bf16[16,160,512]{2,1,0:T(8,128)(2,1)} %get-tuple-element.12.v_in), custom_call_target="tpu_custom_call" | custom-call | tf_op jit(solution)/shard_map/attend/pallas_call | solution.py:869
  184.1 0.0 copy-start
  184.1 1.1 copy-done
  185.2 0.0 copy-start.1
  185.2 1.9 copy-done.1
  187.1 44.2 %finish.1 = f32[512,320]{1,0:T(8,128)S(1)} custom-call(bf16[16,160,128]{2,1,0:T(8,128)(2,1)S(1)} %copy-done, bf16[2560,640]{1,0:T(8,128)(2,1)S(1)} %copy-done.1), custom_call_target="tpu_custom_call" | custom-call | flops 49999998976 | bytes 6000000 | tf_op jit(solution)/shard_map/finish/pallas_call | solution.py:938
  231.3 1.3 add_convert_fusion
  232.6 0.9 copy.21
Async XLA Ops:
  184.1 1.1 copy-start
  185.2 1.9 copy-start.1

commit v4 on v3

--- a/solution.py
+++ b/solution.py
@@ -11,7 +11,6 @@
 EPSILON = 1e-05
 MESH = pl.DeviceIdType.MESH
 VMEM = pltpu.VMEM
-LIMIT = 62 * 1024 * 1024
 F32 = jnp.float32
 BF16 = jnp.bfloat16
 
@@ -154,8 +153,8 @@
 
 def front_kernel(segments, hidden, norm_gain, input_w, gate_w, state_w, step_w, bias, decay, skip, out_gain,
                  out_w, embedding, attn_gain, wk, wv, wq, p_in,
-                 mixed, k_out, v_out, q_out, p_out,
-                 hid, iw, gw, sw, dw, ow, ao, vec, w, rows_in, part, flat_t, run_e, xs, ys, states, tx, rx, planes, tx_t, rx_t, planes_t,
+                 mixed_out, k_out, v_out, q_out, p_out,
+                 mixed, hid, iw, gw, sw, dw, dwt, ow, vec, w, rows_in, part, flat_t, run_e, xs, ys, states, tx, rx, planes, tx_t, rx_t, planes_t,
                  run_rows, run_cols, step_e, bc_rows, bc_cols, pb, sq_all, sq_cols, weighted,
                  load_sem, w_send, w_recv, p_send, p_recv, st_send, st_recv,
                  sq_send, sq_recv, ring, fin, comb, across, rs_send, rs_recv, ag_send, ag_recv,
@@ -174,10 +173,10 @@
     own_rows = pl.ds(pl.multiple_of(s * 320, 64), 320)
     w_loads = [load(i, src, w.at[own_rows, pl.ds(i * 640, 640)]) for i, src in enumerate((wk, wv, wq))]
     l_hid = load(3, hidden, hid)
-    l_sw = load(4, state_w, sw.at[:, pl.ds(0, 128)])
+    l_sw = load(4, state_w, sw)
     l_dw = load(10, step_w, dw)
     l_iw = load(5, input_w, iw)
-    l_pb = load(6, p_in, ao)
+    l_pb = load(6, p_in, pb)
     l_gw = load(7, gate_w, gw)
     l_ow = load(8, out_w, ow)
     greet([(s, p) for p in peers] + [(lax.rem(s + d, 16), c) for d in range(1, 16)])
@@ -290,29 +289,30 @@
     first, second = boundary(segments, 1), boundary(segments, 2)
     base = s * 512
     l_hid.wait()
+    norm_row = norm_gain[...].reshape(1, 2560)
+    out_row = out_gain[...].reshape(1, 640)
 
     def norm_first(p, _):
         at = pl.ds(pl.multiple_of(p * 64, 64), 64)
         value = hid[p].astype(F32)
         factor = lax.rsqrt(jnp.sum(value * value, axis=-1, keepdims=True) / 2560.0 + EPSILON)
-        rows_in[at, pl.ds(0, 2560)] = (value * factor * norm_gain[...]).astype(BF16)
+        rows_in[at, pl.ds(0, 2560)] = (value * factor * norm_row).astype(BF16)
         return 0
 
     lax.fori_loop(0, 8, norm_first, 0)
     tokens = rows_in.at[:, pl.ds(0, 2560)]
-    sw[:, 128:256] = jnp.zeros((2560, 128), BF16)
     vec[...] = jnp.zeros((8, 128), F32)
+    dwt[...] = jnp.zeros((128, 2560), BF16)
     vec[0:1, 0:10] = bias[...]
     vec[1:2, 0:10] = decay[...]
     vec[2:3, 0:10] = skip[...]
     l_sw.wait()
     l_dw.wait()
-    sw[:, 128:138] = dw[...]
-    both = jnp.dot(tokens[...], sw[...], preferred_element_type=F32)
-    bc = silu(both[:, :128])
+    dwt[0:10, :] = dw[...]
+    bc = silu(jnp.dot(tokens[...], sw[...], preferred_element_type=F32))
     bc_rows[...] = bc.astype(BF16)
     bc_cols[...] = bc.T.astype(BF16)
-    logits = both[:, 128:] + vec[0:1, :]
+    logits = lax.dot_general(tokens[...], dwt[...], (((1,), (1,)), ((), ())), preferred_element_type=F32) + vec[0:1, :]
     steps = jnp.maximum(logits, 0.0) + jnp.log1p(jnp.exp(-jnp.abs(logits)))
     rate = -jnp.exp(vec[1:2, :])
     lower = (lax.broadcasted_iota(jnp.int32, (512, 512), 0)
@@ -418,7 +418,6 @@
             waits.append(one)
     w_first(1, 0)
     l_pb.wait()
-    pb[...] = ao[...].astype(F32).T.astype(BF16)
     own_p = pltpu.make_async_copy(pb, p_rows(s), own_sem.at[0])
     own_p.start()
     lax.fori_loop(2, 4, chunk, 0)
@@ -459,7 +458,7 @@
         y = y + xs[at, :] * skip_e
         gated = y * step_e[at, :]
         sq_cols[at, :] = jnp.broadcast_to(jnp.sum(gated * gated, axis=-1, keepdims=True), (128, 128))
-        weighted[at, :] = (gated * out_gain[...]).astype(BF16)
+        weighted[at, :] = (gated * out_row).astype(BF16)
         return 0
 
     w_second(0, 0)
@@ -649,17 +648,19 @@
             remote.start()
             waits.append(remote)
         else:
+            here = pltpu.make_async_copy(piece, q_out.at[s], own_sem.at[2])
             mine = (half == xl) & (j == core)
+            near.append((mine, here, remote))
 
             @pl.when(mine)
             def _():
-                q_out[s] = piece[...]
+                here.start()
 
             @pl.when(jnp.logical_not(mine))
             def _():
                 remote.start()
-                remote.wait_send()
-
+
+    near = []
     early, late = xh, 1 - xh
     lax.fori_loop(early * 4, early * 4 + 4, norm_second, 0)
     w_far(1 - xl, 0)
@@ -673,6 +674,8 @@
     for d in (1, 3):
         pass_on(0, early, 0, d)
     m_end(1 - xh)
+    kept = pltpu.make_async_copy(mixed, mixed_out, own_sem.at[1])
+    kept.start()
     lax.fori_loop(late * 4, late * 4 + 4, norm_second, 0)
     project_tiles(0, 3, late)
     own.append(first_stage(0, late, 1))
@@ -704,10 +707,10 @@
     relay(0, early, 0, 2)
     for d in (0, 1, 3, 2):
         relay(1, early, 0, d)
-    p_third()
     for lane in (0, 1):
         for d in (0, 1, 3, 2):
             relay(lane, late, 1, d)
+    p_third()
     for half in (0, 1):
         for zz in range(4):
             for side in (0, 1):
@@ -719,7 +722,17 @@
         block = lax.rem(s + d, 16)
         copy_to(q_out.at[block], q_out.at[block], q_send.at[0, 0, 0], q_recv.at[block], (block, c)).wait_recv()
     own_p.wait()
+    kept.wait()
     p_last()
+    for mine, here, remote in near:
+        @pl.when(mine)
+        def _():
+            here.wait()
+
+        @pl.when(jnp.logical_not(mine))
+        def _():
+            remote.wait_send()
+
     for one in waits:
         one.wait_send()
 
@@ -738,15 +751,16 @@
         ),
         in_specs=[pl.BlockSpec(memory_space=pltpu.SMEM), anyw, vm, anyw, anyw, anyw, anyw, vm, vm, vm, vm,
                   anyw, anyw, vm, anyw, anyw, anyw, anyw],
-        out_specs=(vm, anyw, anyw, vm, anyw),
+        out_specs=(anyw, anyw, anyw, anyw, anyw),
         scratch_shapes=[
+            VMEM((8, 64, 2560), BF16),
             VMEM((8, 64, 2560), BF16),
             VMEM((2560, 640), BF16),
             VMEM((2560, 640), BF16),
-            VMEM((2560, 256), BF16),
-            VMEM((2560, 10), BF16),
+            VMEM((2560, 128), BF16),
+            VMEM((10, 2560), BF16),
+            VMEM((128, 2560), BF16),
             VMEM((640, 2560), BF16),
-            VMEM((640, 160), BF16),
             VMEM((8, 128), F32),
             VMEM((5120, 1920), BF16),
             VMEM((512, 5120), BF16),
@@ -792,7 +806,7 @@
             dma((2, 4, 2)),
             dma((16,)),
             dma((2, 2)),
-            dma((1,)),
+            dma((3,)),
         ],
         compiler_params=pltpu.CompilerParams(
             collective_id=0, has_side_effects=True, vmem_limit_bytes=67043328
@@ -809,59 +823,66 @@
     return jnp.where(segments[jnp.minimum(count, 8191)] < value, count + 1, count)
 
 
-def attend_kernel(segments, q_in, k_in, v_in, out, landed, keys, values, k_sem, v_sem):
+def attend_kernel(segments, q_hbm, k_in, v_in, out, q_in, landed, keys, values, q_sem, k_sem, v_sem):
     quarter = lax.rem(lax.axis_index("seq"), 4)
 
     def loads(j):
         return [
-            pltpu.make_async_copy(src.at[2 * j + side], dst.at[j, :, pl.ds(side * 512, 512)], sem.at[2 * j + side])
-            for side in (0, 1) for src, dst, sem in ((k_in, landed, k_sem), (v_in, values, v_sem))
+            pltpu.make_async_copy(src.at[4 * j + side], dst.at[j, :, pl.ds(side * 512, 512)], sem.at[4 * j + side])
+            for side in range(4) for src, dst, sem in ((k_in, landed, k_sem), (v_in, values, v_sem))
         ]
 
-    for j in range(8):
+    q_load = pltpu.make_async_copy(q_hbm, q_in, q_sem)
+    q_load.start()
+    for j in range(4):
         for one in loads(j):
             one.start()
     first, second = boundary(segments, 1), boundary(segments, 2)
     scale = (AP ** -0.5) * 1.4426950408889634
-    lane = lax.broadcasted_iota(jnp.int32, (1, 256), 1)
+    lane = lax.broadcasted_iota(jnp.int32, (1, 512), 1)
+    q_load.wait()
 
     def tile(i, _):
-        for one in loads(i):
-            one.wait()
-        keys[i] = landed[i].astype(F32).T.astype(BF16)
-        queries = jnp.concatenate([q_in[2 * i], q_in[2 * i + 1]], axis=1)
-        low_place = i * 1024 + quarter * 128
-        place = low_place + lane + jnp.where(lane >= 128, 384, 0)
+        for n in range(1):
+            for one in loads(i * 1 + n):
+                one.wait()
+            keys[i * 1 + n] = landed[i * 1 + n].astype(F32).T.astype(BF16)
+        queries = jnp.concatenate([q_in[4 * i + n] for n in range(4)], axis=1)
+        low_place = i * 2048 + quarter * 128
+        place = low_place + lane + 384 * (lane // 128)
         begin = start_of(place, first, second)
-        lowest = start_of(low_place, first, second) // 1024
-        plain_from = jnp.minimum((start_of(low_place + 639, first, second) + 1023) // 1024, i)
-
-        def step(j, carry, masked):
+        lowest = start_of(low_place, first, second) // 2048
+        last_begin = start_of(low_place + 1663, first, second)
+        plain_from = jnp.minimum((last_begin + 2047) // 2048, i * 1)
+
+        def step(j, carry, causal, reset):
             top, total, acc = carry
             scores = jnp.dot(keys[j], queries, preferred_element_type=F32)
-            if masked:
-                key = j * 1024 + lax.broadcasted_iota(jnp.int32, (1024, 256), 0)
-                visible = (key >= begin) & (key <= place)
+            if causal or reset:
+                key = j * 2048 + lax.broadcasted_iota(jnp.int32, (2048, 512), 0)
+                visible = key >= begin
+                if causal:
+                    visible = visible & (key <= place)
                 scores = jnp.where(visible, scores, -1e30)
             new_top = jnp.maximum(top, jnp.max(scores, axis=0, keepdims=True))
             weights = jnp.exp2((scores - new_top) * scale)
-            if masked:
-                weights = jnp.where(visible, weights, 0.0)
             keep = jnp.exp2((top - new_top) * scale)
             total = total * keep + jnp.sum(weights, axis=0, keepdims=True)
             acc = acc * keep + jnp.dot(values[j], weights.astype(BF16), preferred_element_type=F32)
             return new_top, total, acc
 
-        carry = (jnp.full((1, 256), -1e30, F32), jnp.zeros((1, 256), F32), jnp.zeros((AP, 256), F32))
-        carry = lax.fori_loop(lowest, plain_from, lambda j, t: step(j, t, True), carry)
-        carry = lax.fori_loop(jnp.maximum(lowest, plain_from), i, lambda j, t: step(j, t, False), carry)
-        top, total, acc = step(i, carry, True)
+        carry = (jnp.full((1, 512), -1e29, F32), jnp.zeros((1, 512), F32), jnp.zeros((AP, 512), F32))
+        carry = lax.fori_loop(lowest, plain_from, lambda j, t: step(j, t, False, True), carry)
+        carry = lax.fori_loop(
+            jnp.maximum(lowest, plain_from), i * 1, lambda j, t: step(j, t, False, False), carry)
+        top, total, acc = lax.fori_loop(
+            jnp.maximum(lowest, i * 1), i * 1 + 1, lambda j, t: step(j, t, True, True), carry)
         context = (acc / total).astype(BF16)
-        out[2 * i] = context[:, :128]
-        out[2 * i + 1] = context[:, 128:]
+        for n in range(4):
+            out[4 * i + n] = context[:, n * 128:n * 128 + 128]
         return 0
 
-    lax.fori_loop(0, 8, tile, 0)
+    lax.fori_loop(0, 4, tile, 0)
 
 
 def attend(segments, q_in, k_in, v_in):
@@ -869,23 +890,30 @@
     return pl.pallas_call(
         attend_kernel,
         out_shape=jax.ShapeDtypeStruct((16, 160, 128), BF16),
-        in_specs=[pl.BlockSpec(memory_space=pltpu.SMEM), vm, anyw, anyw],
+        in_specs=[pl.BlockSpec(memory_space=pltpu.SMEM), anyw, anyw, anyw],
         out_specs=vm,
         scratch_shapes=[
-            VMEM((8, 160, 1024), BF16),
-            VMEM((8, 1024, 160), BF16),
-            VMEM((8, 160, 1024), BF16),
+            VMEM((16, 160, 128), BF16),
+            VMEM((4, 160, 2048), BF16),
+            VMEM((4, 2048, 160), BF16),
+            VMEM((4, 160, 2048), BF16),
+            pltpu.SemaphoreType.DMA,
             pltpu.SemaphoreType.DMA((16,)),
             pltpu.SemaphoreType.DMA((16,)),
         ],
-        compiler_params=pltpu.CompilerParams(vmem_limit_bytes=LIMIT),
+        compiler_params=pltpu.CompilerParams(vmem_limit_bytes=67043328),
         name="attend",
     )(segments, q_in, k_in, v_in)
 
 
-def finish_kernel(ctx, proj_t, out, gathered, part, in_send, in_recv, ring, fin, comb, across, rs_send, rs_recv, local_sem):
+def finish_kernel(ctx, proj_in, mixed, out, proj_t, own_in, gathered, part, in_send, in_recv, ring, fin, comb, across, rs_send, rs_recv, local_sem):
     s, c = lax.axis_index("seq"), lax.axis_index("chan")
     peers = chan_peers(s, c)
+    proj_load = pltpu.make_async_copy(proj_in, proj_t, local_sem.at[1])
+    proj_load.start()
+    window = pl.ds(pl.multiple_of(c * 5 // 2 * 128, 128), 384)
+    own_load = pltpu.make_async_copy(mixed.at[:, window], own_in, local_sem.at[2])
+    own_load.start()
     greet([(s, p) for p in peers] + [(lax.rem(s + d, 16), c) for d in range(1, 16)])
     z = s // 4
     lanes = pl.ds(pl.multiple_of(lax.rem(s, 4) * 128, 128), 128)
@@ -917,6 +945,7 @@
 
         lax.fori_loop(0, 4, rows_of, 0)
 
+    proj_load.wait()
     make(0)
     gather.first(0)
     make(1)
@@ -924,36 +953,42 @@
     gather.first(1)
     gather.second(1)
     gather.cross()
+    own_load.wait()
+    own_t_all = [own_in[n * 256:(n + 1) * 256, :].astype(F32).T for n in range(2)]
     gather.close()
+    odd = lax.rem(c, 2) == 1
     for n in range(2):
         at = pl.ds(n * 256, 256)
-        out[at, :] = gather.result(at).T
+        own_t = own_t_all[n]
+        out[:, at] = (gather.result(at) + jnp.where(odd, own_t[64:, :], own_t[:320, :])).astype(BF16)
     for one in waits + gather.sent:
         one.wait_send()
 
 
-def finish(ctx, proj_t):
+def finish(ctx, proj_t, mixed):
     dma = pltpu.SemaphoreType.DMA
-    vm = pl.BlockSpec(memory_space=VMEM)
+    vm, anyw = pl.BlockSpec(memory_space=VMEM), pl.BlockSpec(memory_space=pl.ANY)
     return pl.pallas_call(
         finish_kernel,
-        out_shape=jax.ShapeDtypeStruct((512, 320), F32),
-        in_specs=[vm, vm],
+        out_shape=jax.ShapeDtypeStruct((320, 512), BF16),
+        in_specs=[anyw, anyw, anyw],
         out_specs=vm,
         scratch_shapes=[
+            VMEM((2560, 640), BF16),
+            VMEM((512, 384), BF16),
             VMEM((640, 512), BF16),
             VMEM((8, 320, 512), BF16),
             dma((15,)),
             dma((16,)),
             *ring_scratch(320, 512),
-            dma((1,)),
+            dma((3,)),
         ],
         compiler_params=pltpu.CompilerParams(
-            collective_id=2, has_side_effects=True, vmem_limit_bytes=40 * 1024 * 1024
+            collective_id=2, has_side_effects=True, vmem_limit_bytes=67043328
         ),
         cost_estimate=pl.CostEstimate(flops=50_000_000_000, bytes_accessed=6_000_000, transcendentals=0),
         name="finish",
-    )(ctx, proj_t)
+    )(ctx, proj_t, mixed)
 
 
 def local(
@@ -976,17 +1011,14 @@
     value_proj,
     attn_out,
 ):
-    chan_index = lax.axis_index("chan")
     mixed, k_all, v_all, q_all, proj_t = front(
-        segments, hidden.reshape(8, 64, 2560), input_norm_gain[None, :], input_proj, gate_proj, state_proj,
-        step_proj, step_bias[None, :], decay_log[None, :], skip_gain[None, :], out_gain[None, :],
+        segments, hidden.reshape(8, 64, 2560), input_norm_gain, input_proj, gate_proj, state_proj,
+        step_proj.T, step_bias[None, :], decay_log[None, :], skip_gain[None, :], out_gain,
         out_proj, embedding.reshape(8, 64, 2560), attn_gain[None, :], key_proj, value_proj, query_proj,
-        attn_out,
+        attn_out.T,
     )
     ctx = attend(segments, q_all, k_all, v_all)
-    out_share = finish(ctx, proj_t)
-    own_mixed = lax.dynamic_slice_in_dim(mixed.reshape(512, 2560), chan_index * 320, 320, 1)
-    return (out_share + own_mixed.astype(jnp.float32)).astype(jnp.bfloat16)
+    return finish(ctx, proj_t, mixed.reshape(512, 2560)).T
 
 
 def solution(mesh):

time: 234 us -> 220 us (0.940)
  local copies, waits for them, and re-layouts: 10.3 us -> 1.72 us
    unnamed x6 -> x1, local copies, waits for them, and re-layouts: 6.84 us -> 1.72 us
    pallas_call x1, Pallas kernels: 153 us -> 150 us  [front(): pl.pallas_call(front_kernel, out_shape=(jax.ShapeDtypeStruct((8, 64, 2560...]
    broadcast_in_dim x2 -> x0, local copies, waits for them, and re-layouts: 2.56 us -> none  [the longest x1 1.31 us: local(): input_norm_gain[None, :]]
    pallas_call x1, Pallas kernels: 24.6 us -> 27.1 us  [attend(): pl.pallas_call(attend_kernel, out_shape=jax.ShapeDtypeStruct((16, 160, 12...]
where the time goes in v4:
time: 220 us; the launch traced here: 222 us
  Pallas kernels  220 us (100%)
    pallas_call x1, Pallas kernels, front(): pl.pallas_call(front_kernel, out_shape=(jax.ShapeDtypeStruct((8, 64, 2560...  150 us
    pallas_call x1, Pallas kernels, finish(): pl.pallas_call(finish_kernel, out_shape=jax.ShapeDtypeStruct((320, 512),...  42.7 us
    pallas_call x1, Pallas kernels, attend(): pl.pallas_call(attend_kernel, out_shape=jax.ShapeDtypeStruct((16, 160, 12...  27.1 us

profile of v4, /device:TPU:1, one launch (start us, length us, event | category | flops | bytes accessed | tf_op | source)
XLA Modules:
  0.0 221.8 jit_solution(5693235469191459373)
XLA Ops:
  0.0 150.2 %front.1 = (bf16[8,64,2560]{2,1,0:T(8,128)(2,1)}, bf16[16,160,512]{2,1,0:T(8,128)(2,1)}, bf16[16,160,512]{2,1,0:T(8,128)(2,1)}, bf16[16,160,128]{2,1,0:T(8,128)(2,1)}, bf16[2560,640]{1,0:T(8,128)(2,1)}) custom-call(s32[8192]{0:T(1024)} %segments.3, bf16[8,64,2560]{2,1,0:T(8,128)(2,1)} %bitcast.10, f32[2560]{0:T(1024)} %norm_gain.1, ...), custom_call_target="tpu_custom_call" | custom-call | tf_op jit(solution)/shard_map/front/pallas_call | solution.py:743
  150.3 27.1 %attend.1.ctx = bf16[16,160,128]{2,1,0:T(8,128)(2,1)} custom-call(s32[8192]{0:T(1024)} %segments.3, bf16[16,160,128]{2,1,0:T(8,128)(2,1)} %get-tuple-element.10.q_hbm, bf16[16,160,512]{2,1,0:T(8,128)(2,1)} %get-tuple-element.11.k_in, bf16[16,160,512]{2,1,0:T(8,128)(2,1)} %get-tuple-element.12.v_in), custom_call_target="tpu_custom_call" | custom-call | tf_op jit(solution)/shard_map/attend/pallas_call | solution.py:890
  177.3 42.7 %finish.1 = bf16[320,512]{1,0:T(8,128)(2,1)} custom-call(bf16[16,160,128]{2,1,0:T(8,128)(2,1)} %attend.1.ctx, bf16[2560,640]{1,0:T(8,128)(2,1)} %get-tuple-element.13.proj_in, bf16[512,2560]{1,0:T(8,128)(2,1)} %bitcast.19), custom_call_target="tpu_custom_call" | custom-call | flops 49999998976 | bytes 6000000 | tf_op jit(solution)/shard_map/finish/pallas_call | solution.py:971
  220.1 1.7 copy.20

commit v5 on v4

--- a/solution.py
+++ b/solution.py
@@ -145,6 +145,14 @@
 
 def start_of(place, first, second):
     return jnp.where(place >= second, second, jnp.where(place >= first, first, 0))
+
+
+def three_parts(value):
+    high = value.astype(BF16)
+    rest = value - high.astype(F32)
+    middle = rest.astype(BF16)
+    low = (rest - middle.astype(F32)).astype(BF16)
+    return jnp.concatenate([high, middle, low], axis=1)
 
 
 def silu(v):
@@ -199,19 +207,19 @@
         rows = w_rows(block, half, group)
         copy_to(rows, rows, w_send.at[0], w_recv.at[block, half, group], (sibling, c)).wait_recv()
 
-    def p_rows(block):
-        return p_out.at[pl.ds(pl.multiple_of(block * 160, 32), 160), :]
-
-    def p_to(block, to, src=None):
-        rows = p_rows(block)
-        one = copy_to(rows if src is None else src, rows, p_send.at[used[1]], p_recv.at[block], (to, c))
+    def p_rows(block, half):
+        return p_out.at[pl.ds(pl.multiple_of(block * 160 + half * 80, 16), 80), :]
+
+    def p_to(block, half, to, src=None):
+        rows = p_rows(block, half)
+        one = copy_to(rows if src is None else src, rows, p_send.at[used[1]], p_recv.at[block, half], (to, c))
         used[1] += 1
         one.start()
         waits.append(one)
 
-    def p_wait(block):
-        rows = p_rows(block)
-        copy_to(rows, rows, p_send.at[0], p_recv.at[block], (seq_at(z, xl, 1 - core), c)).wait_recv()
+    def p_wait(block, half):
+        rows = p_rows(block, half)
+        copy_to(rows, rows, p_send.at[0], p_recv.at[block, half], (sibling, c)).wait_recv()
 
     def w_across(half, group):
         w_to(s, half, group, seq_at(z, 1 - xl, core))
@@ -251,35 +259,42 @@
                     w_wait(seq_at(zz, xx, 1 - core), half, group)
 
     def p_first():
-        for to in (seq_at(z, 1 - xl, core), seq_at(up, xl, core), seq_at(down, xl, core), sibling):
-            p_to(s, to, pb)
+        for half in (0, 1):
+            for to in (seq_at(z, 1 - xl, core), seq_at(up, xl, core), seq_at(down, xl, core), sibling):
+                p_to(s, half, to, pb.at[pl.ds(half * 80, 80), :])
 
     def p_second():
         block = seq_at(z, 1 - xl, core)
-        p_wait(block)
-        for to in (seq_at(up, xl, core), seq_at(down, xl, core), sibling):
-            p_to(block, to)
-        p_wait(seq_at(down, xl, core))
-        p_wait(seq_at(up, xl, core))
-        p_to(seq_at(down, xl, core), seq_at(up, xl, core))
-        p_to(seq_at(down, xl, core), sibling)
-        p_to(seq_at(up, xl, core), sibling)
+        for half in (0, 1):
+            p_wait(block, half)
+            for to in (seq_at(up, xl, core), seq_at(down, xl, core), sibling):
+                p_to(block, half, to)
+        p_ring(xl)
+
+    def p_ring(side):
+        for half in (0, 1):
+            p_wait(seq_at(down, side, core), half)
+            p_wait(seq_at(up, side, core), half)
+        p_to(seq_at(down, side, core), 0, seq_at(up, xl, core))
+        p_to(seq_at(up, side, core), 1, seq_at(down, xl, core))
+        for half in (0, 1):
+            p_to(seq_at(down, side, core), half, sibling)
+            p_to(seq_at(up, side, core), half, sibling)
 
     def p_third():
-        p_wait(seq_at(down, 1 - xl, core))
-        p_wait(seq_at(up, 1 - xl, core))
-        p_to(seq_at(down, 1 - xl, core), seq_at(up, xl, core))
-        p_to(seq_at(down, 1 - xl, core), sibling)
-        p_to(seq_at(up, 1 - xl, core), sibling)
-        p_wait(seq_at(far, xl, core))
-        p_to(seq_at(far, xl, core), sibling)
+        p_ring(1 - xl)
+        for half in (0, 1):
+            p_wait(seq_at(far, xl, core), half)
+            p_to(seq_at(far, xl, core), half, sibling)
 
     def p_last():
-        p_wait(seq_at(far, 1 - xl, core))
-        p_to(seq_at(far, 1 - xl, core), sibling)
+        for half in (0, 1):
+            p_wait(seq_at(far, 1 - xl, core), half)
+            p_to(seq_at(far, 1 - xl, core), half, sibling)
         for zz in range(4):
             for xx in range(2):
-                p_wait(seq_at(zz, xx, 1 - core))
+                for half in (0, 1):
+                    p_wait(seq_at(zz, xx, 1 - core), half)
 
     for one in w_loads:
         one.wait()
@@ -316,16 +331,16 @@
     steps = jnp.maximum(logits, 0.0) + jnp.log1p(jnp.exp(-jnp.abs(logits)))
     rate = -jnp.exp(vec[1:2, :])
     lower = (lax.broadcasted_iota(jnp.int32, (512, 512), 0)
-             >= lax.broadcasted_iota(jnp.int32, (512, 512), 1)).astype(F32)
-    running = jnp.dot(lower, steps * rate, preferred_element_type=F32, precision=lax.Precision.HIGHEST)
-    spread = (lax.broadcasted_iota(jnp.int32, (128, 640), 1) // 64
-              == lax.broadcasted_iota(jnp.int32, (128, 640), 0)).astype(F32)
+             >= lax.broadcasted_iota(jnp.int32, (512, 512), 1)).astype(F32).astype(BF16)
+    sums = jnp.dot(lower, three_parts(steps * rate), preferred_element_type=F32)
+    running = sums[:, :128] + sums[:, 128:256] + sums[:, 256:]
+    spread = (lax.broadcasted_iota(jnp.int32, (384, 640), 1) // 64
+              == lax.rem(lax.broadcasted_iota(jnp.int32, (384, 640), 0), 128)).astype(F32).astype(BF16)
     run_rows[...] = running
     run_cols[...] = running.T
-    wide_steps = jnp.dot(steps, spread, preferred_element_type=F32, precision=lax.Precision.HIGHEST)
-    run_e[...] = jnp.dot(running, spread, preferred_element_type=F32, precision=lax.Precision.HIGHEST)
-    step_e[...] = wide_steps
-    skip_e = jnp.dot(vec[...], spread, preferred_element_type=F32, precision=lax.Precision.HIGHEST)[2:3, :]
+    run_e[...] = jnp.dot(three_parts(running), spread, preferred_element_type=F32)
+    step_e[...] = jnp.dot(three_parts(steps), spread, preferred_element_type=F32)
+    skip_e = jnp.dot(three_parts(vec[...]), spread, preferred_element_type=F32)[2:3, :]
     l_iw.wait()
 
     def input_tile(n, width):
@@ -418,7 +433,8 @@
             waits.append(one)
     w_first(1, 0)
     l_pb.wait()
-    own_p = pltpu.make_async_copy(pb, p_rows(s), own_sem.at[0])
+    own_p = pltpu.make_async_copy(
+        pb, p_out.at[pl.ds(pl.multiple_of(s * 160, 32), 160), :], own_sem.at[0])
     own_p.start()
     lax.fori_loop(2, 4, chunk, 0)
 
@@ -491,8 +507,9 @@
     gather.first(1)
     w_second(1, 0)
     w_ring(xl, 0)
+    w_first(1, 1)
+    gather.cross()
     gather.second(1)
-    gather.cross()
     for i, p in enumerate(sources):
         copy_to(sq_all.at[p], sq_all.at[p], sq_send.at[0], sq_recv.at[p], (s, p)).wait_recv()
     gather.close()
@@ -551,7 +568,6 @@
         one.wait_send()
     l_emb = load(9, embedding, part)
     w_ring(1 - xl, 0)
-    w_first(1, 1)
     w_second(0, 1)
     m_ring(xh)
     for side in (0, 1):
@@ -670,6 +686,7 @@
     project_tiles(3, 5, early)
     own.append(first_stage(1, early, 0))
     w_second(1, 1)
+    p_first()
     m_ring(1 - xh)
     for d in (1, 3):
         pass_on(0, early, 0, d)
@@ -695,7 +712,7 @@
         relay(0, early, 0, d)
     for lane in (0, 1):
         pass_on(lane, late, 1, 2)
-    p_first()
+    p_second()
     w_far(xl, 1)
     w_far(1 - xl, 1)
     w_last(1)
@@ -703,7 +720,6 @@
     send_queries(early, 0)
     project_tiles(5, 7, late)
     send_queries(late, 1)
-    p_second()
     relay(0, early, 0, 2)
     for d in (0, 1, 3, 2):
         relay(1, early, 0, d)
@@ -788,8 +804,8 @@
             dma((11,)),
             dma((60,)),
             dma((16, 2, 2)),
-            dma((15,)),
-            dma((16,)),
+            dma((30,)),
+            dma((16, 2)),
             dma((10,)),
             dma((12,)),
             dma((7,)),
@@ -951,8 +967,8 @@
     make(1)
     gather.second(0)
     gather.first(1)
+    gather.cross()
     gather.second(1)
-    gather.cross()
     own_load.wait()
     own_t_all = [own_in[n * 256:(n + 1) * 256, :].astype(F32).T for n in range(2)]
     gather.close()

time: 220 us -> 205 us (0.932); the launches traced: 222 us -> 204 us
  Pallas kernels: 220 us -> 202 us
    pallas_call x1, Pallas kernels: 150 us -> 140 us  [front(): pl.pallas_call(front_kernel, out_shape=(jax.ShapeDtypeStruct((8, 64, 2560...]
    pallas_call x1, Pallas kernels: 27.1 us -> 20.9 us  [attend(): pl.pallas_call(attend_kernel, out_shape=jax.ShapeDtypeStruct((16, 160, 12...]
where the time goes in v5:
time: 205 us; the launch traced here: 204 us
  Pallas kernels  202 us (99%)
    pallas_call x1, Pallas kernels, front(): pl.pallas_call(front_kernel, out_shape=(jax.ShapeDtypeStruct((8, 64, 2560...  140 us
    pallas_call x1, Pallas kernels, finish(): pl.pallas_call(finish_kernel, out_shape=jax.ShapeDtypeStruct((320, 512),...  41.8 us
    pallas_call x1, Pallas kernels, attend(): pl.pallas_call(attend_kernel, out_shape=jax.ShapeDtypeStruct((16, 160, 12...  20.9 us

profile of v5, /device:TPU:1, one launch (start us, length us, event | category | flops | bytes accessed | tf_op | source)
XLA Modules:
  0.0 204.1 jit_solution(17389699227441889739)
XLA Ops:
  0.0 139.6 %front.1 = (bf16[8,64,2560]{2,1,0:T(8,128)(2,1)}, bf16[16,160,512]{2,1,0:T(8,128)(2,1)}, bf16[16,160,512]{2,1,0:T(8,128)(2,1)}, bf16[16,160,128]{2,1,0:T(8,128)(2,1)}, bf16[2560,640]{1,0:T(8,128)(2,1)}) custom-call(s32[8192]{0:T(1024)} %segments.3, bf16[8,64,2560]{2,1,0:T(8,128)(2,1)} %bitcast.10, f32[2560]{0:T(1024)} %norm_gain.1, ...), custom_call_target="tpu_custom_call" | custom-call | tf_op jit(solution)/shard_map/front/pallas_call | solution.py:759
  139.6 20.9 %attend.1.ctx = bf16[16,160,128]{2,1,0:T(8,128)(2,1)} custom-call(s32[8192]{0:T(1024)} %segments.3, bf16[16,160,128]{2,1,0:T(8,128)(2,1)} %get-tuple-element.10.q_hbm, bf16[16,160,512]{2,1,0:T(8,128)(2,1)} %get-tuple-element.11.k_in, bf16[16,160,512]{2,1,0:T(8,128)(2,1)} %get-tuple-element.12.v_in), custom_call_target="tpu_custom_call" | custom-call | tf_op jit(solution)/shard_map/attend/pallas_call | solution.py:906
  160.5 41.8 %finish.1 = bf16[320,512]{1,0:T(8,128)(2,1)} custom-call(bf16[16,160,128]{2,1,0:T(8,128)(2,1)} %attend.1.ctx, bf16[2560,640]{1,0:T(8,128)(2,1)} %get-tuple-element.13.proj_in, bf16[512,2560]{1,0:T(8,128)(2,1)} %bitcast.19), custom_call_target="tpu_custom_call" | custom-call | flops 49999998976 | bytes 6000000 | tf_op jit(solution)/shard_map/finish/pallas_call | solution.py:987
  202.4 1.7 copy.20

commit v6 on v5

--- a/solution.py
+++ b/solution.py
@@ -258,17 +258,21 @@
                 for half in (0, 1):
                     w_wait(seq_at(zz, xx, 1 - core), half, group)
 
+    def p_cross():
+        for half in (0, 1):
+            p_to(s, half, seq_at(z, 1 - xl, core), pb.at[pl.ds(half * 80, 80), :])
+
     def p_first():
+        block = seq_at(z, 1 - xl, core)
         for half in (0, 1):
-            for to in (seq_at(z, 1 - xl, core), seq_at(up, xl, core), seq_at(down, xl, core), sibling):
+            for to in (seq_at(up, xl, core), seq_at(down, xl, core), sibling):
                 p_to(s, half, to, pb.at[pl.ds(half * 80, 80), :])
-
-    def p_second():
-        block = seq_at(z, 1 - xl, core)
         for half in (0, 1):
             p_wait(block, half)
             for to in (seq_at(up, xl, core), seq_at(down, xl, core), sibling):
                 p_to(block, half, to)
+
+    def p_second():
         p_ring(xl)
 
     def p_ring(side):
@@ -281,20 +285,12 @@
             p_to(seq_at(down, side, core), half, sibling)
             p_to(seq_at(up, side, core), half, sibling)
 
-    def p_third():
-        p_ring(1 - xl)
-        for half in (0, 1):
-            p_wait(seq_at(far, xl, core), half)
-            p_to(seq_at(far, xl, core), half, sibling)
-
     def p_last():
         for half in (0, 1):
-            p_wait(seq_at(far, 1 - xl, core), half)
-            p_to(seq_at(far, 1 - xl, core), half, sibling)
-        for zz in range(4):
-            for xx in range(2):
-                for half in (0, 1):
-                    p_wait(seq_at(zz, xx, 1 - core), half)
+            for block in (seq_at(down, 1 - xl, core), seq_at(up, 1 - xl, core), seq_at(far, xl, core)):
+                p_wait(block, half)
+            for block in (sibling, seq_at(z, 1 - xl, 1 - core), seq_at(up, xl, 1 - core), seq_at(down, xl, 1 - core)):
+                p_wait(block, half)
 
     for one in w_loads:
         one.wait()
@@ -568,6 +564,7 @@
         one.wait_send()
     l_emb = load(9, embedding, part)
     w_ring(1 - xl, 0)
+    p_cross()
     w_second(0, 1)
     m_ring(xh)
     for side in (0, 1):
@@ -686,7 +683,6 @@
     project_tiles(3, 5, early)
     own.append(first_stage(1, early, 0))
     w_second(1, 1)
-    p_first()
     m_ring(1 - xh)
     for d in (1, 3):
         pass_on(0, early, 0, d)
@@ -705,6 +701,7 @@
     pass_on(1, early, 0, 2)
     relay(0, early, 0, 0)
     w_ring(1 - xl, 1)
+    p_first()
     for lane in (0, 1):
         for d in (1, 3):
             pass_on(lane, late, 1, d)
@@ -726,7 +723,6 @@
     for lane in (0, 1):
         for d in (0, 1, 3, 2):
             relay(lane, late, 1, d)
-    p_third()
     for half in (0, 1):
         for zz in range(4):
             for side in (0, 1):
@@ -804,7 +800,7 @@
             dma((11,)),
             dma((60,)),
             dma((16, 2, 2)),
-            dma((30,)),
+            dma((20,)),
             dma((16, 2)),
             dma((10,)),
             dma((12,)),
@@ -922,16 +918,31 @@
     )(segments, q_in, k_in, v_in)
 
 
-def finish_kernel(ctx, proj_in, mixed, out, proj_t, own_in, gathered, part, in_send, in_recv, ring, fin, comb, across, rs_send, rs_recv, local_sem):
+def finish_kernel(ctx, proj_in, mixed, out, proj_t, own_in, gathered, part, p_load, p_send, p_recv, in_send, in_recv, ring, fin, comb, across, rs_send, rs_recv, local_sem):
     s, c = lax.axis_index("seq"), lax.axis_index("chan")
     peers = chan_peers(s, c)
-    proj_load = pltpu.make_async_copy(proj_in, proj_t, local_sem.at[1])
-    proj_load.start()
+    z, xl, core = seq_parts(s)
+    up, down, far = lax.rem(z + 1, 4), lax.rem(z + 3, 4), lax.rem(z + 2, 4)
+    sibling = seq_at(z, xl, 1 - core)
+
+    def p_rows(ref, block, half):
+        if half is None:
+            return ref.at[pl.ds(pl.multiple_of(block * 160, 32), 160), :]
+        return ref.at[pl.ds(pl.multiple_of(block * 160 + half * 80, 16), 80), :]
+
+    p_loads = []
+    for i, block in enumerate((
+        s, seq_at(z, 1 - xl, core), seq_at(up, xl, core), seq_at(down, xl, core), seq_at(far, xl, core),
+        seq_at(up, 1 - xl, core), seq_at(down, 1 - xl, core),
+        sibling, seq_at(z, 1 - xl, 1 - core), seq_at(up, xl, 1 - core), seq_at(down, xl, 1 - core),
+    )):
+        one = pltpu.make_async_copy(p_rows(proj_in, block, None), p_rows(proj_t, block, None), p_load.at[i])
+        one.start()
+        p_loads.append(one)
     window = pl.ds(pl.multiple_of(c * 5 // 2 * 128, 128), 384)
     own_load = pltpu.make_async_copy(mixed.at[:, window], own_in, local_sem.at[2])
     own_load.start()
     greet([(s, p) for p in peers] + [(lax.rem(s + d, 16), c) for d in range(1, 16)])
-    z = s // 4
     lanes = pl.ds(pl.multiple_of(lax.rem(s, 4) * 128, 128), 128)
     waits = []
     for d in range(16):
@@ -944,6 +955,22 @@
             one = copy_to(ctx.at[to], where, in_send.at[d - 1], in_recv.at[s], (to, c))
             one.start()
             waits.append(one)
+    def p_copy(i, src, block, half, to):
+        return copy_to(p_rows(src, block, half), p_rows(proj_t, block, half), p_send.at[i], p_recv.at[i], (to, c))
+
+    def p_to(i, src, block, half, to):
+        one = p_copy(i, src, block, half, to)
+        one.start()
+        waits.append(one)
+
+    p_to(0, proj_in, seq_at(down, 1 - xl, core), 0, seq_at(up, xl, core))
+    p_to(1, proj_in, seq_at(up, 1 - xl, core), 1, seq_at(down, xl, core))
+    p_to(2, proj_in, seq_at(down, 1 - xl, core), None, sibling)
+    p_to(3, proj_in, seq_at(up, 1 - xl, core), None, sibling)
+    p_to(4, proj_in, seq_at(far, xl, core), None, sibling)
+    for half in (0, 1):
+        p_copy(half, proj_t, seq_at(far, 1 - xl, core), half, sibling).wait_recv()
+        p_to(5 + half, proj_t, seq_at(far, 1 - xl, core), half, sibling)
     own.wait()
     for d in range(1, 16):
         block = lax.rem(s + d, 16)
@@ -961,7 +988,13 @@
 
         lax.fori_loop(0, 4, rows_of, 0)
 
-    proj_load.wait()
+    p_copy(2, proj_t, seq_at(down, 1 - xl, 1 - core), None, sibling).wait_recv()
+    p_copy(3, proj_t, seq_at(up, 1 - xl, 1 - core), None, sibling).wait_recv()
+    p_copy(4, proj_t, seq_at(far, xl, 1 - core), None, sibling).wait_recv()
+    for half in (0, 1):
+        p_copy(5 + half, proj_t, seq_at(far, 1 - xl, 1 - core), half, sibling).wait_recv()
+    for one in p_loads:
+        one.wait()
     make(0)
     gather.first(0)
     make(1)
@@ -994,6 +1027,9 @@
             VMEM((512, 384), BF16),
             VMEM((640, 512), BF16),
             VMEM((8, 320, 512), BF16),
+            dma((11,)),
+            dma((7,)),
+            dma((7,)),
             dma((15,)),
             dma((16,)),
             *ring_scratch(320, 512),

time: 205 us -> 207 us (level)
  Pallas kernels: 202 us -> 205 us
    pallas_call x1, Pallas kernels: 41.8 us -> 46.7 us  [finish(): pl.pallas_call(finish_kernel, out_shape=jax.ShapeDtypeStruct((320, 512),...]
    pallas_call x1, Pallas kernels: 140 us -> 137 us  [front(): pl.pallas_call(front_kernel, out_shape=(jax.ShapeDtypeStruct((8, 64, 2560...]
where the time goes in v6:
time: 207 us
  Pallas kernels  205 us (99%)
    pallas_call x1, Pallas kernels, front(): pl.pallas_call(front_kernel, out_shape=(jax.ShapeDtypeStruct((8, 64, 2560...  137 us
    pallas_call x1, Pallas kernels, finish(): pl.pallas_call(finish_kernel, out_shape=jax.ShapeDtypeStruct((320, 512),...  46.7 us
    pallas_call x1, Pallas kernels, attend(): pl.pallas_call(attend_kernel, out_shape=jax.ShapeDtypeStruct((16, 160, 12...  20.9 us

profile of v6, /device:TPU:1, one launch (start us, length us, event | category | flops | bytes accessed | tf_op | source)
XLA Modules:
  0.0 206.5 jit_solution(9849246787933922950)
XLA Ops:
  0.0 137.2 %front.1 = (bf16[8,64,2560]{2,1,0:T(8,128)(2,1)}, bf16[16,160,512]{2,1,0:T(8,128)(2,1)}, bf16[16,160,512]{2,1,0:T(8,128)(2,1)}, bf16[16,160,128]{2,1,0:T(8,128)(2,1)}, bf16[2560,640]{1,0:T(8,128)(2,1)}) custom-call(s32[8192]{0:T(1024)} %segments.3, bf16[8,64,2560]{2,1,0:T(8,128)(2,1)} %bitcast.10, f32[2560]{0:T(1024)} %norm_gain.1, ...), custom_call_target="tpu_custom_call" | custom-call | tf_op jit(solution)/shard_map/front/pallas_call | solution.py:755
  137.2 20.9 %attend.1.ctx = bf16[16,160,128]{2,1,0:T(8,128)(2,1)} custom-call(s32[8192]{0:T(1024)} %segments.3, bf16[16,160,128]{2,1,0:T(8,128)(2,1)} %get-tuple-element.10.q_hbm, bf16[16,160,512]{2,1,0:T(8,128)(2,1)} %get-tuple-element.11.k_in, bf16[16,160,512]{2,1,0:T(8,128)(2,1)} %get-tuple-element.12.v_in), custom_call_target="tpu_custom_call" | custom-call | tf_op jit(solution)/shard_map/attend/pallas_call | solution.py:902
  158.1 46.7 %finish.1 = bf16[320,512]{1,0:T(8,128)(2,1)} custom-call(bf16[16,160,128]{2,1,0:T(8,128)(2,1)} %attend.1.ctx, bf16[2560,640]{1,0:T(8,128)(2,1)} %get-tuple-element.13.proj_in, bf16[512,2560]{1,0:T(8,128)(2,1)} %bitcast.19), custom_call_target="tpu_custom_call" | custom-call | flops 49999998976 | bytes 6000000 | tf_op jit(solution)/shard_map/finish/pallas_call | solution.py:1020
  204.8 1.7 copy.20
